TPU v7x, 256 devices: a whole 4x4x8 slice. The times are simulated.
256 devices in a mesh: section: 4 (over y), pix: 64 (over x, z, core).
Axes of the slice: x: 4, y: 4, z: 8, core: 2. Of those that a mesh axis runs over, the one named last changes fastest.
Arguments:
- slc: float32 [2, 200, 16384], P(None, 'section', 'pix'), may hold values from -6 to 6
- neighbours: int32 [15, 16384], P(None, 'pix'), may hold values from 0 to 16383, as said below
- reference_pixel: int32 [1], replicated, may hold values from 0 to 16383
Outputs:
- phases: float32 [2, 200, 16384], P(None, 'section', 'pix')
- compressed: float32 [2, 4, 16384], P(None, 'section', 'pix')
Inputs may be any that keep to these rules, and one draw needn't show every extreme that they name: neighbours[0, p] = p; every entry lies within 256 of its column's pixel p, and that distance is reached.
All inputs are finite; a program needn't handle non-finite values.
Results may differ from a plain program's by a relative error of at most 0.0003.
Values sent between devices are 32-bit elements; how exact they have to be, the bound alone decides.
A program may use at most 64 MiB of HBM per device.

v0:
```python
import math

import jax
import jax.numpy as jnp
from jax import lax
from jax.sharding import Mesh
from jax.sharding import PartitionSpec as P

ITERS = 16
PIX = ("pix_0", "pix_1", "pix_2")


FLOOR = 0.05
REACH_LIMIT = 256


def copy_for_each(array, axis):
    copies = jnp.broadcast_to(array, (lax.axis_size(axis), *array.shape))
    return lax.all_to_all(copies, axis, split_axis=0, concat_axis=0, tiled=True)


def joined_along(pieces, dim):
    lengths = list(pieces.shape[1:])
    lengths[dim] *= pieces.shape[0]
    return jnp.moveaxis(pieces, 0, dim).reshape(lengths)


def gathered_copies(array, axis, dim):
    pieces = copy_for_each(array, axis)
    return joined_along(pieces, dim)


def extended_2(block, sides, width):
    for axis, dim in sides:
        count = lax.axis_size(axis)
        forward = [(i, i + 1) for i in range(count - 1)]
        backward = [(target, source) for source, target in forward]
        low = lax.ppermute(
            lax.slice_in_dim(block, block.shape[dim] - width, None, axis=dim), axis, forward
        )
        high = lax.ppermute(lax.slice_in_dim(block, 0, width, axis=dim), axis, backward)
        block = jnp.concatenate([low, block, high], axis=dim)
    return block


def spread(array, axes, root):
    array = jnp.where(lax.axis_index(axes) == root, array, jnp.zeros_like(array))
    for axis in axes:
        array = lax.psum(array, axis)
    return array


def unit(real, imag):
    scale = 1.0 / jnp.maximum(jnp.sqrt(real * real + imag * imag), FLOOR)
    return (real * scale, imag * scale)


def solve_block(ext_re, ext_im, index, own_re, own_im, iters):
    near_re = ext_re[:, index]
    near_im = ext_im[:, index]
    power = jnp.sum(near_re * near_re + near_im * near_im, axis=1)
    scale = 1.0 / jnp.sqrt(jnp.maximum(power, 1.0))
    z_re = near_re * scale[:, None, :]
    z_im = near_im * scale[:, None, :]
    count = own_re.shape[0]
    start_re = jnp.full(own_re.shape, 1.0 / math.sqrt(count), jnp.float32)
    start_im = jnp.zeros(own_re.shape, jnp.float32)

    def turn(step, carry):
        vec_re, vec_im = carry
        c_re = jnp.sum(z_re * vec_re[:, None, :] + z_im * vec_im[:, None, :], axis=0)
        c_im = jnp.sum(z_re * vec_im[:, None, :] - z_im * vec_re[:, None, :], axis=0)
        u_re = vec_re + jnp.sum(z_re * c_re[None] - z_im * c_im[None], axis=1)
        u_im = vec_im + jnp.sum(z_re * c_im[None] + z_im * c_re[None], axis=1)
        norm = jnp.sqrt(jnp.sum(u_re * u_re + u_im * u_im, axis=0))
        return (u_re / norm, u_im / norm)

    vec_re, vec_im = lax.fori_loop(0, iters, turn, (start_re, start_im))
    comp_re = jnp.sum(vec_re * own_re + vec_im * own_im, axis=0)
    comp_im = jnp.sum(vec_re * own_im - vec_im * own_re, axis=0)
    return (vec_re, vec_im, comp_re, comp_im)


def solve_section(extended, stack, local_index):
    vec_re, vec_im, comp_re, comp_im = solve_block(
        extended[0], extended[1], local_index, stack[0], stack[1], ITERS
    )
    return (jnp.stack([vec_re, vec_im]), jnp.stack([comp_re, comp_im]))


def on_device(slc, neighbours, reference_pixel):
    dates = slc.shape[1]
    pixels = slc.shape[2]
    reach = min(pixels, REACH_LIMIT)
    sections = lax.axis_size("section")
    me_section = lax.axis_index("section")
    me_pix = lax.axis_index(PIX)
    local_index = neighbours - (me_pix * pixels - reach)
    quarter = pixels // sections
    begin = me_section * quarter
    whole = gathered_copies(slc, "section", 1)
    dates_all = extended_2(whole, ((PIX, 2),), reach)
    own_all = lax.dynamic_slice_in_dim(whole, begin, quarter, 2)
    quarter_index = lax.dynamic_slice_in_dim(local_index, begin, quarter, 1)
    virtual_part = jnp.zeros((2, quarter), jnp.float32)
    vectors = []
    comps = []
    for rnd in range(sections):
        if rnd == 0:
            virtual_ext = jnp.zeros((2, pixels + 2 * reach), jnp.float32)
        else:
            block_virtual = gathered_copies(virtual_part, "section", 1)
            virtual_ext = extended_2(block_virtual, ((PIX, 1),), reach)
        extended = jnp.concatenate(
            [virtual_ext[:, None, :], dates_all[:, rnd * dates : (rnd + 1) * dates]], axis=1
        )
        stack = jnp.concatenate(
            [virtual_part[:, None, :], own_all[:, rnd * dates : (rnd + 1) * dates]], axis=1
        )
        vec_part, virtual_part = solve_section(extended, stack, quarter_index)
        vectors.append(vec_part)
        comps.append(virtual_part)
    datum_re = jnp.ones((quarter,), jnp.float32)
    datum_im = jnp.zeros((quarter,), jnp.float32)
    pieces = [None] * sections
    for rnd in range(sections - 1, -1, -1):
        vec_part = vectors[rnd]
        p_re = vec_part[0, 1:] * datum_re - vec_part[1, 1:] * datum_im
        p_im = vec_part[0, 1:] * datum_im + vec_part[1, 1:] * datum_re
        pieces[rnd] = jnp.stack([p_re, p_im])
        g_re, g_im = unit(vec_part[0, 0], vec_part[1, 0])
        datum_re, datum_im = (datum_re * g_re - datum_im * g_im, datum_re * g_im + datum_im * g_re)
    series_part = jnp.concatenate(pieces, axis=1)
    comp_part = jnp.stack(comps, axis=1)
    moved_series, moved_comp = (
        lax.all_to_all(series_part, "section", split_axis=1, concat_axis=2, tiled=True),
        lax.all_to_all(comp_part, "section", split_axis=1, concat_axis=2, tiled=True),
    )
    s_re = moved_series[0]
    s_im = moved_series[1]
    root = reference_pixel[0] // pixels
    column = reference_pixel[0] - root * pixels
    mine = jnp.stack(
        [
            lax.dynamic_index_in_dim(s_re, column, 1, False),
            lax.dynamic_index_in_dim(s_im, column, 1, False),
        ]
    )
    ref_series = spread(mine, PIX, root)
    u_re, u_im = unit(ref_series[0], ref_series[1])
    gain = math.sqrt(dates + 1)
    out_re = gain * (s_re * u_re[:, None] + s_im * u_im[:, None])
    out_im = gain * (s_im * u_re[:, None] - s_re * u_im[:, None])
    return (jnp.stack([out_re, out_im]), moved_comp)


def solution(mesh):
    finer = Mesh(
        mesh.devices.reshape(mesh.shape["section"], 4, 8, 2), ("section", "pix_0", "pix_1", "pix_2")
    )
    in_specs = (P(None, "section", PIX), P(None, PIX), P())
    out_specs = (P(None, "section", PIX), P(None, "section", PIX))
    return jax.shard_map(
        on_device, mesh=finer, in_specs=in_specs, out_specs=out_specs, check_vma=False
    )
```

profile of v0, /device:TPU:1, one launch (start us, length us, event | category | flops | bytes accessed | tf_op | source)
XLA Modules:
  0.0 206.7 jit_solution(8998482865269612337)
XLA Ops:
  2.4 5.0 %all-to-all-start = ((f32[4,2,50,256]{3,1,2,0:T(2,128)}), f32[4,2,50,256]{3,1,2,0:T(2,128)S(1)}, u32[]{:S(2)}, u32[]{:S(2)}) async-start(f32[4,2,50,256]{3,1,2,0:T(2,128)} %broadcast_in_dim.34), calls=%async_computation | async-start | bytes 819200 | tf_op jit(solution)/shard_map/all_to_all | solution.py:19
  7.4 6.4 %all-to-all-done = f32[4,2,50,256]{3,1,2,0:T(2,128)S(1)} async-done(((f32[4,2,50,256]{3,1,2,0:T(2,128)}), f32[4,2,50,256]{3,1,2,0:T(2,128)S(1)}, u32[]{:S(2)}, u32[]{:S(2)}) %all-to-all-start) | async-done | bytes 409632 | tf_op jit(solution)/shard_map/all_to_all | solution.py:19
  14.0 6.2 %collective-permute-start = (f32[2,200,256]{1,2,0:T(8,128)S(1)}, f32[2,200,256]{1,2,0:T(8,128)S(1)}, u32[]{:S(2)}, u32[]{:S(2)}) collective-permute-start(f32[2,200,256]{1,2,0:T(8,128)S(1)} %copy.174), channel_id=1, source_target_pairs={{0,1},{1,2},{2,3},{3,4},{4,5},{5,6},{6,7},{7,8},{8,9},{9,10},{10,1... | collective-permute-start | bytes 1228808 | tf_op jit(solution)/shard_map/ppermute | solution.py:38
  23.3 3.1 %collective-permute-done = f32[2,200,256]{1,2,0:T(8,128)S(1)} collective-permute-done((f32[2,200,256]{1,2,0:T(8,128)S(1)}, f32[2,200,256]{1,2,0:T(8,128)S(1)}, u32[]{:S(2)}, u32[]{:S(2)}) %collective-permute-start) | collective-permute-done | bytes 409632 | tf_op jit(solution)/shard_map/ppermute | solution.py:38
  26.4 4.4 %collective-permute-done.1 = f32[2,200,256]{1,2,0:T(8,128)S(1)} collective-permute-done((f32[2,200,256]{1,2,0:T(8,128)S(1)}, f32[2,200,256]{1,2,0:T(8,128)S(1)}, u32[]{:S(2)}, u32[]{:S(2)}) %collective-permute-start.1) | collective-permute-done | bytes 409632 | tf_op jit(solution)/shard_map/ppermute | solution.py:41
  35.8 4.0 %gather_fusion.1 = f32[960,51]{1,0:T(8,128)} fusion(f32[51,768]{0,1:T(8,128)S(1)} %get-tuple-element.316, s32[1024]{0:T(1024)S(1)} %pad_clamp_fusion), kind=kCustom, calls=%fused_computation.1 | custom fusion | bytes 395520 | tf_op jit(solution)/shard_map/gather | solution.py:60
  41.4 8.8 %while.52 = (s32[]{:T(128)}, f32[51,64]{1,0:T(8,128)S(1)}, f32[51,64]{1,0:T(8,128)S(1)}, f32[51,15,64]{2,1,0:T(8,128)S(1)}, f32[51,15,64]{2,1,0:T(8,128)S(1)}, /*index=5*/s32[]{:T(128)}, s32[]{:T(128)}) while((s32[]{:T(128)}, f32[51,64]{1,0:T(8,128)S(1)}, f32[51,64]{1,0:T(8,128)S(1)}, f32[51,15,64]{2,1,0:T(8,128)S(1)}, ...), condition=%wide.region_7.0_spmd.clone, body=%wide.region_1.0_spmd.clone.sunk | while | flops 807491 | bytes 1034839 | solution.py:78
  51.0 3.2 %all-to-all-start.1 = ((f32[4,1,128]{2,1,0:T(1,128)}), f32[4,1,128]{2,1,0:T(1,128)S(1)}, u32[]{:S(2)}, u32[]{:S(2)}) async-start(f32[4,1,128]{2,1,0:T(1,128)} %reshape.555), calls=%async_computation.1 | async-start | bytes 4096 | tf_op jit(solution)/shard_map/all_to_all | solution.py:19
  54.2 4.0 %all-to-all-done.1 = f32[4,1,128]{2,1,0:T(1,128)S(1)} async-done(((f32[4,1,128]{2,1,0:T(1,128)}), f32[4,1,128]{2,1,0:T(1,128)S(1)}, u32[]{:S(2)}, u32[]{:S(2)}) %all-to-all-start.1) | async-done | bytes 2080 | tf_op jit(solution)/shard_map/all_to_all | solution.py:19
  76.6 8.8 %while.53 = (s32[]{:T(128)}, f32[51,64]{1,0:T(8,128)S(1)}, f32[51,64]{1,0:T(8,128)S(1)}, f32[51,15,64]{2,1,0:T(8,128)S(1)}, f32[51,15,64]{2,1,0:T(8,128)S(1)}, /*index=5*/s32[]{:T(128)}, s32[]{:T(128)}) while((s32[]{:T(128)}, f32[51,64]{1,0:T(8,128)S(1)}, f32[51,64]{1,0:T(8,128)S(1)}, f32[51,15,64]{2,1,0:T(8,128)S(1)}, ...), condition=%wide.region_17.0_spmd.clone, body=%wide.region_11.0_spmd.clone.sunk | while | flops 807491 | bytes 1034839 | solution.py:78
  86.2 3.2 %all-to-all-start.2 = ((f32[4,1,128]{2,1,0:T(1,128)}), f32[4,1,128]{2,1,0:T(1,128)S(1)}, u32[]{:S(2)}, u32[]{:S(2)}) async-start(f32[4,1,128]{2,1,0:T(1,128)} %reshape.557), calls=%async_computation.2 | async-start | bytes 4096 | tf_op jit(solution)/shard_map/all_to_all | solution.py:19
  89.4 4.0 %all-to-all-done.2 = f32[4,1,128]{2,1,0:T(1,128)S(1)} async-done(((f32[4,1,128]{2,1,0:T(1,128)}), f32[4,1,128]{2,1,0:T(1,128)S(1)}, u32[]{:S(2)}, u32[]{:S(2)}) %all-to-all-start.2) | async-done | bytes 2080 | tf_op jit(solution)/shard_map/all_to_all | solution.py:19
  94.2 3.1 %collective-permute-start.4 = (f32[2,256]{1,0:T(2,128)S(1)}, f32[2,256]{1,0:T(2,128)S(1)}, u32[]{:S(2)}, u32[]{:S(2)}) collective-permute-start(f32[2,256]{1,0:T(2,128)S(1)} %reshape.471), channel_id=1, source_target_pairs={{0,1},{1,2},{2,3},{3,4},{4,5},{5,6},{6,7},{7,8},{8,9},{9,10},{10,1... | collective-permute-start | bytes 6152 | tf_op jit(solution)/shard_map/ppermute | solution.py:38
  109.4 8.8 %while.54 = (s32[]{:T(128)}, f32[51,64]{1,0:T(8,128)S(1)}, f32[51,64]{1,0:T(8,128)S(1)}, f32[51,15,64]{2,1,0:T(8,128)S(1)}, f32[51,15,64]{2,1,0:T(8,128)S(1)}, /*index=5*/s32[]{:T(128)}, s32[]{:T(128)}) while((s32[]{:T(128)}, f32[51,64]{1,0:T(8,128)S(1)}, f32[51,64]{1,0:T(8,128)S(1)}, f32[51,15,64]{2,1,0:T(8,128)S(1)}, ...), condition=%wide.region_27.0_spmd.clone, body=%wide.region_21.0_spmd.clone.sunk | while | flops 807491 | bytes 1034839 | solution.py:78
  119.0 3.2 %all-to-all-start.3 = ((f32[4,1,128]{2,1,0:T(1,128)}), f32[4,1,128]{2,1,0:T(1,128)S(1)}, u32[]{:S(2)}, u32[]{:S(2)}) async-start(f32[4,1,128]{2,1,0:T(1,128)} %reshape.559), calls=%async_computation.3 | async-start | bytes 4096 | tf_op jit(solution)/shard_map/all_to_all | solution.py:19
  122.4 3.9 %all-to-all-done.3 = f32[4,1,128]{2,1,0:T(1,128)S(1)} async-done(((f32[4,1,128]{2,1,0:T(1,128)}), f32[4,1,128]{2,1,0:T(1,128)S(1)}, u32[]{:S(2)}, u32[]{:S(2)}) %all-to-all-start.3) | async-done | bytes 2080 | tf_op jit(solution)/shard_map/all_to_all | solution.py:19
  127.1 3.1 %collective-permute-start.6 = (f32[2,256]{1,0:T(2,128)S(1)}, f32[2,256]{1,0:T(2,128)S(1)}, u32[]{:S(2)}, u32[]{:S(2)}) collective-permute-start(f32[2,256]{1,0:T(2,128)S(1)} %reshape.472), channel_id=1, source_target_pairs={{0,1},{1,2},{2,3},{3,4},{4,5},{5,6},{6,7},{7,8},{8,9},{9,10},{10,1... | collective-permute-start | bytes 6152 | tf_op jit(solution)/shard_map/ppermute | solution.py:38
  142.3 8.5 %while.55 = (s32[]{:T(128)}, f32[51,64]{1,0:T(8,128)S(1)}, f32[51,64]{1,0:T(8,128)S(1)}, f32[51,15,64]{2,1,0:T(8,128)S(1)}, f32[51,15,64]{2,1,0:T(8,128)S(1)}, /*index=5*/s32[]{:T(128)}, s32[]{:T(128)}) while((s32[]{:T(128)}, f32[51,64]{1,0:T(8,128)S(1)}, f32[51,64]{1,0:T(8,128)S(1)}, f32[51,15,64]{2,1,0:T(8,128)S(1)}, ...), condition=%wide.region_37.0_spmd.clone, body=%wide.region_31.0_spmd.clone.sunk | while | flops 807491 | bytes 1034839 | solution.py:78
  151.6 3.2 %all-to-all-start.5 = ((f32[4,1,128]{2,1,0:T(1,128)}), f32[4,1,128]{2,1,0:T(1,128)S(1)}, u32[]{:S(2)}, u32[]{:S(2)}) async-start(f32[4,1,128]{2,1,0:T(1,128)} %reshape.563), calls=%async_computation.5 | async-start | bytes 4096 | tf_op jit(solution)/shard_map/all_to_all | solution.py:137
  158.8 3.3 %all-to-all-start.4 = ((f32[4,1,6400]{2,1,0:T(1,128)}), f32[4,1,6400]{2,1,0:T(1,128)S(1)}, u32[]{:S(2)}, u32[]{:S(2)}) async-start(f32[4,1,6400]{2,1,0:T(1,128)} %reshape.561), calls=%async_computation.4 | async-start | bytes 204800 | tf_op jit(solution)/shard_map/all_to_all | solution.py:136
  164.2 2.9 %all-to-all-done.4 = f32[4,1,6400]{2,1,0:T(1,128)S(1)} async-done(((f32[4,1,6400]{2,1,0:T(1,128)}), f32[4,1,6400]{2,1,0:T(1,128)S(1)}, u32[]{:S(2)}, u32[]{:S(2)}) %all-to-all-start.4) | async-done | bytes 102432 | tf_op jit(solution)/shard_map/all_to_all | solution.py:136
  169.6 11.0 %psum.21 = f32[2,50]{1,0:T(2,128)S(1)} all-reduce(f32[2,50]{1,0:T(2,128)S(1)} %maximum_select_fusion), channel_id=1, replica_groups=mesh['section'=4,'pix_0'=4,'pix_1'=8,'pix_2'=2] {'pix_0'}, use_global_device_ids=true, to_apply=%region_38.0 | all-reduce | flops 100 | bytes 800 | tf_op jit(solution)/shard_map/psum | solution.py:49
  180.6 16.9 %psum.22 = f32[2,50]{1,0:T(2,128)S(1)} all-reduce(f32[2,50]{1,0:T(2,128)S(1)} %psum.21), channel_id=1, replica_groups=mesh['section'=4,'pix_0'=4,'pix_1'=8,'pix_2'=2] {'pix_1'}, use_global_device_ids=true, to_apply=%region_39.0 | all-reduce | flops 100 | bytes 800 | tf_op jit(solution)/shard_map/psum | solution.py:49
  197.4 8.0 %psum.23 = f32[2,50]{1,0:T(2,128)S(1)} all-reduce(f32[2,50]{1,0:T(2,128)S(1)} %psum.22), channel_id=1, replica_groups=mesh['section'=4,'pix_0'=4,'pix_1'=8,'pix_2'=2] {'pix_2'}, use_global_device_ids=true, to_apply=%region_40.41 | all-reduce | flops 100 | bytes 800 | tf_op jit(solution)/shard_map/psum | solution.py:49
  (535 shorter events, 100.1 us)
Async XLA Ops:
  0.6 21.5 %copy-start.7 = (s32[15,256]{1,0:T(8,128)S(1)}, s32[15,256]{1,0:T(8,128)}, u32[]{:S(2)}) copy-start(s32[15,256]{1,0:T(8,128)} %param.12) | copy-start | bytes 46084
  2.4 11.4 %all-to-all-start = ((f32[4,2,50,256]{3,1,2,0:T(2,128)}), f32[4,2,50,256]{3,1,2,0:T(2,128)S(1)}, u32[]{:S(2)}, u32[]{:S(2)}) async-start(f32[4,2,50,256]{3,1,2,0:T(2,128)} %broadcast_in_dim.34), calls=%async_computation | async-start | bytes 819200 | tf_op jit(solution)/shard_map/all_to_all | solution.py:19
  14.0 12.3 %collective-permute-start = (f32[2,200,256]{1,2,0:T(8,128)S(1)}, f32[2,200,256]{1,2,0:T(8,128)S(1)}, u32[]{:S(2)}, u32[]{:S(2)}) collective-permute-start(f32[2,200,256]{1,2,0:T(8,128)S(1)} %copy.174), channel_id=1, source_target_pairs={{0,1},{1,2},{2,3},{3,4},{4,5},{5,6},{6,7},{7,8},{8,9},{9,10},{10,1... | collective-permute-start | bytes 1228808 | tf_op jit(solution)/shard_map/ppermute | solution.py:38
  20.2 10.5 %collective-permute-start.1 = (f32[2,200,256]{1,2,0:T(8,128)S(1)}, f32[2,200,256]{1,2,0:T(8,128)S(1)}, u32[]{:S(2)}, u32[]{:S(2)}) collective-permute-start(f32[2,200,256]{1,2,0:T(8,128)S(1)} %copy.174), channel_id=1, source_target_pairs={{1,0},{2,1},{3,2},{4,3},{5,4},{6,5},{7,6},{8,7},{9,8},{10,9},{11,1... | collective-permute-start | bytes 1228808 | tf_op jit(solution)/shard_map/ppermute | solution.py:41
  41.4 8.9 %copy-start.1 = (f32[1,51,64]{2,0,1:T(1,128)S(1)}, f32[1,51,64]{2,0,1:T(1,128)}, u32[]{:S(2)}) copy-start(f32[1,51,64]{2,0,1:T(1,128)} %get-tuple-element.340) | copy-start | bytes 39172
  41.4 8.9 %copy-start.2 = (f32[1,51,64]{2,0,1:T(1,128)S(1)}, f32[1,51,64]{2,0,1:T(1,128)}, u32[]{:S(2)}) copy-start(f32[1,51,64]{2,0,1:T(1,128)} %get-tuple-element.341) | copy-start | bytes 39172
  50.2 18.4 %copy-start = (f32[2,50,768]{1,2,0:T(8,128)S(1)}, f32[2,50,768]{1,2,0:T(8,128)}, u32[]{:S(2)}) copy-start(f32[2,50,768]{1,2,0:T(8,128)} %get-tuple-element.310) | copy-start | bytes 921604
  51.0 7.3 %all-to-all-start.1 = ((f32[4,1,128]{2,1,0:T(1,128)}), f32[4,1,128]{2,1,0:T(1,128)S(1)}, u32[]{:S(2)}, u32[]{:S(2)}) async-start(f32[4,1,128]{2,1,0:T(1,128)} %reshape.555), calls=%async_computation.1 | async-start | bytes 4096 | tf_op jit(solution)/shard_map/all_to_all | solution.py:19
  59.6 5.5 %collective-permute-start.2 = (f32[2,256]{1,0:T(2,128)S(1)}, f32[2,256]{1,0:T(2,128)S(1)}, u32[]{:S(2)}, u32[]{:S(2)}) collective-permute-start(f32[2,256]{1,0:T(2,128)S(1)} %reshape.470), channel_id=1, source_target_pairs={{0,1},{1,2},{2,3},{3,4},{4,5},{5,6},{6,7},{7,8},{8,9},{9,10},{10,1... | collective-permute-start | bytes 6152 | tf_op jit(solution)/shard_map/ppermute | solution.py:38
  62.5 4.9 %collective-permute-start.3 = (f32[2,256]{1,0:T(2,128)S(1)}, f32[2,256]{1,0:T(2,128)S(1)}, u32[]{:S(2)}, u32[]{:S(2)}) collective-permute-start(f32[2,256]{1,0:T(2,128)S(1)} %reshape.470), channel_id=1, source_target_pairs={{1,0},{2,1},{3,2},{4,3},{5,4},{6,5},{7,6},{8,7},{9,8},{10,9},{11,1... | collective-permute-start | bytes 6152 | tf_op jit(solution)/shard_map/ppermute | solution.py:41
  76.6 8.9 %copy-start.3 = (f32[1,51,64]{2,0,1:T(1,128)S(1)}, f32[1,51,64]{2,0,1:T(1,128)}, u32[]{:S(2)}) copy-start(f32[1,51,64]{2,0,1:T(1,128)} %get-tuple-element.338) | copy-start | bytes 39172
  76.6 8.9 %copy-start.4 = (f32[1,51,64]{2,0,1:T(1,128)S(1)}, f32[1,51,64]{2,0,1:T(1,128)}, u32[]{:S(2)}) copy-start(f32[1,51,64]{2,0,1:T(1,128)} %get-tuple-element.339) | copy-start | bytes 39172
  86.2 7.3 %all-to-all-start.2 = ((f32[4,1,128]{2,1,0:T(1,128)}), f32[4,1,128]{2,1,0:T(1,128)S(1)}, u32[]{:S(2)}, u32[]{:S(2)}) async-start(f32[4,1,128]{2,1,0:T(1,128)} %reshape.557), calls=%async_computation.2 | async-start | bytes 4096 | tf_op jit(solution)/shard_map/all_to_all | solution.py:19
  94.2 5.7 %collective-permute-start.4 = (f32[2,256]{1,0:T(2,128)S(1)}, f32[2,256]{1,0:T(2,128)S(1)}, u32[]{:S(2)}, u32[]{:S(2)}) collective-permute-start(f32[2,256]{1,0:T(2,128)S(1)} %reshape.471), channel_id=1, source_target_pairs={{0,1},{1,2},{2,3},{3,4},{4,5},{5,6},{6,7},{7,8},{8,9},{9,10},{10,1... | collective-permute-start | bytes 6152 | tf_op jit(solution)/shard_map/ppermute | solution.py:38
  97.3 4.9 %collective-permute-start.5 = (f32[2,256]{1,0:T(2,128)S(1)}, f32[2,256]{1,0:T(2,128)S(1)}, u32[]{:S(2)}, u32[]{:S(2)}) collective-permute-start(f32[2,256]{1,0:T(2,128)S(1)} %reshape.471), channel_id=1, source_target_pairs={{1,0},{2,1},{3,2},{4,3},{5,4},{6,5},{7,6},{8,7},{9,8},{10,9},{11,1... | collective-permute-start | bytes 6152 | tf_op jit(solution)/shard_map/ppermute | solution.py:41
  109.4 8.9 %copy-start.5 = (f32[1,51,64]{2,0,1:T(1,128)S(1)}, f32[1,51,64]{2,0,1:T(1,128)}, u32[]{:S(2)}) copy-start(f32[1,51,64]{2,0,1:T(1,128)} %get-tuple-element.336) | copy-start | bytes 39172
  109.4 8.9 %copy-start.6 = (f32[1,51,64]{2,0,1:T(1,128)S(1)}, f32[1,51,64]{2,0,1:T(1,128)}, u32[]{:S(2)}) copy-start(f32[1,51,64]{2,0,1:T(1,128)} %get-tuple-element.337) | copy-start | bytes 39172
  119.0 7.3 %all-to-all-start.3 = ((f32[4,1,128]{2,1,0:T(1,128)}), f32[4,1,128]{2,1,0:T(1,128)S(1)}, u32[]{:S(2)}, u32[]{:S(2)}) async-start(f32[4,1,128]{2,1,0:T(1,128)} %reshape.559), calls=%async_computation.3 | async-start | bytes 4096 | tf_op jit(solution)/shard_map/all_to_all | solution.py:19
  127.1 5.1 %collective-permute-start.6 = (f32[2,256]{1,0:T(2,128)S(1)}, f32[2,256]{1,0:T(2,128)S(1)}, u32[]{:S(2)}, u32[]{:S(2)}) collective-permute-start(f32[2,256]{1,0:T(2,128)S(1)} %reshape.472), channel_id=1, source_target_pairs={{0,1},{1,2},{2,3},{3,4},{4,5},{5,6},{6,7},{7,8},{8,9},{9,10},{10,1... | collective-permute-start | bytes 6152 | tf_op jit(solution)/shard_map/ppermute | solution.py:38
  130.2 4.9 %collective-permute-start.7 = (f32[2,256]{1,0:T(2,128)S(1)}, f32[2,256]{1,0:T(2,128)S(1)}, u32[]{:S(2)}, u32[]{:S(2)}) collective-permute-start(f32[2,256]{1,0:T(2,128)S(1)} %reshape.472), channel_id=1, source_target_pairs={{1,0},{2,1},{3,2},{4,3},{5,4},{6,5},{7,6},{8,7},{9,8},{10,9},{11,1... | collective-permute-start | bytes 6152 | tf_op jit(solution)/shard_map/ppermute | solution.py:41
  151.6 7.3 %all-to-all-start.5 = ((f32[4,1,128]{2,1,0:T(1,128)}), f32[4,1,128]{2,1,0:T(1,128)S(1)}, u32[]{:S(2)}, u32[]{:S(2)}) async-start(f32[4,1,128]{2,1,0:T(1,128)} %reshape.563), calls=%async_computation.5 | async-start | bytes 4096 | tf_op jit(solution)/shard_map/all_to_all | solution.py:137
  158.8 8.3 %all-to-all-start.4 = ((f32[4,1,6400]{2,1,0:T(1,128)}), f32[4,1,6400]{2,1,0:T(1,128)S(1)}, u32[]{:S(2)}, u32[]{:S(2)}) async-start(f32[4,1,6400]{2,1,0:T(1,128)} %reshape.561), calls=%async_computation.4 | async-start | bytes 204800 | tf_op jit(solution)/shard_map/all_to_all | solution.py:136
where the time goes:
time: 208 us; the launch traced here: 207 us
  starting transfers between devices  44.2 us (21%)
  other arithmetic  41.7 us (20%)
  local copies, waits for them, and re-layouts  41.6 us (20%)
  waiting for transfers between devices  38.9 us (19%)
  blocking collectives  35.9 us (17%)
  loops' own time  2.34 us (1%)
    psum x3, blocking collectives, spread(): array = lax.psum(array, axis)  35.9 us
    all_to_all x4, waiting for transfers between devices, copy_for_each(): return lax.all_to_all(copies, axis, split_axis=0, concat_axis=0, tiled=True)  18.3 us
    reduce_sum x64, other arithmetic, turn(): u_im = vec_im + jnp.sum(z_re * c_im[None] + z_im * c_re[None], axis=1)  17.2 us
    ppermute x4, starting transfers between devices, extended_2(): lax.ppermute(lax.slice_in_dim(block, block.shape[dim] - width, None, axis...  15.3 us
    gather x8, local copies, waits for them, and re-layouts, solve_block(): near_im = ext_im[:, index]  14.7 us
    all_to_all x4, starting transfers between devices, copy_for_each(): return lax.all_to_all(copies, axis, split_axis=0, concat_axis=0, tiled=True)  14.7 us
    gather x8, local copies, waits for them, and re-layouts, solve_block(): near_re = ext_re[:, index]  12.6 us
    ppermute x4, waiting for transfers between devices, extended_2(): lax.ppermute(lax.slice_in_dim(block, 0, width, axis=dim), axis, backward)  11.9 us
  transfers between devices with their start and end apart: 14, of which 11 were waited for; matrix products, arithmetic and copies ran while one was open for 2% of the time, Pallas kernels for 0%

commit v1 on v0

v1 whole, which is shorter than its diff:
```python
import math

import jax
import jax.numpy as jnp
from jax import lax
from jax.experimental import pallas as pl
from jax.experimental.pallas import tpu as pltpu
from jax.sharding import PartitionSpec as P

ITERS = 16
FLOOR = 0.05
REACH = 256
NB = 15
ROWS = 50
PAD = 56
GROUPS = PAD // 8
TILES = 2
SPAN = 5
SCALE = 2.0**-45
START = 1.0 / math.sqrt(ROWS + 1)
GAIN = math.sqrt(ROWS + 1)
SECTIONS = 4
PIX = 64
MESH = pl.DeviceIdType.MESH
F32 = jnp.float32


def bcast(row):
    return jnp.broadcast_to(row, (8, 128))


def pick(sources, lane, tile):
    out = jnp.zeros((8, 128), F32)
    for m, source in enumerate(sources):
        got = jnp.take_along_axis(source, lane, axis=1, mode="promise_in_bounds")
        out = jnp.where(tile == m, got, out)
    return out


def column_sum(x):
    return jnp.sum(x, axis=0, keepdims=True)


def unit(re, im):
    scale = 1.0 / jnp.maximum(jnp.sqrt(re * re + im * im), FLOOR)
    return re * scale, im * scale


def remote(src, dst, send, recv, device):
    return pltpu.make_async_remote_copy(
        src_ref=src, dst_ref=dst, send_sem=send, recv_sem=recv, device_id=device, device_id_type=MESH
    )


def kernel(
    slc_hbm, nbr, ref, phases, comp,
    slc, left, right, ext, lanes, tiles, zs, kre, kim, cvec, bvec, xsum, zbuf, sbuf,
    vbuf, msg, fmsg, fbuf, series, rmsg, rbuf1, rmsg2, rbuf2,
    load_sem, halo_send, halo_recv, v_send, v_recv, f_send, f_recv, r_send, r_recv,
):
    sec = lax.axis_index("section")
    pix = lax.axis_index("pix")
    before = lax.rem(pix + (PIX - 1), PIX)
    after = lax.rem(pix + 1, PIX)
    near = (before, pix, after)
    sec_up = lax.rem(sec + 1, SECTIONS)
    sec_down = lax.rem(sec + (SECTIONS - 1), SECTIONS)
    x = pix // 16
    z = lax.rem(pix // 2, 8)
    core = lax.rem(pix, 2)
    group = x * 2 + core
    first = []
    second = []
    for d in range(1, 8):
        g = lax.rem(group + d, 8)
        first.append((g // 2) * 16 + z * 2 + lax.rem(g, 2))
        second.append(x * 16 + lax.rem(z + d, 8) * 2 + core)

    load = pltpu.make_async_copy(slc_hbm, slc, load_sem)
    load.start()
    barrier = pltpu.get_barrier_semaphore()
    peers = [(sec, before), (sec, after), (lax.rem(sec + 2, SECTIONS), pix)]
    peers += [(s, p) for s in (sec_up, sec_down) for p in near]
    peers += [(sec, p) for p in first + second]
    for peer in peers:
        pl.semaphore_signal(barrier, inc=1, device_id=peer, device_id_type=MESH)
    load.wait()
    pl.semaphore_wait(barrier, len(peers))

    to_left = remote(slc, right, halo_send.at[0], halo_recv.at[0], (sec, before))
    to_right = remote(slc, left, halo_send.at[1], halo_recv.at[1], (sec, after))
    to_left.start()
    to_right.start()

    base = pix * (TILES * 128) - REACH
    for t in range(TILES):
        rel = nbr[:, t * 128 : (t + 1) * 128] - (base + t * 128)
        lanes[t, 0:NB, :] = jnp.bitwise_and(rel, 127)
        tiles[t, 0:NB, :] = jnp.right_shift(rel, 7)
        lanes[t, NB : NB + 1, :] = jnp.zeros((1, 128), jnp.int32)
        tiles[t, NB : NB + 1, :] = jnp.full((1, 128), SPAN, jnp.int32)
    for c in range(2):
        for m in range(6):
            ext[c, m, PAD - 8 : PAD, :] = jnp.zeros((8, 128), F32)
        for m in range(2):
            ext[c, 2 + m, 0:ROWS, :] = slc[c, :, m * 128 : (m + 1) * 128]
    kre[...] = jnp.zeros_like(kre)
    kim[...] = jnp.zeros_like(kim)
    for t in range(TILES):
        for c in range(2):
            own = ext[c, 2 + t, 0:8, :]
            for g in range(1, GROUPS):
                own = own + ext[c, 2 + t, g * 8 : (g + 1) * 8, :]
            xsum[t, c : c + 1, :] = column_sum(own)

    to_left.wait()
    to_right.wait()
    for c in range(2):
        for m in range(2):
            ext[c, m, 0:ROWS, :] = left[c, :, m * 128 : (m + 1) * 128]
            ext[c, 4 + m, 0:ROWS, :] = right[c, :, m * 128 : (m + 1) * 128]

    for t in range(TILES):

        @pl.loop(0, GROUPS)
        def _(g):
            rows = pl.ds(pl.multiple_of(g * 8, 8), 8)
            src = [[ext[c, t + m, rows, :] for m in range(SPAN)] for c in range(2)]
            got = []
            power = jnp.zeros((8, 128), F32)
            for k in range(NB):
                if k == 0:
                    re, im = src[0][2], src[1][2]
                else:
                    lane = bcast(lanes[t, k : k + 1, :])
                    tile = bcast(tiles[t, k : k + 1, :])
                    re = pick(src[0], lane, tile)
                    im = pick(src[1], lane, tile)
                power = power + (re * re + im * im)
                zs[t, k, 0, rows, :] = re
                zs[t, k, 1, rows, :] = im
            w = lax.rsqrt(jnp.maximum(power, 1.0))
            for k in range(NB):
                zs[t, k, 0, rows, :] = zs[t, k, 0, rows, :] * w
                zs[t, k, 1, rows, :] = zs[t, k, 1, rows, :] * w
            zs[t, NB, 0, rows, :] = src[0][2]
            zs[t, NB, 1, rows, :] = src[1][2]

    for t in range(TILES):
        for kg in range(2):
            count = 8 if kg == 0 else NB - 8

            @pl.loop(8 * kg, NB + 1)
            def _(l):
                acc_re = [jnp.zeros((8, 128), F32) for _ in range(count)]
                acc_im = [jnp.zeros((8, 128), F32) for _ in range(count)]
                for g in range(GROUPS):
                    rows = slice(g * 8, (g + 1) * 8)
                    lr = zs[t, l, 0, rows, :]
                    li = zs[t, l, 1, rows, :]
                    for i in range(count):
                        kr = zs[t, 8 * kg + i, 0, rows, :]
                        ki = zs[t, 8 * kg + i, 1, rows, :]
                        acc_re[i] = acc_re[i] + (kr * lr + ki * li)
                        acc_im[i] = acc_im[i] + (kr * li - ki * lr)
                for i in range(count):
                    kre[t, l, 8 * kg + i : 8 * kg + i + 1, :] = column_sum(acc_re[i])
                    kim[t, l, 8 * kg + i : 8 * kg + i + 1, :] = column_sum(acc_im[i])

        for l in range(8):
            for k in range(8, NB):
                kre[t, l, k : k + 1, :] = kre[t, k, l : l + 1, :]
                kim[t, l, k : k + 1, :] = -kim[t, k, l : l + 1, :]

        bvec[t, 0] = kre[t, NB]
        bvec[t, 1] = kim[t, NB]
        cvec[t, 0, NB : NB + 1, :] = jnp.zeros((1, 128), F32)
        cvec[t, 1, NB : NB + 1, :] = jnp.zeros((1, 128), F32)

        @pl.loop(0, NB)
        def _(k):
            sr = zs[t, k, 0, 0:8, :]
            si = zs[t, k, 1, 0:8, :]
            for g in range(1, GROUPS):
                sr = sr + zs[t, k, 0, g * 8 : (g + 1) * 8, :]
                si = si + zs[t, k, 1, g * 8 : (g + 1) * 8, :]
            cvec[t, 0, pl.ds(k, 1), :] = START * column_sum(sr)
            cvec[t, 1, pl.ds(k, 1), :] = -START * column_sum(si)

    @pl.when(sec == 0)
    def _():
        zbuf[...] = jnp.zeros_like(zbuf)

    @pl.when(sec > 0)
    def _():
        for i in range(3):
            remote(msg, vbuf.at[i], v_send.at[i], v_recv.at[i], (sec_down, near[i])).wait_recv()
        for t in range(TILES):
            z0 = []
            for kg in range(2):
                rows = slice(8 * kg, 8 * kg + 8)
                lane = lanes[t, rows, :]
                tile = tiles[t, rows, :]
                pair = []
                for c in range(2):
                    src = []
                    for m in range(SPAN):
                        at = t + m
                        src.append(bcast(vbuf[at // 2, c : c + 1, (at % 2) * 128 : (at % 2) * 128 + 128]))
                    pair.append(pick(src, lane, tile))
                z0.append(pair)
            power = column_sum(z0[0][0] * z0[0][0] + z0[0][1] * z0[0][1] + (z0[1][0] * z0[1][0] + z0[1][1] * z0[1][1]))
            w = lax.rsqrt(jnp.maximum(power, 1.0))
            vr = vbuf[1, 0:1, t * 128 : (t + 1) * 128]
            vi = vbuf[1, 1:2, t * 128 : (t + 1) * 128]
            xsum[t, 0:1, :] = xsum[t, 0:1, :] + vr
            xsum[t, 1:2, :] = xsum[t, 1:2, :] + vi
            for kg in range(2):
                rows = slice(8 * kg, 8 * kg + 8)
                zr, zi = z0[kg][0] * w, z0[kg][1] * w
                z0[kg] = (zr, zi)
                zbuf[t, 0, rows, :] = zr
                zbuf[t, 1, rows, :] = zi
                cvec[t, 0, rows, :] = cvec[t, 0, rows, :] + START * zr
                cvec[t, 1, rows, :] = cvec[t, 1, rows, :] - START * zi
                bvec[t, 0, rows, :] = bvec[t, 0, rows, :] + (zr * vr + zi * vi)
                bvec[t, 1, rows, :] = bvec[t, 1, rows, :] + (zr * vi - zi * vr)
            for l in range(NB):
                lr = bcast(zbuf[t, 0, l : l + 1, :])
                li = bcast(zbuf[t, 1, l : l + 1, :])
                for kg in range(2):
                    rows = slice(8 * kg, 8 * kg + 8)
                    zr, zi = z0[kg]
                    kre[t, l, rows, :] = kre[t, l, rows, :] + (zr * lr + zi * li)
                    kim[t, l, rows, :] = kim[t, l, rows, :] + (zr * li - zi * lr)

    def product(state):
        for i, (t, c, kg) in enumerate((t, c, kg) for t in range(TILES) for c in range(2) for kg in range(2)):
            sbuf[t, c, 8 * kg : 8 * kg + 8, :] = state[i]
        out = []
        for t in range(TILES):
            y = [[None, None], [None, None]]
            for l in range(NB):
                lr = bcast(sbuf[t, 0, l : l + 1, :])
                li = bcast(sbuf[t, 1, l : l + 1, :])
                for kg in range(2):
                    rows = slice(8 * kg, 8 * kg + 8)
                    ar, ai = kre[t, l, rows, :], kim[t, l, rows, :]
                    re = ar * lr - ai * li
                    im = ar * li + ai * lr
                    y[0][kg] = re if l == 0 else y[0][kg] + re
                    y[1][kg] = im if l == 0 else y[1][kg] + im
            out += [y[0][0], y[0][1], y[1][0], y[1][1]]
        return out

    places = [(t, c, kg) for t in range(TILES) for c in range(2) for kg in range(2)]

    def c0(i):
        t, c, kg = places[i]
        return cvec[t, c, 8 * kg : 8 * kg + 8, :]

    def turn(_, state):
        return tuple(a + y + c0(i) for i, (a, y) in enumerate(zip(state, product(state))))

    state = lax.fori_loop(0, ITERS - 1, turn, tuple(c0(i) for i in range(8)))
    state = [a * SCALE for a in state]
    ks = product(state)
    norms = []
    for t in range(TILES):
        s = state[4 * t : 4 * t + 4]
        y = ks[4 * t : 4 * t + 4]
        total = None
        for i in range(4):
            term = s[i] * (y[i] + (2.0 * SCALE) * c0(4 * t + i))
            total = term if total is None else total + term
        norm = lax.rsqrt(column_sum(total) + SCALE * SCALE)
        norms.append(norm)
        cr = ci = fr = fi = None
        for kg in range(2):
            rows = slice(8 * kg, 8 * kg + 8)
            sr, si = s[kg], s[2 + kg]
            br, bi = bvec[t, 0, rows, :], bvec[t, 1, rows, :]
            zr, zi = zbuf[t, 0, rows, :], zbuf[t, 1, rows, :]
            a, b = sr * br + si * bi, sr * bi - si * br
            e, f = zr * sr - zi * si, zr * si + zi * sr
            cr = a if kg == 0 else column_sum(cr + a)
            ci = b if kg == 0 else column_sum(ci + b)
            fr = e if kg == 0 else column_sum(fr + e)
            fi = f if kg == 0 else column_sum(fi + f)
        cols = slice(t * 128, (t + 1) * 128)
        msg[0:1, cols] = (cr + (SCALE * START) * xsum[t, 0:1, :]) * norm
        msg[1:2, cols] = (ci + (SCALE * START) * xsum[t, 1:2, :]) * norm
        fr, fi = unit((fr + SCALE * START) * norm, fi * norm)
        fmsg[0:1, cols] = fr
        fmsg[1:2, cols] = fi

    @pl.when(sec < SECTIONS - 1)
    def _():
        for i in range(3):
            remote(msg, vbuf.at[2 - i], v_send.at[i], v_recv.at[2 - i], (sec_up, near[i])).start()

    for s in range(1, SECTIONS):

        @pl.when(sec == s)
        def _():
            for j in range(s):
                remote(fmsg, fbuf.at[s - 1], f_send.at[j], f_recv.at[s - 1], (j, pix)).start()

    comp[0, 0:1, :] = msg[0:1, :]
    comp[1, 0:1, :] = msg[1:2, :]

    for i, (t, c, kg) in enumerate(places):
        sbuf[t, c, 8 * kg : 8 * kg + 8, :] = state[i] * norms[t]
    for t in range(TILES):

        @pl.loop(0, GROUPS)
        def _(g):
            rows = pl.ds(pl.multiple_of(g * 8, 8), 8)
            re = bcast((SCALE * START) * norms[t])
            im = jnp.zeros((8, 128), F32)
            for k in range(NB):
                sr = bcast(sbuf[t, 0, k : k + 1, :])
                si = bcast(sbuf[t, 1, k : k + 1, :])
                zr, zi = zs[t, k, 0, rows, :], zs[t, k, 1, rows, :]
                re = re + (zr * sr - zi * si)
                im = im + (zr * si + zi * sr)
            series[t, 0, rows, :] = re
            series[t, 1, rows, :] = im

    for s in range(SECTIONS - 1, 0, -1):

        @pl.when(sec < s)
        def _():
            remote(fmsg, fbuf.at[s - 1], f_send.at[0], f_recv.at[s - 1], (s, pix)).wait_recv()
            for t in range(TILES):
                fr = fbuf[s - 1, 0:1, t * 128 : (t + 1) * 128]
                fi = fbuf[s - 1, 1:2, t * 128 : (t + 1) * 128]
                re, im = series[t, 0], series[t, 1]
                series[t, 0] = re * fr - im * fi
                series[t, 1] = re * fi + im * fr

    want = ref[0] - pix * (TILES * 128)
    lane = lax.broadcasted_iota(jnp.int32, (PAD, 128), 1)
    diag = lane == lax.broadcasted_iota(jnp.int32, (PAD, 128), 0)
    for c in range(2):
        column = jnp.zeros((PAD, 128), F32)
        for t in range(TILES):
            column = column + jnp.where(lane == want - t * 128, series[t, c], 0.0)
        column = jnp.sum(column, axis=1, keepdims=True)
        rmsg[c : c + 1, :] = column_sum(jnp.where(diag, column, 0.0))
    copies = []
    for d in range(1, 8):
        copies.append(remote(rmsg, rbuf1.at[d - 1], r_send.at[d - 1], r_recv.at[d - 1], (sec, first[d - 1])))
        copies[-1].start()
    for copy in copies:
        copy.wait_recv()
    total = rmsg[...]
    for d in range(1, 8):
        total = total + rbuf1[d - 1]
    rmsg2[...] = total
    for d in range(1, 8):
        copies.append(remote(rmsg2, rbuf2.at[d - 1], r_send.at[6 + d], r_recv.at[6 + d], (sec, second[d - 1])))
        copies[-1].start()
    for copy in copies[7:]:
        copy.wait_recv()
    for d in range(1, 8):
        total = total + rbuf2[d - 1]
    u = []
    for c in range(2):
        u.append(jnp.sum(jnp.where(diag, jnp.broadcast_to(total[c : c + 1, :], (PAD, 128)), 0.0), axis=1, keepdims=True))
    ur, ui = unit(u[0], u[1])
    ur, ui = GAIN * ur, GAIN * ui
    for t in range(TILES):
        re, im = series[t, 0], series[t, 1]
        cols = slice(t * 128, (t + 1) * 128)
        phases[0, :, cols] = (re * ur + im * ui)[0:ROWS]
        phases[1, :, cols] = (im * ur - re * ui)[0:ROWS]

    for copy in copies:
        copy.wait_send()

    @pl.when(sec < SECTIONS - 1)
    def _():
        for i in range(3):
            remote(msg, vbuf.at[2 - i], v_send.at[i], v_recv.at[2 - i], (sec_up, near[i])).wait_send()

    for s in range(1, SECTIONS):

        @pl.when(sec == s)
        def _():
            for j in range(s):
                remote(fmsg, fbuf.at[s - 1], f_send.at[j], f_recv.at[s - 1], (j, pix)).wait_send()


def on_device(slc, neighbours, reference_pixel):
    vmem = pl.BlockSpec(memory_space=pltpu.VMEM)
    pixels = slc.shape[2]
    dma = pltpu.SemaphoreType.DMA
    return pl.pallas_call(
        kernel,
        out_shape=(
            jax.ShapeDtypeStruct((2, ROWS, pixels), F32),
            jax.ShapeDtypeStruct((2, 1, pixels), F32),
        ),
        in_specs=[pl.BlockSpec(memory_space=pl.ANY), vmem, pl.BlockSpec(memory_space=pltpu.SMEM)],
        out_specs=(vmem, vmem),
        scratch_shapes=[
            pltpu.VMEM((2, ROWS, pixels), F32),
            pltpu.VMEM((2, ROWS, pixels), F32),
            pltpu.VMEM((2, ROWS, pixels), F32),
            pltpu.VMEM((2, 6, PAD, 128), F32),
            pltpu.VMEM((TILES, 16, 128), jnp.int32),
            pltpu.VMEM((TILES, 16, 128), jnp.int32),
            pltpu.VMEM((TILES, 16, 2, PAD, 128), F32),
            pltpu.VMEM((TILES, 16, 16, 128), F32),
            pltpu.VMEM((TILES, 16, 16, 128), F32),
            pltpu.VMEM((TILES, 2, 16, 128), F32),
            pltpu.VMEM((TILES, 2, 16, 128), F32),
            pltpu.VMEM((TILES, 2, 128), F32),
            pltpu.VMEM((TILES, 2, 16, 128), F32),
            pltpu.VMEM((TILES, 2, 16, 128), F32),
            pltpu.VMEM((3, 2, pixels), F32),
            pltpu.VMEM((2, pixels), F32),
            pltpu.VMEM((2, pixels), F32),
            pltpu.VMEM((3, 2, pixels), F32),
            pltpu.VMEM((TILES, 2, PAD, 128), F32),
            pltpu.VMEM((2, 128), F32),
            pltpu.VMEM((7, 2, 128), F32),
            pltpu.VMEM((2, 128), F32),
            pltpu.VMEM((7, 2, 128), F32),
            dma(()),
            dma((2,)),
            dma((2,)),
            dma((3,)),
            dma((3,)),
            dma((3,)),
            dma((3,)),
            dma((14,)),
            dma((14,)),
        ],
        compiler_params=pltpu.CompilerParams(collective_id=0, has_side_effects=True),
        cost_estimate=pl.CostEstimate(flops=100_000_000, bytes_accessed=1_000_000, transcendentals=0),
    )(slc, neighbours, reference_pixel)


def solution(mesh):
    return jax.shard_map(
        on_device,
        mesh=mesh,
        in_specs=(P(None, "section", "pix"), P(None, "pix"), P()),
        out_specs=(P(None, "section", "pix"), P(None, "section", "pix")),
        check_vma=False,
    )
```

time: 208 us -> 56.8 us (0.27)
  Pallas kernels: 0 us -> 51.6 us
  starting transfers between devices: 44.2 us -> 0 us
  other arithmetic: 41.7 us -> 0 us
  waiting for transfers between devices: 38.9 us -> 0 us
  local copies, waits for them, and re-layouts: 41.6 us -> 3.71 us
  blocking collectives: 35.9 us -> 0 us
  loops' own time: 2.34 us -> 0 us
    pallas_call x0 -> x1, Pallas kernels: none -> 51.6 us  [on_device(): pl.pallas_call(kernel, out_shape=(jax.ShapeDtypeStruct((2, ROWS, pixels),...]
    psum x3 -> x0, blocking collectives: 35.9 us -> none  [spread(): array = lax.psum(array, axis)]
    reduce_sum x200 -> x0, other arithmetic: 31.4 us -> none  [the longest x64 17.2 us: turn(): u_im = vec_im + jnp.sum(z_re * c_im[None] + z_im * c_re[None], axis=1)]
    gather x16 -> x0, local copies, waits for them, and re-layouts: 27.3 us -> none  [the longest x8 14.7 us: solve_block(): near_im = ext_im[:, index]]
    all_to_all x6 -> x0, waiting for transfers between devices: 23.9 us -> none  [the longest x4 18.3 us: copy_for_each(): return lax.all_to_all(copies, axis, split_axis=0, concat_axis=0, tiled=True)]
    ppermute x8 -> x0, starting transfers between devices: 23 us -> none  [the longest x4 15.3 us: extended_2(): lax.ppermute(lax.slice_in_dim(block, block.shape[dim] - width, None, axis...]
    all_to_all x6 -> x0, starting transfers between devices: 21.2 us -> none  [the longest x4 14.7 us: copy_for_each(): return lax.all_to_all(copies, axis, split_axis=0, concat_axis=0, tiled=True)]
    ppermute x8 -> x0, waiting for transfers between devices: 14.9 us -> none  [the longest x4 11.9 us: extended_2(): lax.ppermute(lax.slice_in_dim(block, 0, width, axis=dim), axis, backward)]
  transfers between devices with their start and end apart: 14 -> 0, of which waited for: 11 -> 0; matrix products, arithmetic and copies ran while one was open for 2% -> 0% of each run, Pallas kernels for 0% -> 0%
where the time goes in v1:
time: 56.8 us; the launch traced here: 56.6 us
  Pallas kernels  51.6 us (91%)
  local copies, waits for them, and re-layouts  3.71 us (7%)
  between operations  1.29 us (2%)
    pallas_call x1, Pallas kernels, on_device(): pl.pallas_call(kernel, out_shape=(jax.ShapeDtypeStruct((2, ROWS, pixels),...  51.6 us
    unnamed x4, local copies, waits for them, and re-layouts  2.12 us
    pallas_call x1, local copies, waits for them, and re-layouts, on_device(): pl.pallas_call(kernel, out_shape=(jax.ShapeDtypeStruct((2, ROWS, pixels),...  1.59 us

profile of v1, /device:TPU:1, one launch (start us, length us, event | category | flops | bytes accessed | tf_op | source)
XLA Modules:
  0.0 56.6 jit_solution(14477617222569177558)
XLA Ops:
  1.3 1.5 %copy.5.slc_hbm = f32[2,50,256]{2,1,0:T(8,128)} copy(f32[2,50,256]{2,0,1:T(2,128)} %param.3) | data formatting | bytes 204800 | tf_op args[0]
  2.8 51.6 %shard_map.50 = (f32[2,50,256]{2,1,0:T(8,128)}, f32[2,1,256]{2,1,0:T(1,128)}) custom-call(f32[2,50,256]{2,1,0:T(8,128)} %copy.5.slc_hbm, s32[15,256]{1,0:T(8,128)} %nbr.1, s32[1]{0:T(128)S(6)} %copy.8.ref), custom_call_target="tpu_custom_call" | custom-call | flops 100000000 | bytes 1000000 | tf_op jit(solution)/shard_map/pallas_call | solution.py:399
  54.4 0.0 copy-start
  54.4 1.6 %copy.6 = f32[2,50,256]{2,0,1:T(2,128)} copy(f32[2,50,256]{2,1,0:T(8,128)} %get-tuple-element.2) | data formatting | bytes 204800 | tf_op jit(solution)/shard_map/pallas_call | solution.py:399
  56.0 0.0 copy-done
  56.0 0.6 %copy.9 = f32[2,1,256]{2,1,0:T(1,128)} copy(f32[2,1,256]{2,1,0:T(1,128)S(1)} %copy-done) | data formatting | bytes 4096
Async XLA Ops:
  54.4 1.6 %copy-start = (f32[2,1,256]{2,1,0:T(1,128)S(1)}, f32[2,1,256]{2,1,0:T(1,128)}, u32[]{:S(2)}) copy-start(f32[2,1,256]{2,1,0:T(1,128)} %get-tuple-element.7) | copy-start | bytes 6148

commit v2 on v1

--- a/solution.py
+++ b/solution.py
@@ -14,6 +14,7 @@
 ROWS = 50
 PAD = 56
 GROUPS = PAD // 8
+FLAT = 4 * ROWS
 TILES = 2
 SPAN = 5
 SCALE = 2.0**-45
@@ -32,9 +33,12 @@
 def pick(sources, lane, tile):
     out = jnp.zeros((8, 128), F32)
     for m, source in enumerate(sources):
-        got = jnp.take_along_axis(source, lane, axis=1, mode="promise_in_bounds")
-        out = jnp.where(tile == m, got, out)
+        out = jnp.where(tile == m, take(source, lane), out)
     return out
+
+
+def take(source, lane):
+    return jnp.take_along_axis(source, lane, axis=1, mode="promise_in_bounds")
 
 
 def column_sum(x):
@@ -53,8 +57,8 @@
 
 
 def kernel(
-    slc_hbm, nbr, ref, phases, comp,
-    slc, left, right, ext, lanes, tiles, zs, kre, kim, cvec, bvec, xsum, zbuf, sbuf,
+    slc_hbm, nbr_hbm, ref_hbm, phases, comp,
+    nbr, ref, blocks, ext, lanes, tiles, zs, wbuf, red, kre, kim, cvec, bvec, xsum, zbuf, sbuf,
     vbuf, msg, fmsg, fbuf, series, rmsg, rbuf1, rmsg2, rbuf2,
     load_sem, halo_send, halo_recv, v_send, v_recv, f_send, f_recv, r_send, r_recv,
 ):
@@ -63,6 +67,7 @@
     before = lax.rem(pix + (PIX - 1), PIX)
     after = lax.rem(pix + 1, PIX)
     near = (before, pix, after)
+    present = (pix > 0, pix >= 0, pix < PIX - 1)
     sec_up = lax.rem(sec + 1, SECTIONS)
     sec_down = lax.rem(sec + (SECTIONS - 1), SECTIONS)
     x = pix // 16
@@ -76,21 +81,45 @@
         first.append((g // 2) * 16 + z * 2 + lax.rem(g, 2))
         second.append(x * 16 + lax.rem(z + d, 8) * 2 + core)
 
-    load = pltpu.make_async_copy(slc_hbm, slc, load_sem)
-    load.start()
+    own_rows = pl.ds(0, FLAT)
+    loads = [
+        pltpu.make_async_copy(slc_hbm, blocks.at[1, own_rows], load_sem.at[0]),
+        pltpu.make_async_copy(nbr_hbm, nbr, load_sem.at[1]),
+        pltpu.make_async_copy(ref_hbm, ref, load_sem.at[2]),
+    ]
+    for load in loads:
+        load.start()
     barrier = pltpu.get_barrier_semaphore()
     peers = [(sec, before), (sec, after), (lax.rem(sec + 2, SECTIONS), pix)]
     peers += [(s, p) for s in (sec_up, sec_down) for p in near]
     peers += [(sec, p) for p in first + second]
     for peer in peers:
         pl.semaphore_signal(barrier, inc=1, device_id=peer, device_id_type=MESH)
-    load.wait()
+    for i in range(3):
+        blocks[i, FLAT:, :] = jnp.zeros((32 * GROUPS - FLAT, 128), F32)
+    kre[...] = jnp.zeros_like(kre)
+    kim[...] = jnp.zeros_like(kim)
+    red[...] = jnp.zeros_like(red)
+    cvec[...] = jnp.zeros_like(cvec)
+    bvec[...] = jnp.zeros_like(bvec)
+    for i in (0, 2):
+
+        @pl.when(jnp.logical_not(present[i]))
+        def _():
+            blocks[i] = jnp.zeros((32 * GROUPS, 128), F32)
+            vbuf[i] = jnp.zeros_like(vbuf[i])
+
     pl.semaphore_wait(barrier, len(peers))
 
-    to_left = remote(slc, right, halo_send.at[0], halo_recv.at[0], (sec, before))
-    to_right = remote(slc, left, halo_send.at[1], halo_recv.at[1], (sec, after))
-    to_left.start()
-    to_right.start()
+    halos = [
+        remote(slc_hbm, blocks.at[2 - i, own_rows], halo_send.at[i // 2], halo_recv.at[i // 2], (sec, near[i]))
+        for i in (0, 2)
+    ]
+    for i, halo in zip((0, 2), halos):
+        pl.when(present[i])(halo.start)
+
+    for load in loads:
+        load.wait()
 
     base = pix * (TILES * 128) - REACH
     for t in range(TILES):
@@ -99,93 +128,119 @@
         tiles[t, 0:NB, :] = jnp.right_shift(rel, 7)
         lanes[t, NB : NB + 1, :] = jnp.zeros((1, 128), jnp.int32)
         tiles[t, NB : NB + 1, :] = jnp.full((1, 128), SPAN, jnp.int32)
-    for c in range(2):
-        for m in range(6):
-            ext[c, m, PAD - 8 : PAD, :] = jnp.zeros((8, 128), F32)
-        for m in range(2):
-            ext[c, 2 + m, 0:ROWS, :] = slc[c, :, m * 128 : (m + 1) * 128]
-    kre[...] = jnp.zeros_like(kre)
-    kim[...] = jnp.zeros_like(kim)
+
+    def spread(i):
+        for g in range(GROUPS):
+            for m in range(2):
+                for c in range(2):
+                    ext[2 * i + m, c, g * 8 : (g + 1) * 8, :] = blocks[i, pl.ds(g * 32 + m * 2 + c, 8, stride=4), :]
+
+    spread(1)
     for t in range(TILES):
         for c in range(2):
-            own = ext[c, 2 + t, 0:8, :]
-            for g in range(1, GROUPS):
-                own = own + ext[c, 2 + t, g * 8 : (g + 1) * 8, :]
-            xsum[t, c : c + 1, :] = column_sum(own)
-
-    to_left.wait()
-    to_right.wait()
-    for c in range(2):
-        for m in range(2):
-            ext[c, m, 0:ROWS, :] = left[c, :, m * 128 : (m + 1) * 128]
-            ext[c, 4 + m, 0:ROWS, :] = right[c, :, m * 128 : (m + 1) * 128]
-
-    for t in range(TILES):
-
-        @pl.loop(0, GROUPS)
-        def _(g):
-            rows = pl.ds(pl.multiple_of(g * 8, 8), 8)
-            src = [[ext[c, t + m, rows, :] for m in range(SPAN)] for c in range(2)]
-            got = []
-            power = jnp.zeros((8, 128), F32)
+            total = None
+            for g in range(GROUPS):
+                own = ext[2 + t, c, g * 8 : (g + 1) * 8, :]
+                zs[t, 0, c, g * 8 : (g + 1) * 8, :] = own
+                total = own if total is None else total + own
+            xsum[t, c : c + 1, :] = column_sum(total)
+        zs[t, 0, 2] = zs[t, 0, 0] - zs[t, 0, 1]
+
+    for i, halo in zip((0, 2), halos):
+        pl.when(present[i])(halo.wait_send)
+        pl.when(present[2 - i])(halo.wait_recv)
+    spread(0)
+    spread(2)
+
+    @pl.loop(0, 2 * TILES)
+    def _(step):
+        t = step // 2
+        for i in range(NB // 2):
+            k = 1 + lax.rem(step, 2) * (NB // 2) + i
+            lane = bcast(lanes[t, pl.ds(k, 1), :])
+            tile = bcast(tiles[t, pl.ds(k, 1), :])
+            here = [tile == m for m in range(SPAN)]
+            for g in range(GROUPS):
+                rows = slice(g * 8, (g + 1) * 8)
+                pair = []
+                for c in range(2):
+                    out = take(ext[t, c, rows, :], lane)
+                    for m in range(1, SPAN):
+                        out = jnp.where(here[m], take(ext[t + m, c, rows, :], lane), out)
+                    zs[t, k, c, rows, :] = out
+                    pair.append(out)
+                zs[t, k, 2, rows, :] = pair[0] - pair[1]
+
+    @pl.loop(0, TILES)
+    def _(t):
+        for g in range(GROUPS):
+            rows = slice(g * 8, (g + 1) * 8)
+            power = None
             for k in range(NB):
-                if k == 0:
-                    re, im = src[0][2], src[1][2]
-                else:
-                    lane = bcast(lanes[t, k : k + 1, :])
-                    tile = bcast(tiles[t, k : k + 1, :])
-                    re = pick(src[0], lane, tile)
-                    im = pick(src[1], lane, tile)
-                power = power + (re * re + im * im)
-                zs[t, k, 0, rows, :] = re
-                zs[t, k, 1, rows, :] = im
-            w = lax.rsqrt(jnp.maximum(power, 1.0))
-            for k in range(NB):
-                zs[t, k, 0, rows, :] = zs[t, k, 0, rows, :] * w
-                zs[t, k, 1, rows, :] = zs[t, k, 1, rows, :] * w
-            zs[t, NB, 0, rows, :] = src[0][2]
-            zs[t, NB, 1, rows, :] = src[1][2]
-
-    for t in range(TILES):
-        for kg in range(2):
-            count = 8 if kg == 0 else NB - 8
-
-            @pl.loop(8 * kg, NB + 1)
-            def _(l):
-                acc_re = [jnp.zeros((8, 128), F32) for _ in range(count)]
-                acc_im = [jnp.zeros((8, 128), F32) for _ in range(count)]
+                re, im = zs[t, k, 0, rows, :], zs[t, k, 1, rows, :]
+                term = re * re + im * im
+                power = term if power is None else power + term
+            wbuf[t, rows, :] = lax.rsqrt(jnp.maximum(power, 1.0))
+
+        def fold(slot, parts):
+            for i, part in enumerate(parts):
+                red[slot, i * 8 : (i + 1) * 8, :] = part
+            total = None
+            for i in range(8):
+                row = red[slot, pl.ds(i, 8, stride=8), :]
+                total = row if total is None else total + row
+            return total
+
+        slot = 0
+        for l in range(NB + 1):
+            for kg in range(2):
+                low, high = 8 * kg, min(8 * kg + 8, l + 1, NB)
+                if high <= low:
+                    continue
+                count = high - low
+                p, q, r = [None] * count, [None] * count, [None] * count
+                cr, ci = [None] * count, [None] * count
+
+                def put(box, i, value):
+                    box[i] = value if box[i] is None else box[i] + value
+
                 for g in range(GROUPS):
                     rows = slice(g * 8, (g + 1) * 8)
-                    lr = zs[t, l, 0, rows, :]
-                    li = zs[t, l, 1, rows, :]
+                    w = wbuf[t, rows, :]
+                    if l < NB:
+                        w2 = w * w
+                        lr, li = zs[t, l, 0, rows, :] * w2, zs[t, l, 1, rows, :] * w2
+                    else:
+                        lr, li = zs[t, 0, 0, rows, :] * w, zs[t, 0, 1, rows, :] * w
+                    le = lr + li
                     for i in range(count):
-                        kr = zs[t, 8 * kg + i, 0, rows, :]
-                        ki = zs[t, 8 * kg + i, 1, rows, :]
-                        acc_re[i] = acc_re[i] + (kr * lr + ki * li)
-                        acc_im[i] = acc_im[i] + (kr * li - ki * lr)
-                for i in range(count):
-                    kre[t, l, 8 * kg + i : 8 * kg + i + 1, :] = column_sum(acc_re[i])
-                    kim[t, l, 8 * kg + i : 8 * kg + i + 1, :] = column_sum(acc_im[i])
-
-        for l in range(8):
-            for k in range(8, NB):
-                kre[t, l, k : k + 1, :] = kre[t, k, l : l + 1, :]
-                kim[t, l, k : k + 1, :] = -kim[t, k, l : l + 1, :]
-
-        bvec[t, 0] = kre[t, NB]
-        bvec[t, 1] = kim[t, NB]
-        cvec[t, 0, NB : NB + 1, :] = jnp.zeros((1, 128), F32)
-        cvec[t, 1, NB : NB + 1, :] = jnp.zeros((1, 128), F32)
-
-        @pl.loop(0, NB)
-        def _(k):
-            sr = zs[t, k, 0, 0:8, :]
-            si = zs[t, k, 1, 0:8, :]
-            for g in range(1, GROUPS):
-                sr = sr + zs[t, k, 0, g * 8 : (g + 1) * 8, :]
-                si = si + zs[t, k, 1, g * 8 : (g + 1) * 8, :]
-            cvec[t, 0, pl.ds(k, 1), :] = START * column_sum(sr)
-            cvec[t, 1, pl.ds(k, 1), :] = -START * column_sum(si)
+                        k = low + i
+                        kr, ki = zs[t, k, 0, rows, :], zs[t, k, 1, rows, :]
+                        put(p, i, kr * lr)
+                        put(q, i, ki * li)
+                        if k != l:
+                            put(r, i, zs[t, k, 2, rows, :] * le)
+                        if l == NB:
+                            put(cr, i, kr * w)
+                            put(ci, i, ki * w)
+                re = fold(4 * kg + slot, [a + b for a, b in zip(p, q)])
+                im = fold(4 * kg + slot + 1, [jnp.zeros((8, 128), F32) if c is None else c + (b - a) for a, b, c in zip(p, q, r)])
+                rows = slice(low, low + 8)
+                if l < NB:
+                    kre[t, l, rows, :] = re
+                    kim[t, l, rows, :] = im
+                    for i in range(count):
+                        k = low + i
+                        if k != l:
+                            kre[t, k, l : l + 1, :] = re[i : i + 1, :]
+                            kim[t, k, l : l + 1, :] = -im[i : i + 1, :]
+                else:
+                    bvec[t, 0, rows, :] = re
+                    bvec[t, 1, rows, :] = im
+                    slot = 2 - slot
+                    cvec[t, 0, rows, :] = START * fold(4 * kg + slot, cr)
+                    cvec[t, 1, rows, :] = -START * fold(4 * kg + slot + 1, ci)
+                slot = 2 - slot
 
     @pl.when(sec == 0)
     def _():
@@ -194,7 +249,7 @@
     @pl.when(sec > 0)
     def _():
         for i in range(3):
-            remote(msg, vbuf.at[i], v_send.at[i], v_recv.at[i], (sec_down, near[i])).wait_recv()
+            pl.when(present[i])(remote(msg, vbuf.at[i], v_send.at[i], v_recv.at[i], (sec_down, near[i])).wait_recv)
         for t in range(TILES):
             z0 = []
             for kg in range(2):
@@ -297,7 +352,7 @@
     @pl.when(sec < SECTIONS - 1)
     def _():
         for i in range(3):
-            remote(msg, vbuf.at[2 - i], v_send.at[i], v_recv.at[2 - i], (sec_up, near[i])).start()
+            pl.when(present[i])(remote(msg, vbuf.at[2 - i], v_send.at[i], v_recv.at[2 - i], (sec_up, near[i])).start)
 
     for s in range(1, SECTIONS):
 
@@ -316,16 +371,17 @@
         @pl.loop(0, GROUPS)
         def _(g):
             rows = pl.ds(pl.multiple_of(g * 8, 8), 8)
-            re = bcast((SCALE * START) * norms[t])
-            im = jnp.zeros((8, 128), F32)
+            re = im = None
             for k in range(NB):
                 sr = bcast(sbuf[t, 0, k : k + 1, :])
                 si = bcast(sbuf[t, 1, k : k + 1, :])
                 zr, zi = zs[t, k, 0, rows, :], zs[t, k, 1, rows, :]
-                re = re + (zr * sr - zi * si)
-                im = im + (zr * si + zi * sr)
-            series[t, 0, rows, :] = re
-            series[t, 1, rows, :] = im
+                a, b = zr * sr - zi * si, zr * si + zi * sr
+                re = a if re is None else re + a
+                im = b if im is None else im + b
+            w = wbuf[t, rows, :]
+            series[t, 0, rows, :] = bcast((SCALE * START) * norms[t]) + w * re
+            series[t, 1, rows, :] = w * im
 
     for s in range(SECTIONS - 1, 0, -1):
 
@@ -372,9 +428,10 @@
     ur, ui = GAIN * ur, GAIN * ui
     for t in range(TILES):
         re, im = series[t, 0], series[t, 1]
-        cols = slice(t * 128, (t + 1) * 128)
-        phases[0, :, cols] = (re * ur + im * ui)[0:ROWS]
-        phases[1, :, cols] = (im * ur - re * ui)[0:ROWS]
+        for c, part in enumerate((re * ur + im * ui, im * ur - re * ui)):
+            for g in range(GROUPS):
+                count = min(8, ROWS - g * 8)
+                phases[pl.ds(g * 32 + t * 2 + c, count, stride=4), :] = part[g * 8 : g * 8 + count]
 
     for copy in copies:
         copy.wait_send()
@@ -382,7 +439,7 @@
     @pl.when(sec < SECTIONS - 1)
     def _():
         for i in range(3):
-            remote(msg, vbuf.at[2 - i], v_send.at[i], v_recv.at[2 - i], (sec_up, near[i])).wait_send()
+            pl.when(present[i])(remote(msg, vbuf.at[2 - i], v_send.at[i], v_recv.at[2 - i], (sec_up, near[i])).wait_send)
 
     for s in range(1, SECTIONS):
 
@@ -394,24 +451,28 @@
 
 def on_device(slc, neighbours, reference_pixel):
     vmem = pl.BlockSpec(memory_space=pltpu.VMEM)
+    any_space = pl.BlockSpec(memory_space=pl.ANY)
     pixels = slc.shape[2]
     dma = pltpu.SemaphoreType.DMA
-    return pl.pallas_call(
+    flat = slc.reshape(2, ROWS, TILES, 128).transpose(1, 2, 0, 3).reshape(FLAT, 128)
+    phases, comp = pl.pallas_call(
         kernel,
         out_shape=(
-            jax.ShapeDtypeStruct((2, ROWS, pixels), F32),
+            jax.ShapeDtypeStruct((FLAT, 128), F32),
             jax.ShapeDtypeStruct((2, 1, pixels), F32),
         ),
-        in_specs=[pl.BlockSpec(memory_space=pl.ANY), vmem, pl.BlockSpec(memory_space=pltpu.SMEM)],
+        in_specs=[any_space, any_space, any_space],
         out_specs=(vmem, vmem),
         scratch_shapes=[
-            pltpu.VMEM((2, ROWS, pixels), F32),
-            pltpu.VMEM((2, ROWS, pixels), F32),
-            pltpu.VMEM((2, ROWS, pixels), F32),
-            pltpu.VMEM((2, 6, PAD, 128), F32),
+            pltpu.VMEM((NB, pixels), jnp.int32),
+            pltpu.SMEM((1,), jnp.int32),
+            pltpu.VMEM((3, 32 * GROUPS, 128), F32),
+            pltpu.VMEM((6, 2, PAD, 128), F32),
             pltpu.VMEM((TILES, 16, 128), jnp.int32),
             pltpu.VMEM((TILES, 16, 128), jnp.int32),
-            pltpu.VMEM((TILES, 16, 2, PAD, 128), F32),
+            pltpu.VMEM((TILES, NB, 3, PAD, 128), F32),
+            pltpu.VMEM((TILES, PAD, 128), F32),
+            pltpu.VMEM((8, 64, 128), F32),
             pltpu.VMEM((TILES, 16, 16, 128), F32),
             pltpu.VMEM((TILES, 16, 16, 128), F32),
             pltpu.VMEM((TILES, 2, 16, 128), F32),
@@ -428,7 +489,7 @@
             pltpu.VMEM((7, 2, 128), F32),
             pltpu.VMEM((2, 128), F32),
             pltpu.VMEM((7, 2, 128), F32),
-            dma(()),
+            dma((3,)),
             dma((2,)),
             dma((2,)),
             dma((3,)),
@@ -438,9 +499,12 @@
             dma((14,)),
             dma((14,)),
         ],
-        compiler_params=pltpu.CompilerParams(collective_id=0, has_side_effects=True),
+        compiler_params=pltpu.CompilerParams(
+            collective_id=0, has_side_effects=True, vmem_limit_bytes=16 * 2**20
+        ),
         cost_estimate=pl.CostEstimate(flops=100_000_000, bytes_accessed=1_000_000, transcendentals=0),
-    )(slc, neighbours, reference_pixel)
+    )(flat, neighbours, reference_pixel)
+    return phases.reshape(ROWS, TILES, 2, 128).transpose(2, 0, 1, 3).reshape(2, ROWS, pixels), comp
 
 
 def solution(mesh):

time: 56.8 us -> 49 us (0.86)
  Pallas kernels: 51.6 us -> 44.7 us
  local copies, waits for them, and re-layouts: 3.71 us -> 2.83 us
    pallas_call x1, Pallas kernels: 51.6 us -> 44.7 us  [on_device(): pl.pallas_call(kernel, out_shape=(jax.ShapeDtypeStruct((FLAT, 128), F32),...]
    pallas_call x1 -> x0, local copies, waits for them, and re-layouts: 1.59 us -> none  [on_device(): pl.pallas_call(kernel, out_shape=(jax.ShapeDtypeStruct((2, ROWS, pixels),...]
    unnamed x4 -> x6, local copies, waits for them, and re-layouts: 2.12 us -> 2.83 us
where the time goes in v2:
time: 49 us; the launch traced here: 48.8 us
  Pallas kernels  44.7 us (91%)
  local copies, waits for them, and re-layouts  2.83 us (6%)
  between operations  1.29 us (3%)
    pallas_call x1, Pallas kernels, on_device(): pl.pallas_call(kernel, out_shape=(jax.ShapeDtypeStruct((FLAT, 128), F32),...  44.7 us
    unnamed x6, local copies, waits for them, and re-layouts  2.83 us

profile of v2, /device:TPU:1, one launch (start us, length us, event | category | flops | bytes accessed | tf_op | source)
XLA Modules:
  0.0 48.8 jit_solution(7757147380906378251)
XLA Ops:
  1.3 0.0 copy-start
  1.3 0.9 %copy-done = f32[2,50,256]{2,0,1:T(2,128)S(1)} copy-done((f32[2,50,256]{2,0,1:T(2,128)S(1)}, f32[2,50,256]{2,0,1:T(2,128)}, u32[]{:S(2)}) %copy-start) | copy-done | bytes 102424
  2.2 0.0 copy-start.1
  2.2 0.7 %copy-done.1 = s32[15,256]{1,0:T(8,128)S(1)} copy-done((s32[15,256]{1,0:T(8,128)S(1)}, s32[15,256]{1,0:T(8,128)}, u32[]{:S(2)}) %copy-start.1) | copy-done | bytes 15384
  2.9 44.7 %shard_map.50 = (f32[200,128]{1,0:T(8,128)S(1)}, f32[2,1,256]{2,1,0:T(1,128)S(1)}) custom-call(f32[200,128]{1,0:T(8,128)S(1)} %bitcast.11, s32[15,256]{1,0:T(8,128)S(1)} %copy-done.1, s32[1]{0:T(128)S(6)} %copy.9.ref_hbm), custom_call_target="tpu_custom_call" | custom-call | flops 100000000 | bytes 1000000 | tf_op jit(solution)/shard_map/pallas_call | solution.py:458
  47.6 0.6 %copy.10 = f32[2,50,256]{2,0,1:T(2,128)} copy(f32[2,50,256]{2,0,1:T(2,128)S(1)} %bitcast.10) | data formatting | bytes 204800
  48.3 0.6 %copy.11 = f32[2,1,256]{2,1,0:T(1,128)} copy(f32[2,1,256]{2,1,0:T(1,128)S(1)} %get-tuple-element.9) | data formatting | bytes 4096
Async XLA Ops:
  1.3 0.9 %copy-start = (f32[2,50,256]{2,0,1:T(2,128)S(1)}, f32[2,50,256]{2,0,1:T(2,128)}, u32[]{:S(2)}) copy-start(f32[2,50,256]{2,0,1:T(2,128)} %param.3) | copy-start | bytes 307204
  2.2 0.7 %copy-start.1 = (s32[15,256]{1,0:T(8,128)S(1)}, s32[15,256]{1,0:T(8,128)}, u32[]{:S(2)}) copy-start(s32[15,256]{1,0:T(8,128)} %nbr_hbm.1) | copy-start | bytes 46084

commit v3 on v2

--- a/solution.py
+++ b/solution.py
@@ -60,7 +60,7 @@
     slc_hbm, nbr_hbm, ref_hbm, phases, comp,
     nbr, ref, blocks, ext, lanes, tiles, zs, wbuf, red, kre, kim, cvec, bvec, xsum, zbuf, sbuf,
     vbuf, msg, fmsg, fbuf, series, rmsg, rbuf1, rmsg2, rbuf2,
-    load_sem, halo_send, halo_recv, v_send, v_recv, f_send, f_recv, r_send, r_recv,
+    load_sem, halo_send, halo_recv, v_send, v_recv, f_send, f_recv, r_send, r_recv, ready,
 ):
     sec = lax.axis_index("section")
     pix = lax.axis_index("pix")
@@ -90,11 +90,18 @@
     for load in loads:
         load.start()
     barrier = pltpu.get_barrier_semaphore()
-    peers = [(sec, before), (sec, after), (lax.rem(sec + 2, SECTIONS), pix)]
-    peers += [(s, p) for s in (sec_up, sec_down) for p in near]
-    peers += [(sec, p) for p in first + second]
-    for peer in peers:
-        pl.semaphore_signal(barrier, inc=1, device_id=peer, device_id_type=MESH)
+    peers = [(sec, before), (sec, after), (sec_up, pix), (sec_down, pix)]
+    peers += [(sec, x * 16 + lax.rem(z + d, 8) * 2 + core) for d in (1, 7)]
+    peers += [(sec, lax.rem(x + d, 4) * 16 + z * 2 + core) for d in (1, 3)]
+
+    def tell(sem):
+        for peer in peers:
+            pl.semaphore_signal(sem, inc=1, device_id=peer, device_id_type=MESH)
+
+    def hear(sem):
+        pl.semaphore_wait(sem, len(peers))
+
+    tell(barrier)
     for i in range(3):
         blocks[i, FLAT:, :] = jnp.zeros((32 * GROUPS - FLAT, 128), F32)
     kre[...] = jnp.zeros_like(kre)
@@ -109,16 +116,18 @@
             blocks[i] = jnp.zeros((32 * GROUPS, 128), F32)
             vbuf[i] = jnp.zeros_like(vbuf[i])
 
-    pl.semaphore_wait(barrier, len(peers))
-
+    hear(barrier)
+    tell(ready.at[0])
+
+    loads[0].wait()
     halos = [
-        remote(slc_hbm, blocks.at[2 - i, own_rows], halo_send.at[i // 2], halo_recv.at[i // 2], (sec, near[i]))
+        remote(blocks.at[1, own_rows], blocks.at[2 - i, own_rows], halo_send.at[i // 2], halo_recv.at[i // 2], (sec, near[i]))
         for i in (0, 2)
     ]
     for i, halo in zip((0, 2), halos):
         pl.when(present[i])(halo.start)
 
-    for load in loads:
+    for load in loads[1:]:
         load.wait()
 
     base = pix * (TILES * 128) - REACH
@@ -146,30 +155,39 @@
             xsum[t, c : c + 1, :] = column_sum(total)
         zs[t, 0, 2] = zs[t, 0, 0] - zs[t, 0, 1]
 
+    def gather(t, mine, theirs, begin):
+        @pl.loop(0, 2)
+        def _(half):
+            for i in range(NB // 2):
+                k = 1 + half * (NB // 2) + i
+                lane = bcast(lanes[t, pl.ds(k, 1), :])
+                tile = bcast(tiles[t, pl.ds(k, 1), :])
+                here = [tile == m for m in theirs]
+                for g in range(GROUPS):
+                    rows = slice(g * 8, (g + 1) * 8)
+                    pair = []
+                    for c in range(2):
+                        out = take(ext[t + mine, c, rows, :], lane) if begin else zs[t, k, c, rows, :]
+                        for there, m in zip(here, theirs):
+                            out = jnp.where(there, take(ext[t + m, c, rows, :], lane), out)
+                        zs[t, k, c, rows, :] = out
+                        pair.append(out)
+                    if not begin:
+                        zs[t, k, 2, rows, :] = pair[0] - pair[1]
+
+    for t in range(TILES):
+        gather(t, 2 - t, (3 - t,), True)
+
     for i, halo in zip((0, 2), halos):
         pl.when(present[i])(halo.wait_send)
         pl.when(present[2 - i])(halo.wait_recv)
     spread(0)
     spread(2)
 
-    @pl.loop(0, 2 * TILES)
-    def _(step):
-        t = step // 2
-        for i in range(NB // 2):
-            k = 1 + lax.rem(step, 2) * (NB // 2) + i
-            lane = bcast(lanes[t, pl.ds(k, 1), :])
-            tile = bcast(tiles[t, pl.ds(k, 1), :])
-            here = [tile == m for m in range(SPAN)]
-            for g in range(GROUPS):
-                rows = slice(g * 8, (g + 1) * 8)
-                pair = []
-                for c in range(2):
-                    out = take(ext[t, c, rows, :], lane)
-                    for m in range(1, SPAN):
-                        out = jnp.where(here[m], take(ext[t + m, c, rows, :], lane), out)
-                    zs[t, k, c, rows, :] = out
-                    pair.append(out)
-                zs[t, k, 2, rows, :] = pair[0] - pair[1]
+    for t in range(TILES):
+        gather(t, None, tuple(m for m in range(SPAN) if t + m not in (2, 3)), False)
+    hear(ready.at[0])
+    tell(ready.at[1])
 
     @pl.loop(0, TILES)
     def _(t):
@@ -241,6 +259,9 @@
                     cvec[t, 0, rows, :] = START * fold(4 * kg + slot, cr)
                     cvec[t, 1, rows, :] = -START * fold(4 * kg + slot + 1, ci)
                 slot = 2 - slot
+
+    hear(ready.at[1])
+    tell(ready.at[2])
 
     @pl.when(sec == 0)
     def _():
@@ -361,6 +382,7 @@
             for j in range(s):
                 remote(fmsg, fbuf.at[s - 1], f_send.at[j], f_recv.at[s - 1], (j, pix)).start()
 
+    hear(ready.at[2])
     comp[0, 0:1, :] = msg[0:1, :]
     comp[1, 0:1, :] = msg[1:2, :]
 
@@ -451,7 +473,7 @@
 
 def on_device(slc, neighbours, reference_pixel):
     vmem = pl.BlockSpec(memory_space=pltpu.VMEM)
-    any_space = pl.BlockSpec(memory_space=pl.ANY)
+    hbm = pl.BlockSpec(memory_space=pltpu.HBM)
     pixels = slc.shape[2]
     dma = pltpu.SemaphoreType.DMA
     flat = slc.reshape(2, ROWS, TILES, 128).transpose(1, 2, 0, 3).reshape(FLAT, 128)
@@ -461,7 +483,7 @@
             jax.ShapeDtypeStruct((FLAT, 128), F32),
             jax.ShapeDtypeStruct((2, 1, pixels), F32),
         ),
-        in_specs=[any_space, any_space, any_space],
+        in_specs=[hbm, hbm, hbm],
         out_specs=(vmem, vmem),
         scratch_shapes=[
             pltpu.VMEM((NB, pixels), jnp.int32),
@@ -498,6 +520,7 @@
             dma((3,)),
             dma((14,)),
             dma((14,)),
+            pltpu.SemaphoreType.REGULAR((3,)),
         ],
         compiler_params=pltpu.CompilerParams(
             collective_id=0, has_side_effects=True, vmem_limit_bytes=16 * 2**20

time: 49 us -> 48.1 us (0.982)
  Pallas kernels: 44.7 us -> 43.8 us
    pallas_call x1, Pallas kernels: 44.7 us -> 43.8 us  [on_device(): pl.pallas_call(kernel, out_shape=(jax.ShapeDtypeStruct((FLAT, 128), F32),...]
where the time goes in v3:
time: 48.1 us; the launch traced here: 47.9 us
  Pallas kernels  43.8 us (91%)
  local copies, waits for them, and re-layouts  2.83 us (6%)
  between operations  1.29 us (3%)
    pallas_call x1, Pallas kernels, on_device(): pl.pallas_call(kernel, out_shape=(jax.ShapeDtypeStruct((FLAT, 128), F32),...  43.8 us
    unnamed x6, local copies, waits for them, and re-layouts  2.83 us

profile of v3, /device:TPU:1, one launch (start us, length us, event | category | flops | bytes accessed | tf_op | source)
XLA Modules:
  0.0 47.9 jit_solution(3655383423301353835)
XLA Ops:
  1.3 0.0 copy-start
  1.3 0.9 %copy-done = f32[2,50,256]{2,0,1:T(2,128)S(1)} copy-done((f32[2,50,256]{2,0,1:T(2,128)S(1)}, f32[2,50,256]{2,0,1:T(2,128)}, u32[]{:S(2)}) %copy-start) | copy-done | bytes 102424
  2.2 0.0 copy-start.1
  2.2 0.7 %copy-done.1 = s32[15,256]{1,0:T(8,128)S(1)} copy-done((s32[15,256]{1,0:T(8,128)S(1)}, s32[15,256]{1,0:T(8,128)}, u32[]{:S(2)}) %copy-start.1) | copy-done | bytes 15384
  2.9 43.8 %shard_map.50 = (f32[200,128]{1,0:T(8,128)S(1)}, f32[2,1,256]{2,1,0:T(1,128)S(1)}) custom-call(f32[200,128]{1,0:T(8,128)S(1)} %bitcast.11, s32[15,256]{1,0:T(8,128)S(1)} %copy-done.1, s32[1]{0:T(128)S(6)} %copy.9.ref_hbm), custom_call_target="tpu_custom_call" | custom-call | flops 100000000 | bytes 1000000 | tf_op jit(solution)/shard_map/pallas_call | solution.py:480
  46.7 0.6 %copy.10 = f32[2,50,256]{2,0,1:T(2,128)} copy(f32[2,50,256]{2,0,1:T(2,128)S(1)} %bitcast.10) | data formatting | bytes 204800
  47.3 0.6 %copy.11 = f32[2,1,256]{2,1,0:T(1,128)} copy(f32[2,1,256]{2,1,0:T(1,128)S(1)} %get-tuple-element.9) | data formatting | bytes 4096
Async XLA Ops:
  1.3 0.9 %copy-start = (f32[2,50,256]{2,0,1:T(2,128)S(1)}, f32[2,50,256]{2,0,1:T(2,128)}, u32[]{:S(2)}) copy-start(f32[2,50,256]{2,0,1:T(2,128)} %param.3) | copy-start | bytes 307204
  2.2 0.7 %copy-start.1 = (s32[15,256]{1,0:T(8,128)S(1)}, s32[15,256]{1,0:T(8,128)}, u32[]{:S(2)}) copy-start(s32[15,256]{1,0:T(8,128)} %nbr_hbm.1) | copy-start | bytes 46084

commit v4 on v3

--- a/solution.py
+++ b/solution.py
@@ -57,8 +57,8 @@
 
 
 def kernel(
-    slc_hbm, nbr_hbm, ref_hbm, phases, comp,
-    nbr, ref, blocks, ext, lanes, tiles, zs, wbuf, red, kre, kim, cvec, bvec, xsum, zbuf, sbuf,
+    slc_hbm, nbr_hbm, ref, phases, comp,
+    nbr, blocks, ext, lanes, tiles, zs, wbuf, red, kre, kim, cvec, bvec, xsum, zbuf, sbuf,
     vbuf, msg, fmsg, fbuf, series, rmsg, rbuf1, rmsg2, rbuf2,
     load_sem, halo_send, halo_recv, v_send, v_recv, f_send, f_recv, r_send, r_recv, ready,
 ):
@@ -85,7 +85,6 @@
     loads = [
         pltpu.make_async_copy(slc_hbm, blocks.at[1, own_rows], load_sem.at[0]),
         pltpu.make_async_copy(nbr_hbm, nbr, load_sem.at[1]),
-        pltpu.make_async_copy(ref_hbm, ref, load_sem.at[2]),
     ]
     for load in loads:
         load.start()
@@ -483,11 +482,10 @@
             jax.ShapeDtypeStruct((FLAT, 128), F32),
             jax.ShapeDtypeStruct((2, 1, pixels), F32),
         ),
-        in_specs=[hbm, hbm, hbm],
+        in_specs=[hbm, hbm, pl.BlockSpec(memory_space=pltpu.SMEM)],
         out_specs=(vmem, vmem),
         scratch_shapes=[
             pltpu.VMEM((NB, pixels), jnp.int32),
-            pltpu.SMEM((1,), jnp.int32),
             pltpu.VMEM((3, 32 * GROUPS, 128), F32),
             pltpu.VMEM((6, 2, PAD, 128), F32),
             pltpu.VMEM((TILES, 16, 128), jnp.int32),
@@ -511,7 +509,7 @@
             pltpu.VMEM((7, 2, 128), F32),
             pltpu.VMEM((2, 128), F32),
             pltpu.VMEM((7, 2, 128), F32),
-            dma((3,)),
+            dma((2,)),
             dma((2,)),
             dma((2,)),
             dma((3,)),
@@ -526,7 +524,7 @@
             collective_id=0, has_side_effects=True, vmem_limit_bytes=16 * 2**20
         ),
         cost_estimate=pl.CostEstimate(flops=100_000_000, bytes_accessed=1_000_000, transcendentals=0),
-    )(flat, neighbours, reference_pixel)
+    )(*(pltpu.with_memory_space_constraint(a, pltpu.HBM) for a in (flat, neighbours)), reference_pixel)
     return phases.reshape(ROWS, TILES, 2, 128).transpose(2, 0, 1, 3).reshape(2, ROWS, pixels), comp
 
 

time: 48.1 us -> 46.5 us (0.967)
  local copies, waits for them, and re-layouts: 2.83 us -> 1.22 us
    unnamed x6 -> x2, local copies, waits for them, and re-layouts: 2.83 us -> 1.22 us
where the time goes in v4:
time: 46.5 us; the launch traced here: 46.4 us
  Pallas kernels  43.9 us (94%)
  between operations  1.28 us (3%)
  local copies, waits for them, and re-layouts  1.22 us (3%)
    pallas_call x1, Pallas kernels, on_device(): pl.pallas_call(kernel, out_shape=(jax.ShapeDtypeStruct((FLAT, 128), F32),...  43.9 us
    unnamed x2, local copies, waits for them, and re-layouts  1.22 us

profile of v4, /device:TPU:1, one launch (start us, length us, event | category | flops | bytes accessed | tf_op | source)
XLA Modules:
  0.0 46.4 jit_solution(2093604866498286763)
XLA Ops:
  1.3 43.9 %shard_map.50 = (f32[200,128]{1,0:T(8,128)S(1)}, f32[2,1,256]{2,1,0:T(1,128)S(1)}) custom-call(f32[200,128]{1,0:T(8,128)} %bitcast.11, s32[15,256]{1,0:T(8,128)} %nbr_hbm.1, s32[1]{0:T(128)S(6)} %copy.9.ref), custom_call_target="tpu_custom_call" | custom-call | flops 100000000 | bytes 1000000 | tf_op jit(solution)/shard_map/pallas_call | solution.py:479
  45.2 0.6 %copy.10 = f32[2,50,256]{2,0,1:T(2,128)} copy(f32[2,50,256]{2,0,1:T(2,128)S(1)} %bitcast.10) | data formatting | bytes 204800
  45.8 0.6 %copy.11 = f32[2,1,256]{2,1,0:T(1,128)} copy(f32[2,1,256]{2,1,0:T(1,128)S(1)} %get-tuple-element.9) | data formatting | bytes 4096

commit v5 on v4

--- a/solution.py
+++ b/solution.py
@@ -45,6 +45,20 @@
     return jnp.sum(x, axis=0, keepdims=True)
 
 
+def eye(count, shift=0):
+    lane = lax.broadcasted_iota(jnp.int32, (count, 128), 1)
+    return lane == lax.broadcasted_iota(jnp.int32, (count, 128), 0) + shift
+
+
+def to_row(column, shift=0):
+    return column_sum(jnp.where(eye(column.shape[0], shift), column, 0.0))
+
+
+def to_column(row, count):
+    spread = jnp.broadcast_to(row, (count, 128))
+    return jnp.sum(jnp.where(eye(count), spread, 0.0), axis=1, keepdims=True)
+
+
 def unit(re, im):
     scale = 1.0 / jnp.maximum(jnp.sqrt(re * re + im * im), FLOOR)
     return re * scale, im * scale
@@ -59,8 +73,11 @@
 def kernel(
     slc_hbm, nbr_hbm, ref, phases, comp,
     nbr, blocks, ext, lanes, tiles, zs, wbuf, red, kre, kim, cvec, bvec, xsum, zbuf, sbuf,
-    vbuf, msg, fmsg, fbuf, series, rmsg, rbuf1, rmsg2, rbuf2,
-    load_sem, halo_send, halo_recv, v_send, v_recv, f_send, f_recv, r_send, r_recv, ready,
+    vbuf, msg, fmsg, fbuf, series, datum,
+    nmsg, nbuf1, nmsg2, nbuf2, ncol, emsg, ebuf1, emsg2, ebuf2, eall, gmsg, gbuf, rmsg, rbuf1, bmsg, bbuf,
+    kref, kimf, cref, zref, sref,
+    load_sem, halo_send, halo_recv, v_send, v_recv, f_send, f_recv, n_send, n_recv, e_send, e_recv,
+    y_send, y_recv, g_send, g_recv, r_send, r_recv, b_send, b_recv, ready,
 ):
     sec = lax.axis_index("section")
     pix = lax.axis_index("pix")
@@ -81,6 +98,42 @@
         first.append((g // 2) * 16 + z * 2 + lax.rem(g, 2))
         second.append(x * 16 + lax.rem(z + d, 8) * 2 + core)
 
+    want = ref[0] - pix * (TILES * 128)
+
+    def at_ref(parts):
+        total = None
+        for t, part in enumerate(parts):
+            lane = lax.broadcasted_iota(jnp.int32, part.shape, 1)
+            part = jnp.where(lane == want - t * 128, part, 0.0)
+            total = part if total is None else total + part
+        return jnp.sum(total, axis=1, keepdims=True)
+
+    def copies(src, dst, send, recv, devices, base=0):
+        return [
+            remote(src, dst.at[i], send.at[base + i], recv.at[base + i], (sec, device))
+            for i, device in enumerate(devices)
+        ]
+
+    def start(made):
+        for copy in made:
+            copy.start()
+
+    def finish(made):
+        for copy in made:
+            copy.wait_send()
+            copy.wait_recv()
+
+    def sum_of(own, buffers):
+        total = own[...]
+        for i in range(7):
+            total = total + buffers[i]
+        return total
+
+    steps_n = copies(nmsg, nbuf1, n_send, n_recv, first), copies(nmsg2, nbuf2, n_send, n_recv, second, 7)
+    steps_e = copies(emsg, ebuf1, e_send, e_recv, first), copies(emsg2, ebuf2, e_send, e_recv, second, 7)
+    steps_r = copies(rmsg, rbuf1, r_send, r_recv, first)
+    steps_b = copies(bmsg, bbuf, b_send, b_recv, second)
+
     own_rows = pl.ds(0, FLAT)
     loads = [
         pltpu.make_async_copy(slc_hbm, blocks.at[1, own_rows], load_sem.at[0]),
@@ -176,6 +229,8 @@
 
     for t in range(TILES):
         gather(t, 2 - t, (3 - t,), True)
+    hear(ready.at[0])
+    tell(ready.at[1])
 
     for i, halo in zip((0, 2), halos):
         pl.when(present[i])(halo.wait_send)
@@ -185,8 +240,14 @@
 
     for t in range(TILES):
         gather(t, None, tuple(m for m in range(SPAN) if t + m not in (2, 3)), False)
-    hear(ready.at[0])
-    tell(ready.at[1])
+    hear(ready.at[1])
+    tell(ready.at[2])
+
+    @pl.when(sec == 2)
+    def _():
+        column = at_ref([nbr[:, t * 128 : (t + 1) * 128].astype(F32) for t in range(TILES)])
+        nmsg[...] = to_row(column)
+        start(steps_n[0])
 
     @pl.loop(0, TILES)
     def _(t):
@@ -259,8 +320,67 @@
                     cvec[t, 1, rows, :] = -START * fold(4 * kg + slot + 1, ci)
                 slot = 2 - slot
 
-    hear(ready.at[1])
-    tell(ready.at[2])
+    @pl.when(sec >= 2)
+    def _():
+        hear(ready.at[2])
+        tell(ready.at[3])
+
+    @pl.when(sec == 2)
+    def _():
+        finish(steps_n[0])
+        nmsg2[...] = sum_of(nmsg, nbuf1)
+        start(steps_n[1])
+
+    def expand():
+        for l in range(NB):
+            kref[0, l] = jnp.broadcast_to(eall[0:16, l : l + 1], (16, 128))
+            kimf[0, l] = jnp.broadcast_to(eall[0:16, 16 + l : 17 + l], (16, 128))
+        for c in range(2):
+            cref[0, c] = jnp.broadcast_to(eall[0:16, 32 + c : 33 + c], (16, 128))
+
+    @pl.when(sec == SECTIONS - 1)
+    def _():
+        lane = lax.broadcasted_iota(jnp.int32, (16, 128), 1)
+        emsg[16:32, :] = jnp.zeros((16, 128), F32)
+        acc = jnp.zeros((16, 128), F32)
+        for c in range(2):
+            acc = jnp.where(lane == 32 + c, at_ref([cvec[t, c] for t in range(TILES)]), acc)
+        emsg[0:16, :] = acc
+
+        @pl.loop(0, NB)
+        def _(k):
+            acc = emsg[0:16, :]
+            acc = jnp.where(lane == k, at_ref([kre[t, k] for t in range(TILES)]), acc)
+            emsg[0:16, :] = jnp.where(lane == 16 + k, at_ref([kim[t, k] for t in range(TILES)]), acc)
+            parts = [at_ref([zs[t, k, c] * wbuf[t] for t in range(TILES)]) for c in range(2)]
+            emsg[pl.ds(16 + k, 1), :] = to_row(parts[0]) + to_row(parts[1], 64)
+
+        start(steps_e[0])
+        finish(steps_e[0])
+        emsg2[...] = sum_of(emsg, ebuf1)
+        start(steps_e[1])
+        finish(steps_e[1])
+        eall[...] = sum_of(emsg2, ebuf2)
+        for j in range(SECTIONS - 1):
+            remote(eall.at[pl.ds(0, 16)], eall.at[pl.ds(0, 16)], y_send.at[j], y_recv, (j, pix)).start()
+        expand()
+
+    @pl.when(sec == 2)
+    def _():
+        finish(steps_n[1])
+        column = to_column(sum_of(nmsg2, nbuf2), 16)
+        row = lax.broadcasted_iota(jnp.int32, (16, 128), 0)
+        ncol[...] = jnp.where(row == NB, ref[0].astype(F32), column) - (pix * (TILES * 128)).astype(F32)
+
+    def add_date(kr, ki, zb, t, z0):
+        for l in range(NB):
+            lr = bcast(zb[t, 0, l : l + 1, :])
+            li = bcast(zb[t, 1, l : l + 1, :])
+            for kg in range(2):
+                rows = slice(8 * kg, 8 * kg + 8)
+                zr, zi = z0[kg]
+                kr[t, l, rows, :] = kr[t, l, rows, :] + (zr * lr + zi * li)
+                ki[t, l, rows, :] = ki[t, l, rows, :] + (zr * li - zi * lr)
 
     @pl.when(sec == 0)
     def _():
@@ -300,56 +420,53 @@
                 cvec[t, 1, rows, :] = cvec[t, 1, rows, :] - START * zi
                 bvec[t, 0, rows, :] = bvec[t, 0, rows, :] + (zr * vr + zi * vi)
                 bvec[t, 1, rows, :] = bvec[t, 1, rows, :] + (zr * vi - zi * vr)
-            for l in range(NB):
-                lr = bcast(zbuf[t, 0, l : l + 1, :])
-                li = bcast(zbuf[t, 1, l : l + 1, :])
-                for kg in range(2):
-                    rows = slice(8 * kg, 8 * kg + 8)
-                    zr, zi = z0[kg]
-                    kre[t, l, rows, :] = kre[t, l, rows, :] + (zr * lr + zi * li)
-                    kim[t, l, rows, :] = kim[t, l, rows, :] + (zr * li - zi * lr)
-
-    def product(state):
-        for i, (t, c, kg) in enumerate((t, c, kg) for t in range(TILES) for c in range(2) for kg in range(2)):
-            sbuf[t, c, 8 * kg : 8 * kg + 8, :] = state[i]
-        out = []
-        for t in range(TILES):
-            y = [[None, None], [None, None]]
-            for l in range(NB):
-                lr = bcast(sbuf[t, 0, l : l + 1, :])
-                li = bcast(sbuf[t, 1, l : l + 1, :])
-                for kg in range(2):
-                    rows = slice(8 * kg, 8 * kg + 8)
-                    ar, ai = kre[t, l, rows, :], kim[t, l, rows, :]
-                    re = ar * lr - ai * li
-                    im = ar * li + ai * lr
-                    y[0][kg] = re if l == 0 else y[0][kg] + re
-                    y[1][kg] = im if l == 0 else y[1][kg] + im
-            out += [y[0][0], y[0][1], y[1][0], y[1][1]]
-        return out
-
-    places = [(t, c, kg) for t in range(TILES) for c in range(2) for kg in range(2)]
-
-    def c0(i):
-        t, c, kg = places[i]
-        return cvec[t, c, 8 * kg : 8 * kg + 8, :]
-
-    def turn(_, state):
-        return tuple(a + y + c0(i) for i, (a, y) in enumerate(zip(state, product(state))))
-
-    state = lax.fori_loop(0, ITERS - 1, turn, tuple(c0(i) for i in range(8)))
-    state = [a * SCALE for a in state]
-    ks = product(state)
-    norms = []
+            add_date(kre, kim, zbuf, t, z0)
+
+    def solve(kr, ki, cv, sb, count):
+        places = [(t, c, kg) for t in range(count) for c in range(2) for kg in range(2)]
+
+        def product(state):
+            for i, (t, c, kg) in enumerate(places):
+                sb[t, c, 8 * kg : 8 * kg + 8, :] = state[i]
+            out = []
+            for t in range(count):
+                y = [[None, None], [None, None]]
+                for l in range(NB):
+                    lr = bcast(sb[t, 0, l : l + 1, :])
+                    li = bcast(sb[t, 1, l : l + 1, :])
+                    for kg in range(2):
+                        rows = slice(8 * kg, 8 * kg + 8)
+                        ar, ai = kr[t, l, rows, :], ki[t, l, rows, :]
+                        re = ar * lr - ai * li
+                        im = ar * li + ai * lr
+                        y[0][kg] = re if l == 0 else y[0][kg] + re
+                        y[1][kg] = im if l == 0 else y[1][kg] + im
+                out += [y[0][0], y[0][1], y[1][0], y[1][1]]
+            return out
+
+        def c0(i):
+            t, c, kg = places[i]
+            return cv[t, c, 8 * kg : 8 * kg + 8, :]
+
+        def turn(_, state):
+            return tuple(a + y + c0(i) for i, (a, y) in enumerate(zip(state, product(state))))
+
+        state = lax.fori_loop(0, ITERS - 1, turn, tuple(c0(i) for i in range(len(places))))
+        state = [a * SCALE for a in state]
+        ks = product(state)
+        norms = []
+        for t in range(count):
+            total = None
+            for i in range(4 * t, 4 * t + 4):
+                term = state[i] * (ks[i] + (2.0 * SCALE) * c0(i))
+                total = term if total is None else total + term
+            norms.append(lax.rsqrt(column_sum(total) + SCALE * SCALE))
+        return state, norms
+
+    state, norms = solve(kre, kim, cvec, sbuf, TILES)
     for t in range(TILES):
         s = state[4 * t : 4 * t + 4]
-        y = ks[4 * t : 4 * t + 4]
-        total = None
-        for i in range(4):
-            term = s[i] * (y[i] + (2.0 * SCALE) * c0(4 * t + i))
-            total = term if total is None else total + term
-        norm = lax.rsqrt(column_sum(total) + SCALE * SCALE)
-        norms.append(norm)
+        norm = norms[t]
         cr = ci = fr = fi = None
         for kg in range(2):
             rows = slice(8 * kg, 8 * kg + 8)
@@ -381,11 +498,44 @@
             for j in range(s):
                 remote(fmsg, fbuf.at[s - 1], f_send.at[j], f_recv.at[s - 1], (j, pix)).start()
 
-    hear(ready.at[2])
+    steps_g = [
+        (s, d, remote(gmsg, gbuf.at[d], g_send.at[8 * s + d], g_recv.at[d], (s, pix if d == 0 else first[d - 1])))
+        for s in range(SECTIONS)
+        for d in range(8)
+        if (s, d) != (2, 0)
+    ]
+
+    @pl.when(sec < 2)
+    def _():
+        hear(ready.at[2])
+        tell(ready.at[3])
+
+    hear(ready.at[3])
+
+    @pl.when(sec == 2)
+    def _():
+        lane = lax.broadcasted_iota(jnp.int32, (16, 128), 1).astype(F32)
+        row = lax.broadcasted_iota(jnp.int32, (16, 128), 0)
+        for c in range(2):
+            total = None
+            for t in range(TILES):
+                cols = slice(t * 128, (t + 1) * 128)
+                value = jnp.where(
+                    row == NB,
+                    jnp.broadcast_to(fmsg[c : c + 1, cols], (16, 128)),
+                    jnp.broadcast_to(msg[c : c + 1, cols], (16, 128)),
+                )
+                value = jnp.where(ncol[...] - t * 128.0 == lane, value, 0.0)
+                total = value if total is None else total + value
+            gmsg[c : c + 1, :] = to_row(jnp.sum(total, axis=1, keepdims=True))
+        for _, _, copy in steps_g:
+            copy.start()
+        gbuf[0] = gmsg[...]
+
     comp[0, 0:1, :] = msg[0:1, :]
     comp[1, 0:1, :] = msg[1:2, :]
 
-    for i, (t, c, kg) in enumerate(places):
+    for i, (t, c, kg) in enumerate((t, c, kg) for t in range(TILES) for c in range(2) for kg in range(2)):
         sbuf[t, c, 8 * kg : 8 * kg + 8, :] = state[i] * norms[t]
     for t in range(TILES):
 
@@ -404,58 +554,122 @@
             series[t, 0, rows, :] = bcast((SCALE * START) * norms[t]) + w * re
             series[t, 1, rows, :] = w * im
 
-    for s in range(SECTIONS - 1, 0, -1):
-
-        @pl.when(sec < s)
-        def _():
-            remote(fmsg, fbuf.at[s - 1], f_send.at[0], f_recv.at[s - 1], (s, pix)).wait_recv()
-            for t in range(TILES):
-                fr = fbuf[s - 1, 0:1, t * 128 : (t + 1) * 128]
-                fi = fbuf[s - 1, 1:2, t * 128 : (t + 1) * 128]
-                re, im = series[t, 0], series[t, 1]
-                series[t, 0] = re * fr - im * fi
-                series[t, 1] = re * fi + im * fr
-
-    want = ref[0] - pix * (TILES * 128)
-    lane = lax.broadcasted_iota(jnp.int32, (PAD, 128), 1)
-    diag = lane == lax.broadcasted_iota(jnp.int32, (PAD, 128), 0)
-    for c in range(2):
-        column = jnp.zeros((PAD, 128), F32)
+    def take_f(j):
+        remote(fmsg, fbuf.at[j - 1], f_send.at[0], f_recv.at[j - 1], (j, pix)).wait_recv()
+
+    @pl.when(sec == 0)
+    def _():
+        take_f(1)
         for t in range(TILES):
-            column = column + jnp.where(lane == want - t * 128, series[t, c], 0.0)
-        column = jnp.sum(column, axis=1, keepdims=True)
-        rmsg[c : c + 1, :] = column_sum(jnp.where(diag, column, 0.0))
-    copies = []
+            fr = fbuf[0, 0:1, t * 128 : (t + 1) * 128]
+            fi = fbuf[0, 1:2, t * 128 : (t + 1) * 128]
+            re, im = series[t, 0], series[t, 1]
+            series[t, 0] = re * fr - im * fi
+            series[t, 1] = re * fi + im * fr
+
+    @pl.when(sec < SECTIONS - 1)
+    def _():
+        for c in range(2):
+            rmsg[c : c + 1, :] = to_row(at_ref([series[t, c] for t in range(TILES)]))
+        start(steps_r)
+        remote(eall.at[pl.ds(0, 16)], eall.at[pl.ds(0, 16)], y_send.at[0], y_recv, (SECTIONS - 1, pix)).wait_recv()
+        expand()
+
+    for s, d, copy in steps_g:
+        if s == 0:
+            if d == 0:
+                pl.when(sec != 2)(copy.wait_recv)
+            else:
+                copy.wait_recv()
+    total = gbuf[0]
     for d in range(1, 8):
-        copies.append(remote(rmsg, rbuf1.at[d - 1], r_send.at[d - 1], r_recv.at[d - 1], (sec, first[d - 1])))
-        copies[-1].start()
-    for copy in copies:
-        copy.wait_recv()
-    total = rmsg[...]
-    for d in range(1, 8):
-        total = total + rbuf1[d - 1]
-    rmsg2[...] = total
-    for d in range(1, 8):
-        copies.append(remote(rmsg2, rbuf2.at[d - 1], r_send.at[6 + d], r_recv.at[6 + d], (sec, second[d - 1])))
-        copies[-1].start()
-    for copy in copies[7:]:
-        copy.wait_recv()
-    for d in range(1, 8):
-        total = total + rbuf2[d - 1]
-    u = []
-    for c in range(2):
-        u.append(jnp.sum(jnp.where(diag, jnp.broadcast_to(total[c : c + 1, :], (PAD, 128)), 0.0), axis=1, keepdims=True))
-    ur, ui = unit(u[0], u[1])
-    ur, ui = GAIN * ur, GAIN * ui
+        total = total + gbuf[d]
+    bmsg[2:4, :] = total
+
+    @pl.when(sec < SECTIONS - 1)
+    def _():
+        finish(steps_r)
+        bmsg[0:2, :] = sum_of(rmsg, rbuf1)
+
+    @pl.when(sec == SECTIONS - 1)
+    def _():
+        bmsg[0:2, :] = jnp.zeros((2, 128), F32)
+
+    start(steps_b)
+    finish(steps_b)
+    total = sum_of(bmsg, bbuf)
+
+    values = [to_column(total[2 + c : 3 + c, :], 16) for c in range(2)]
+    f2r, f2i = values[0][NB:16], values[1][NB:16]
+    row = lax.broadcasted_iota(jnp.int32, (16, 128), 0)
+    zr, zi = (jnp.where(row < NB, value, 0.0) for value in values)
+    w = lax.rsqrt(jnp.maximum(column_sum(zr * zr + zi * zi), 1.0))
+    zr, zi = zr * w, zi * w
+    zref[0, 0] = zr
+    zref[0, 1] = zi
+    cref[0, 0] = cref[0, 0] + START * zr
+    cref[0, 1] = cref[0, 1] - START * zi
+    add_date(kref, kimf, zref, 0, [(zr[0:8], zi[0:8]), (zr[8:16], zi[8:16])])
+    state_ref, norm_ref = solve(kref, kimf, cref, sref, 1)
+    sr = jnp.concatenate(state_ref[0:2], axis=0)
+    si = jnp.concatenate(state_ref[2:4], axis=0)
+    norm = norm_ref[0]
+    f3r = column_sum(zr * sr - zi * si)
+    f3i = column_sum(zr * si + zi * sr)
+    f3r, f3i = unit((f3r + SCALE * START) * norm, f3i * norm)
+    fr = jnp.where(sec < 2, f3r * f2r - f3i * f2i, f3r)
+    fi = jnp.where(sec < 2, f3r * f2i + f3i * f2r, f3i)
+    vr, vi = total[0:1, :], total[1:2, :]
+    rmsg[0:1, :] = vr * fr - vi * fi
+    rmsg[1:2, :] = vr * fi + vi * fr
+
+    @pl.when(sec == SECTIONS - 1)
+    def _():
+        z = eall[16:32, :]
+        a = bcast(column_sum(z * sr))
+        b = bcast(column_sum(z * si))
+        re = a - pltpu.roll(b, 64, 1)
+        im = b + pltpu.roll(a, 64, 1)
+        rmsg[0:1, :] = (re[0:1] + SCALE * START) * norm
+        rmsg[1:2, :] = im[0:1] * norm
+
+    ur, ui = unit(rmsg[0:1, :], rmsg[1:2, :])
+    ur, ui = GAIN * to_column(ur, PAD), GAIN * to_column(ui, PAD)
+
+    datum[0:1, :] = jnp.ones((1, TILES * 128), F32)
+    datum[1:2, :] = jnp.zeros((1, TILES * 128), F32)
+
+    @pl.when(sec < SECTIONS - 1)
+    def _():
+        take_f(3)
+        datum[...] = fbuf[2]
+
+    @pl.when(sec < 2)
+    def _():
+        take_f(2)
+        dr, di = datum[0:1, :], datum[1:2, :]
+        fr, fi = fbuf[1, 0:1, :], fbuf[1, 1:2, :]
+        datum[0:1, :] = dr * fr - di * fi
+        datum[1:2, :] = dr * fi + di * fr
+
     for t in range(TILES):
+        dr, di = datum[0:1, t * 128 : (t + 1) * 128], datum[1:2, t * 128 : (t + 1) * 128]
         re, im = series[t, 0], series[t, 1]
+        re, im = re * dr - im * di, re * di + im * dr
         for c, part in enumerate((re * ur + im * ui, im * ur - re * ui)):
             for g in range(GROUPS):
                 count = min(8, ROWS - g * 8)
                 phases[pl.ds(g * 32 + t * 2 + c, count, stride=4), :] = part[g * 8 : g * 8 + count]
 
-    for copy in copies:
-        copy.wait_send()
+    @pl.when(sec == 2)
+    def _():
+        for _, _, copy in steps_g:
+            copy.wait_send()
+
+    @pl.when(sec == SECTIONS - 1)
+    def _():
+        for j in range(SECTIONS - 1):
+            remote(eall.at[pl.ds(0, 16)], eall.at[pl.ds(0, 16)], y_send.at[j], y_recv, (j, pix)).wait_send()
 
     @pl.when(sec < SECTIONS - 1)
     def _():
@@ -505,10 +719,28 @@
             pltpu.VMEM((2, pixels), F32),
             pltpu.VMEM((3, 2, pixels), F32),
             pltpu.VMEM((TILES, 2, PAD, 128), F32),
+            pltpu.VMEM((2, pixels), F32),
+            pltpu.VMEM((1, 128), F32),
+            pltpu.VMEM((7, 1, 128), F32),
+            pltpu.VMEM((1, 128), F32),
+            pltpu.VMEM((7, 1, 128), F32),
+            pltpu.VMEM((16, 128), F32),
+            pltpu.VMEM((32, 128), F32),
+            pltpu.VMEM((7, 32, 128), F32),
+            pltpu.VMEM((32, 128), F32),
+            pltpu.VMEM((7, 32, 128), F32),
+            pltpu.VMEM((32, 128), F32),
+            pltpu.VMEM((2, 128), F32),
+            pltpu.VMEM((8, 2, 128), F32),
             pltpu.VMEM((2, 128), F32),
             pltpu.VMEM((7, 2, 128), F32),
-            pltpu.VMEM((2, 128), F32),
-            pltpu.VMEM((7, 2, 128), F32),
+            pltpu.VMEM((4, 128), F32),
+            pltpu.VMEM((7, 4, 128), F32),
+            pltpu.VMEM((1, 16, 16, 128), F32),
+            pltpu.VMEM((1, 16, 16, 128), F32),
+            pltpu.VMEM((1, 2, 16, 128), F32),
+            pltpu.VMEM((1, 2, 16, 128), F32),
+            pltpu.VMEM((1, 2, 16, 128), F32),
             dma((2,)),
             dma((2,)),
             dma((2,)),
@@ -518,7 +750,17 @@
             dma((3,)),
             dma((14,)),
             dma((14,)),
-            pltpu.SemaphoreType.REGULAR((3,)),
+            dma((14,)),
+            dma((14,)),
+            dma((3,)),
+            dma(()),
+            dma((32,)),
+            dma((8,)),
+            dma((7,)),
+            dma((7,)),
+            dma((7,)),
+            dma((7,)),
+            pltpu.SemaphoreType.REGULAR((4,)),
         ],
         compiler_params=pltpu.CompilerParams(
             collective_id=0, has_side_effects=True, vmem_limit_bytes=16 * 2**20

time: 46.5 us -> 41.4 us (0.89)
  Pallas kernels: 43.9 us -> 38.8 us
    pallas_call x1, Pallas kernels: 43.9 us -> 38.8 us  [on_device(): pl.pallas_call(kernel, out_shape=(jax.ShapeDtypeStruct((FLAT, 128), F32),...]
where the time goes in v5:
time: 41.4 us; the launch traced here: 41.3 us
  Pallas kernels  38.8 us (94%)
  between operations  1.28 us (3%)
  local copies, waits for them, and re-layouts  1.22 us (3%)
    pallas_call x1, Pallas kernels, on_device(): pl.pallas_call(kernel, out_shape=(jax.ShapeDtypeStruct((FLAT, 128), F32),...  38.8 us
    unnamed x2, local copies, waits for them, and re-layouts  1.22 us

profile of v5, /device:TPU:1, one launch (start us, length us, event | category | flops | bytes accessed | tf_op | source)
XLA Modules:
  0.0 41.3 jit_solution(5915937342533700558)
XLA Ops:
  1.3 38.8 %shard_map.50 = (f32[200,128]{1,0:T(8,128)S(1)}, f32[2,1,256]{2,1,0:T(1,128)S(1)}) custom-call(f32[200,128]{1,0:T(8,128)} %bitcast.11, s32[15,256]{1,0:T(8,128)} %nbr_hbm.1, s32[1]{0:T(128)S(6)} %copy.9.ref), custom_call_target="tpu_custom_call" | custom-call | flops 100000000 | bytes 1000000 | tf_op jit(solution)/shard_map/pallas_call | solution.py:693
  40.0 0.6 %copy.10 = f32[2,50,256]{2,0,1:T(2,128)} copy(f32[2,50,256]{2,0,1:T(2,128)S(1)} %bitcast.10) | data formatting | bytes 204800
  40.7 0.6 %copy.11 = f32[2,1,256]{2,1,0:T(1,128)} copy(f32[2,1,256]{2,1,0:T(1,128)S(1)} %get-tuple-element.9) | data formatting | bytes 4096

commit v6 on v5

--- a/solution.py
+++ b/solution.py
@@ -76,8 +76,8 @@
     vbuf, msg, fmsg, fbuf, series, datum,
     nmsg, nbuf1, nmsg2, nbuf2, ncol, emsg, ebuf1, emsg2, ebuf2, eall, gmsg, gbuf, rmsg, rbuf1, bmsg, bbuf,
     kref, kimf, cref, zref, sref,
-    load_sem, halo_send, halo_recv, v_send, v_recv, f_send, f_recv, n_send, n_recv, e_send, e_recv,
-    y_send, y_recv, g_send, g_recv, r_send, r_recv, b_send, b_recv, ready,
+    load_sem, halo_send, halo_recv, v_send, v_recv, f_send, f_recv, early_sem,
+    y_send, y_recv, g_send, g_recv, r_sem, b_sem, ready,
 ):
     sec = lax.axis_index("section")
     pix = lax.axis_index("pix")
@@ -85,6 +85,7 @@
     after = lax.rem(pix + 1, PIX)
     near = (before, pix, after)
     present = (pix > 0, pix >= 0, pix < PIX - 1)
+    inner = jnp.logical_and(present[0], present[2])
     sec_up = lax.rem(sec + 1, SECTIONS)
     sec_down = lax.rem(sec + (SECTIONS - 1), SECTIONS)
     x = pix // 16
@@ -108,20 +109,16 @@
             total = part if total is None else total + part
         return jnp.sum(total, axis=1, keepdims=True)
 
-    def copies(src, dst, send, recv, devices, base=0):
-        return [
-            remote(src, dst.at[i], send.at[base + i], recv.at[base + i], (sec, device))
-            for i, device in enumerate(devices)
-        ]
-
-    def start(made):
-        for copy in made:
-            copy.start()
-
-    def finish(made):
-        for copy in made:
-            copy.wait_send()
-            copy.wait_recv()
+    def arrived(ref, sem):
+        pltpu.make_async_copy(ref, ref, sem).wait()
+
+    def start(src, dst, sem, devices):
+        for i, device in enumerate(devices):
+            remote(src, dst.at[i], sem.at[0], sem.at[1], (sec, device)).start()
+
+    def finish(src, dst, sem, devices):
+        arrived(dst, sem.at[0])
+        arrived(dst, sem.at[1])
 
     def sum_of(own, buffers):
         total = own[...]
@@ -129,16 +126,17 @@
             total = total + buffers[i]
         return total
 
-    steps_n = copies(nmsg, nbuf1, n_send, n_recv, first), copies(nmsg2, nbuf2, n_send, n_recv, second, 7)
-    steps_e = copies(emsg, ebuf1, e_send, e_recv, first), copies(emsg2, ebuf2, e_send, e_recv, second, 7)
-    steps_r = copies(rmsg, rbuf1, r_send, r_recv, first)
-    steps_b = copies(bmsg, bbuf, b_send, b_recv, second)
-
-    own_rows = pl.ds(0, FLAT)
+    steps_n = (nmsg, nbuf1, early_sem.at[0], first), (nmsg2, nbuf2, early_sem.at[1], second)
+    steps_e = (emsg, ebuf1, early_sem.at[0], first), (emsg2, ebuf2, early_sem.at[1], second)
+    steps_r = (rmsg, rbuf1, r_sem, first)
+    steps_b = (bmsg, bbuf, b_sem, second)
+
+    chunks = [(0, 3), (3, GROUPS)]
+    spans = [pl.ds(32 * low, min(32 * high, FLAT) - 32 * low) for low, high in chunks]
     loads = [
-        pltpu.make_async_copy(slc_hbm, blocks.at[1, own_rows], load_sem.at[0]),
-        pltpu.make_async_copy(nbr_hbm, nbr, load_sem.at[1]),
+        pltpu.make_async_copy(slc_hbm.at[span], blocks.at[1, span], load_sem.at[i]) for i, span in enumerate(spans)
     ]
+    loads.append(pltpu.make_async_copy(nbr_hbm, nbr, load_sem.at[2]))
     for load in loads:
         load.start()
     barrier = pltpu.get_barrier_semaphore()
@@ -154,6 +152,18 @@
         pl.semaphore_wait(sem, len(peers))
 
     tell(barrier)
+    hear(barrier)
+    tell(ready.at[0])
+
+    def halo(i, n):
+        part = blocks.at[1, spans[n]]
+        return remote(part, blocks.at[2 - i, spans[n]], halo_send.at[i // 2], halo_recv.at[i // 2, n], (sec, near[i]))
+
+    for n in range(len(chunks)):
+        loads[n].wait()
+        for i in (0, 2):
+            pl.when(present[i])(halo(i, n).start)
+
     for i in range(3):
         blocks[i, FLAT:, :] = jnp.zeros((32 * GROUPS - FLAT, 128), F32)
     kre[...] = jnp.zeros_like(kre)
@@ -168,19 +178,7 @@
             blocks[i] = jnp.zeros((32 * GROUPS, 128), F32)
             vbuf[i] = jnp.zeros_like(vbuf[i])
 
-    hear(barrier)
-    tell(ready.at[0])
-
-    loads[0].wait()
-    halos = [
-        remote(blocks.at[1, own_rows], blocks.at[2 - i, own_rows], halo_send.at[i // 2], halo_recv.at[i // 2], (sec, near[i]))
-        for i in (0, 2)
-    ]
-    for i, halo in zip((0, 2), halos):
-        pl.when(present[i])(halo.start)
-
-    for load in loads[1:]:
-        load.wait()
+    loads[2].wait()
 
     base = pix * (TILES * 128) - REACH
     for t in range(TILES):
@@ -190,8 +188,8 @@
         lanes[t, NB : NB + 1, :] = jnp.zeros((1, 128), jnp.int32)
         tiles[t, NB : NB + 1, :] = jnp.full((1, 128), SPAN, jnp.int32)
 
-    def spread(i):
-        for g in range(GROUPS):
+    def spread(i, groups=range(GROUPS)):
+        for g in groups:
             for m in range(2):
                 for c in range(2):
                     ext[2 * i + m, c, g * 8 : (g + 1) * 8, :] = blocks[i, pl.ds(g * 32 + m * 2 + c, 8, stride=4), :]
@@ -207,7 +205,7 @@
             xsum[t, c : c + 1, :] = column_sum(total)
         zs[t, 0, 2] = zs[t, 0, 0] - zs[t, 0, 1]
 
-    def gather(t, mine, theirs, begin):
+    def gather(t, mine, theirs, begin, groups=range(GROUPS)):
         @pl.loop(0, 2)
         def _(half):
             for i in range(NB // 2):
@@ -215,7 +213,7 @@
                 lane = bcast(lanes[t, pl.ds(k, 1), :])
                 tile = bcast(tiles[t, pl.ds(k, 1), :])
                 here = [tile == m for m in theirs]
-                for g in range(GROUPS):
+                for g in groups:
                     rows = slice(g * 8, (g + 1) * 8)
                     pair = []
                     for c in range(2):
@@ -232,14 +230,13 @@
     hear(ready.at[0])
     tell(ready.at[1])
 
-    for i, halo in zip((0, 2), halos):
-        pl.when(present[i])(halo.wait_send)
-        pl.when(present[2 - i])(halo.wait_recv)
-    spread(0)
-    spread(2)
-
-    for t in range(TILES):
-        gather(t, None, tuple(m for m in range(SPAN) if t + m not in (2, 3)), False)
+    for n, (low, high) in enumerate(chunks):
+        for i in (0, 2):
+            pl.when(present[2 - i])(halo(i, n).wait_recv)
+        for i in (0, 2):
+            spread(i, range(low, high))
+        for t in range(TILES):
+            gather(t, None, tuple(m for m in range(SPAN) if t + m not in (2, 3)), False, range(low, high))
     hear(ready.at[1])
     tell(ready.at[2])
 
@@ -247,7 +244,7 @@
     def _():
         column = at_ref([nbr[:, t * 128 : (t + 1) * 128].astype(F32) for t in range(TILES)])
         nmsg[...] = to_row(column)
-        start(steps_n[0])
+        start(*steps_n[0])
 
     @pl.loop(0, TILES)
     def _(t):
@@ -327,9 +324,9 @@
 
     @pl.when(sec == 2)
     def _():
-        finish(steps_n[0])
+        finish(*steps_n[0])
         nmsg2[...] = sum_of(nmsg, nbuf1)
-        start(steps_n[1])
+        start(*steps_n[1])
 
     def expand():
         for l in range(NB):
@@ -355,19 +352,19 @@
             parts = [at_ref([zs[t, k, c] * wbuf[t] for t in range(TILES)]) for c in range(2)]
             emsg[pl.ds(16 + k, 1), :] = to_row(parts[0]) + to_row(parts[1], 64)
 
-        start(steps_e[0])
-        finish(steps_e[0])
+        start(*steps_e[0])
+        finish(*steps_e[0])
         emsg2[...] = sum_of(emsg, ebuf1)
-        start(steps_e[1])
-        finish(steps_e[1])
+        start(*steps_e[1])
+        finish(*steps_e[1])
         eall[...] = sum_of(emsg2, ebuf2)
         for j in range(SECTIONS - 1):
-            remote(eall.at[pl.ds(0, 16)], eall.at[pl.ds(0, 16)], y_send.at[j], y_recv, (j, pix)).start()
+            remote(eall.at[pl.ds(0, 16)], eall.at[pl.ds(0, 16)], y_send, y_recv, (j, pix)).start()
         expand()
 
     @pl.when(sec == 2)
     def _():
-        finish(steps_n[1])
+        finish(*steps_n[1])
         column = to_column(sum_of(nmsg2, nbuf2), 16)
         row = lax.broadcasted_iota(jnp.int32, (16, 128), 0)
         ncol[...] = jnp.where(row == NB, ref[0].astype(F32), column) - (pix * (TILES * 128)).astype(F32)
@@ -388,8 +385,8 @@
 
     @pl.when(sec > 0)
     def _():
-        for i in range(3):
-            pl.when(present[i])(remote(msg, vbuf.at[i], v_send.at[i], v_recv.at[i], (sec_down, near[i])).wait_recv)
+        pl.when(inner)(lambda: arrived(vbuf, v_recv))
+        pl.when(jnp.logical_not(inner))(lambda: arrived(vbuf.at[0:2], v_recv))
         for t in range(TILES):
             z0 = []
             for kg in range(2):
@@ -489,17 +486,17 @@
     @pl.when(sec < SECTIONS - 1)
     def _():
         for i in range(3):
-            pl.when(present[i])(remote(msg, vbuf.at[2 - i], v_send.at[i], v_recv.at[2 - i], (sec_up, near[i])).start)
+            pl.when(present[i])(remote(msg, vbuf.at[2 - i], v_send, v_recv, (sec_up, near[i])).start)
 
     for s in range(1, SECTIONS):
 
         @pl.when(sec == s)
         def _():
             for j in range(s):
-                remote(fmsg, fbuf.at[s - 1], f_send.at[j], f_recv.at[s - 1], (j, pix)).start()
+                remote(fmsg, fbuf.at[s - 1], f_send, f_recv.at[s - 1], (j, pix)).start()
 
     steps_g = [
-        (s, d, remote(gmsg, gbuf.at[d], g_send.at[8 * s + d], g_recv.at[d], (s, pix if d == 0 else first[d - 1])))
+        remote(gmsg, gbuf.at[d], g_send, g_recv, (s, pix if d == 0 else first[d - 1]))
         for s in range(SECTIONS)
         for d in range(8)
         if (s, d) != (2, 0)
@@ -528,7 +525,7 @@
                 value = jnp.where(ncol[...] - t * 128.0 == lane, value, 0.0)
                 total = value if total is None else total + value
             gmsg[c : c + 1, :] = to_row(jnp.sum(total, axis=1, keepdims=True))
-        for _, _, copy in steps_g:
+        for copy in steps_g:
             copy.start()
         gbuf[0] = gmsg[...]
 
@@ -555,7 +552,7 @@
             series[t, 1, rows, :] = w * im
 
     def take_f(j):
-        remote(fmsg, fbuf.at[j - 1], f_send.at[0], f_recv.at[j - 1], (j, pix)).wait_recv()
+        arrived(fbuf.at[j - 1], f_recv.at[j - 1])
 
     @pl.when(sec == 0)
     def _():
@@ -571,16 +568,18 @@
     def _():
         for c in range(2):
             rmsg[c : c + 1, :] = to_row(at_ref([series[t, c] for t in range(TILES)]))
-        start(steps_r)
-        remote(eall.at[pl.ds(0, 16)], eall.at[pl.ds(0, 16)], y_send.at[0], y_recv, (SECTIONS - 1, pix)).wait_recv()
+        start(*steps_r)
+        remote(eall.at[pl.ds(0, 16)], eall.at[pl.ds(0, 16)], y_send, y_recv, (SECTIONS - 1, pix)).wait_recv()
         expand()
 
-    for s, d, copy in steps_g:
-        if s == 0:
-            if d == 0:
-                pl.when(sec != 2)(copy.wait_recv)
-            else:
-                copy.wait_recv()
+    @pl.when(sec == 2)
+    def _():
+        arrived(gbuf.at[1:8], g_recv)
+
+    @pl.when(sec != 2)
+    def _():
+        arrived(gbuf.at[0:8], g_recv)
+
     total = gbuf[0]
     for d in range(1, 8):
         total = total + gbuf[d]
@@ -588,15 +587,15 @@
 
     @pl.when(sec < SECTIONS - 1)
     def _():
-        finish(steps_r)
+        finish(*steps_r)
         bmsg[0:2, :] = sum_of(rmsg, rbuf1)
 
     @pl.when(sec == SECTIONS - 1)
     def _():
         bmsg[0:2, :] = jnp.zeros((2, 128), F32)
 
-    start(steps_b)
-    finish(steps_b)
+    start(*steps_b)
+    finish(*steps_b)
     total = sum_of(bmsg, bbuf)
 
     values = [to_column(total[2 + c : 3 + c, :], 16) for c in range(2)]
@@ -661,27 +660,37 @@
                 count = min(8, ROWS - g * 8)
                 phases[pl.ds(g * 32 + t * 2 + c, count, stride=4), :] = part[g * 8 : g * 8 + count]
 
+    for i in (0, 2):
+        pl.when(present[i])(lambda i=i: arrived(blocks.at[1, pl.ds(0, FLAT)], halo_send.at[i // 2]))
     @pl.when(sec == 2)
     def _():
-        for _, _, copy in steps_g:
-            copy.wait_send()
+        arrived(gbuf, g_send)
 
     @pl.when(sec == SECTIONS - 1)
     def _():
-        for j in range(SECTIONS - 1):
-            remote(eall.at[pl.ds(0, 16)], eall.at[pl.ds(0, 16)], y_send.at[j], y_recv, (j, pix)).wait_send()
+        arrived(ebuf1.at[0:3, 0:16], y_send)
 
     @pl.when(sec < SECTIONS - 1)
     def _():
-        for i in range(3):
-            pl.when(present[i])(remote(msg, vbuf.at[2 - i], v_send.at[i], v_recv.at[2 - i], (sec_up, near[i])).wait_send)
+        pl.when(inner)(lambda: arrived(vbuf, v_send))
+        pl.when(jnp.logical_not(inner))(lambda: arrived(vbuf.at[0:2], v_send))
 
     for s in range(1, SECTIONS):
 
         @pl.when(sec == s)
         def _():
-            for j in range(s):
-                remote(fmsg, fbuf.at[s - 1], f_send.at[j], f_recv.at[s - 1], (j, pix)).wait_send()
+            arrived(fbuf.at[0:s], f_send)
+
+
+def hand_out(phases_in, comp_in, phases, comp, sem):
+    copies = [
+        pltpu.make_async_copy(phases_in, phases, sem.at[0]),
+        pltpu.make_async_copy(comp_in, comp, sem.at[1]),
+    ]
+    for copy in copies:
+        copy.start()
+    for copy in copies:
+        copy.wait()
 
 
 def on_device(slc, neighbours, reference_pixel):
@@ -731,7 +740,7 @@
             pltpu.VMEM((7, 32, 128), F32),
             pltpu.VMEM((32, 128), F32),
             pltpu.VMEM((2, 128), F32),
-            pltpu.VMEM((8, 2, 128), F32),
+            pltpu.VMEM((31, 2, 128), F32),
             pltpu.VMEM((2, 128), F32),
             pltpu.VMEM((7, 2, 128), F32),
             pltpu.VMEM((4, 128), F32),
@@ -741,25 +750,20 @@
             pltpu.VMEM((1, 2, 16, 128), F32),
             pltpu.VMEM((1, 2, 16, 128), F32),
             pltpu.VMEM((1, 2, 16, 128), F32),
+            dma((3,)),
+            dma((2,)),
+            dma((2, 2)),
+            dma(()),
+            dma(()),
+            dma(()),
+            dma((3,)),
+            dma((2, 2)),
+            dma(()),
+            dma(()),
+            dma(()),
+            dma(()),
             dma((2,)),
             dma((2,)),
-            dma((2,)),
-            dma((3,)),
-            dma((3,)),
-            dma((3,)),
-            dma((3,)),
-            dma((14,)),
-            dma((14,)),
-            dma((14,)),
-            dma((14,)),
-            dma((3,)),
-            dma(()),
-            dma((32,)),
-            dma((8,)),
-            dma((7,)),
-            dma((7,)),
-            dma((7,)),
-            dma((7,)),
             pltpu.SemaphoreType.REGULAR((4,)),
         ],
         compiler_params=pltpu.CompilerParams(
@@ -767,6 +771,17 @@
         ),
         cost_estimate=pl.CostEstimate(flops=100_000_000, bytes_accessed=1_000_000, transcendentals=0),
     )(*(pltpu.with_memory_space_constraint(a, pltpu.HBM) for a in (flat, neighbours)), reference_pixel)
+    phases, comp = pl.pallas_call(
+        hand_out,
+        out_shape=(
+            jax.ShapeDtypeStruct((FLAT, 128), F32),
+            jax.ShapeDtypeStruct((2, 1, pixels), F32),
+        ),
+        in_specs=[pl.BlockSpec(memory_space=pl.ANY)] * 2,
+        out_specs=(hbm, hbm),
+        scratch_shapes=[dma((2,))],
+        compiler_params=pltpu.CompilerParams(vmem_limit_bytes=2**20),
+    )(phases, comp)
     return phases.reshape(ROWS, TILES, 2, 128).transpose(2, 0, 1, 3).reshape(2, ROWS, pixels), comp
 
 

time: 41.4 us -> 39.5 us (0.954)
  local copies, waits for them, and re-layouts: 1.22 us -> 0 us
  Pallas kernels: 38.8 us -> 38.1 us
    pallas_call x1, Pallas kernels: 38.8 us -> 37.4 us  [on_device(): pl.pallas_call(kernel, out_shape=(jax.ShapeDtypeStruct((FLAT, 128), F32),...]
    unnamed x2 -> x0, local copies, waits for them, and re-layouts: 1.22 us -> none
    pallas_call x0 -> x1, Pallas kernels: none -> 0.66 us  [on_device(): pl.pallas_call(hand_out, out_shape=(jax.ShapeDtypeStruct((FLAT, 128), F32...]
where the time goes in v6:
time: 39.5 us; the launch traced here: 39.4 us
  Pallas kernels  38.1 us (96%)
  between operations  1.28 us (3%)
    pallas_call x1, Pallas kernels, on_device(): pl.pallas_call(kernel, out_shape=(jax.ShapeDtypeStruct((FLAT, 128), F32),...  37.4 us

profile of v6, /device:TPU:1, one launch (start us, length us, event | category | flops | bytes accessed | tf_op | source)
XLA Modules:
  0.0 39.4 jit_solution(17007655638905852369)
XLA Ops:
  1.3 37.4 %shard_map.50 = (f32[200,128]{1,0:T(8,128)S(1)}, f32[2,1,256]{2,1,0:T(1,128)S(1)}) custom-call(f32[200,128]{1,0:T(8,128)} %bitcast.10, s32[15,256]{1,0:T(8,128)} %nbr_hbm.1, s32[1]{0:T(128)S(6)} %copy.7.ref), custom_call_target="tpu_custom_call" | custom-call | flops 100000000 | bytes 1000000 | tf_op jit(solution)/shard_map/pallas_call | solution.py:702
  38.7 0.7 %shard_map.51 = (f32[200,128]{1,0:T(8,128)}, f32[2,1,256]{2,1,0:T(1,128)}) custom-call(f32[200,128]{1,0:T(8,128)S(1)} %get-tuple-element.6.phases_in, f32[2,1,256]{2,1,0:T(1,128)S(1)} %get-tuple-element.7.comp_in), custom_call_target="tpu_custom_call" | custom-call | tf_op jit(solution)/shard_map/pallas_call | solution.py:774

commit v7 on v6

--- a/solution.py
+++ b/solution.py
@@ -203,40 +203,51 @@
                 zs[t, 0, c, g * 8 : (g + 1) * 8, :] = own
                 total = own if total is None else total + own
             xsum[t, c : c + 1, :] = column_sum(total)
-        zs[t, 0, 2] = zs[t, 0, 0] - zs[t, 0, 1]
-
-    def gather(t, mine, theirs, begin, groups=range(GROUPS)):
-        @pl.loop(0, 2)
-        def _(half):
+
+    def gather(t, offsets, begin, groups=range(GROUPS), halves=None):
+        def some(half):
             for i in range(NB // 2):
                 k = 1 + half * (NB // 2) + i
                 lane = bcast(lanes[t, pl.ds(k, 1), :])
                 tile = bcast(tiles[t, pl.ds(k, 1), :])
-                here = [tile == m for m in theirs]
                 for g in groups:
                     rows = slice(g * 8, (g + 1) * 8)
-                    pair = []
                     for c in range(2):
-                        out = take(ext[t + mine, c, rows, :], lane) if begin else zs[t, k, c, rows, :]
-                        for there, m in zip(here, theirs):
-                            out = jnp.where(there, take(ext[t + m, c, rows, :], lane), out)
+                        out = None if begin else zs[t, k, c, rows, :]
+                        for m in offsets:
+                            got = take(ext[t + m, c, rows, :], lane)
+                            out = got if out is None else jnp.where(tile == m, got, out)
                         zs[t, k, c, rows, :] = out
-                        pair.append(out)
-                    if not begin:
-                        zs[t, k, 2, rows, :] = pair[0] - pair[1]
+
+        if halves is None:
+            pl.loop(0, 2)(some)
+        else:
+            for half in halves:
+                some(half)
 
     for t in range(TILES):
-        gather(t, 2 - t, (3 - t,), True)
+        gather(t, (2 - t, 3 - t), True)
     hear(ready.at[0])
     tell(ready.at[1])
 
-    for n, (low, high) in enumerate(chunks):
-        for i in (0, 2):
-            pl.when(present[2 - i])(halo(i, n).wait_recv)
-        for i in (0, 2):
-            spread(i, range(low, high))
-        for t in range(TILES):
-            gather(t, None, tuple(m for m in range(SPAN) if t + m not in (2, 3)), False, range(low, high))
+    def side(s, groups, halves=None):
+        spread(2 * s, groups)
+        close, distant = 1 + 3 * s, 5 * s
+        gather(s, (close - s, distant - s), False, groups, halves)
+        gather(1 - s, (close - (1 - s),), False, groups, halves)
+
+    def both(soon):
+        late = 1 - soon
+        for n in range(len(chunks)):
+            arrived(blocks.at[2 * soon, spans[n]], halo_recv.at[1 - soon, n])
+        side(soon, range(GROUPS))
+        for n, (low, high) in enumerate(chunks):
+            pl.when(inner)(lambda n=n: arrived(blocks.at[2 * late, spans[n]], halo_recv.at[1 - late, n]))
+            side(late, range(low, high), range(2))
+
+    pl.when(core == 0)(lambda: both(1))
+    pl.when(core == 1)(lambda: both(0))
+
     hear(ready.at[1])
     tell(ready.at[2])
 
@@ -253,6 +264,7 @@
             power = None
             for k in range(NB):
                 re, im = zs[t, k, 0, rows, :], zs[t, k, 1, rows, :]
+                zs[t, k, 2, rows, :] = re - im
                 term = re * re + im * im
                 power = term if power is None else power + term
             wbuf[t, rows, :] = lax.rsqrt(jnp.maximum(power, 1.0))
@@ -483,18 +495,6 @@
         fmsg[0:1, cols] = fr
         fmsg[1:2, cols] = fi
 
-    @pl.when(sec < SECTIONS - 1)
-    def _():
-        for i in range(3):
-            pl.when(present[i])(remote(msg, vbuf.at[2 - i], v_send, v_recv, (sec_up, near[i])).start)
-
-    for s in range(1, SECTIONS):
-
-        @pl.when(sec == s)
-        def _():
-            for j in range(s):
-                remote(fmsg, fbuf.at[s - 1], f_send, f_recv.at[s - 1], (j, pix)).start()
-
     steps_g = [
         remote(gmsg, gbuf.at[d], g_send, g_recv, (s, pix if d == 0 else first[d - 1]))
         for s in range(SECTIONS)
@@ -502,15 +502,9 @@
         if (s, d) != (2, 0)
     ]
 
-    @pl.when(sec < 2)
-    def _():
-        hear(ready.at[2])
-        tell(ready.at[3])
-
-    hear(ready.at[3])
-
     @pl.when(sec == 2)
     def _():
+        hear(ready.at[3])
         lane = lax.broadcasted_iota(jnp.int32, (16, 128), 1).astype(F32)
         row = lax.broadcasted_iota(jnp.int32, (16, 128), 0)
         for c in range(2):
@@ -529,27 +523,48 @@
             copy.start()
         gbuf[0] = gmsg[...]
 
+    @pl.when(sec < SECTIONS - 1)
+    def _():
+        for i in range(3):
+            pl.when(present[i])(remote(msg, vbuf.at[2 - i], v_send, v_recv, (sec_up, near[i])).start)
+
+    for s in range(1, SECTIONS):
+
+        @pl.when(sec == s)
+        def _():
+            for j in range(s):
+                remote(fmsg, fbuf.at[s - 1], f_send, f_recv.at[s - 1], (j, pix)).start()
+
+    @pl.when(sec < 2)
+    def _():
+        hear(ready.at[2])
+        tell(ready.at[3])
+
+    pl.when(sec != 2)(lambda: hear(ready.at[3]))
     comp[0, 0:1, :] = msg[0:1, :]
     comp[1, 0:1, :] = msg[1:2, :]
 
-    for i, (t, c, kg) in enumerate((t, c, kg) for t in range(TILES) for c in range(2) for kg in range(2)):
-        sbuf[t, c, 8 * kg : 8 * kg + 8, :] = state[i] * norms[t]
-    for t in range(TILES):
-
-        @pl.loop(0, GROUPS)
-        def _(g):
-            rows = pl.ds(pl.multiple_of(g * 8, 8), 8)
-            re = im = None
-            for k in range(NB):
-                sr = bcast(sbuf[t, 0, k : k + 1, :])
-                si = bcast(sbuf[t, 1, k : k + 1, :])
-                zr, zi = zs[t, k, 0, rows, :], zs[t, k, 1, rows, :]
-                a, b = zr * sr - zi * si, zr * si + zi * sr
-                re = a if re is None else re + a
-                im = b if im is None else im + b
-            w = wbuf[t, rows, :]
-            series[t, 0, rows, :] = bcast((SCALE * START) * norms[t]) + w * re
-            series[t, 1, rows, :] = w * im
+    def vector():
+        for i, (t, c, kg) in enumerate((t, c, kg) for t in range(TILES) for c in range(2) for kg in range(2)):
+            sbuf[t, c, 8 * kg : 8 * kg + 8, :] = state[i] * norms[t]
+        for t in range(TILES):
+
+            @pl.loop(0, GROUPS)
+            def _(g):
+                rows = pl.ds(pl.multiple_of(g * 8, 8), 8)
+                re = im = None
+                for k in range(NB):
+                    sr = bcast(sbuf[t, 0, k : k + 1, :])
+                    si = bcast(sbuf[t, 1, k : k + 1, :])
+                    zr, zi = zs[t, k, 0, rows, :], zs[t, k, 1, rows, :]
+                    a, b = zr * sr - zi * si, zr * si + zi * sr
+                    re = a if re is None else re + a
+                    im = b if im is None else im + b
+                w = wbuf[t, rows, :]
+                series[t, 0, rows, :] = bcast((SCALE * START) * norms[t]) + w * re
+                series[t, 1, rows, :] = w * im
+
+    pl.when(sec < SECTIONS - 1)(vector)
 
     def take_f(j):
         arrived(fbuf.at[j - 1], f_recv.at[j - 1])
@@ -595,6 +610,7 @@
         bmsg[0:2, :] = jnp.zeros((2, 128), F32)
 
     start(*steps_b)
+    pl.when(sec == SECTIONS - 1)(vector)
     finish(*steps_b)
     total = sum_of(bmsg, bbuf)
 

time: 39.5 us -> 38.7 us (0.980)
  Pallas kernels: 38.1 us -> 37.2 us
    pallas_call x1, Pallas kernels: 37.4 us -> 36.5 us  [on_device(): pl.pallas_call(kernel, out_shape=(jax.ShapeDtypeStruct((FLAT, 128), F32),...]
where the time goes in v7:
time: 38.7 us; the launch traced here: 38.5 us
  Pallas kernels  37.2 us (96%)
  between operations  1.28 us (3%)
    pallas_call x1, Pallas kernels, on_device(): pl.pallas_call(kernel, out_shape=(jax.ShapeDtypeStruct((FLAT, 128), F32),...  36.5 us

profile of v7, /device:TPU:1, one launch (start us, length us, event | category | flops | bytes accessed | tf_op | source)
XLA Modules:
  0.0 38.5 jit_solution(7007633879439144909)
XLA Ops:
  1.3 36.5 %shard_map.50 = (f32[200,128]{1,0:T(8,128)S(1)}, f32[2,1,256]{2,1,0:T(1,128)S(1)}) custom-call(f32[200,128]{1,0:T(8,128)} %bitcast.10, s32[15,256]{1,0:T(8,128)} %nbr_hbm.1, s32[1]{0:T(128)S(6)} %copy.7.ref), custom_call_target="tpu_custom_call" | custom-call | flops 100000000 | bytes 1000000 | tf_op jit(solution)/shard_map/pallas_call | solution.py:718
  37.8 0.7 %shard_map.51 = (f32[200,128]{1,0:T(8,128)}, f32[2,1,256]{2,1,0:T(1,128)}) custom-call(f32[200,128]{1,0:T(8,128)S(1)} %get-tuple-element.6.phases_in, f32[2,1,256]{2,1,0:T(1,128)S(1)} %get-tuple-element.7.comp_in), custom_call_target="tpu_custom_call" | custom-call | tf_op jit(solution)/shard_map/pallas_call | solution.py:790

commit v8 on v7

--- a/solution.py
+++ b/solution.py
@@ -75,7 +75,7 @@
     nbr, blocks, ext, lanes, tiles, zs, wbuf, red, kre, kim, cvec, bvec, xsum, zbuf, sbuf,
     vbuf, msg, fmsg, fbuf, series, datum,
     nmsg, nbuf1, nmsg2, nbuf2, ncol, emsg, ebuf1, emsg2, ebuf2, eall, gmsg, gbuf, rmsg, rbuf1, bmsg, bbuf,
-    kref, kimf, cref, zref, sref,
+    kref, kimf, cref, zref, sref, kre2, kim2, qvec, gvec, result, inverse, kref2, kimf2, qref, gref,
     load_sem, halo_send, halo_recv, v_send, v_recv, f_send, f_recv, early_sem,
     y_send, y_recv, g_send, g_recv, r_sem, b_sem, ready,
 ):
@@ -329,10 +329,135 @@
                     cvec[t, 1, rows, :] = -START * fold(4 * kg + slot + 1, ci)
                 slot = 2 - slot
 
+    def pieces(count):
+        return [(t, c, kg) for t in range(count) for c in range(2) for kg in range(2)]
+
+    def load(ref, count):
+        return [ref[t, c, 8 * kg : 8 * kg + 8, :] for t, c, kg in pieces(count)]
+
+    def save(ref, value):
+        for (t, c, kg), part in zip(pieces(len(value) // 4), value):
+            ref[t, c, 8 * kg : 8 * kg + 8, :] = part
+
+    def plus(*values):
+        return [sum(parts[1:], parts[0]) for parts in zip(*values)]
+
+    def times(factor, value):
+        return [factor * part for part in value]
+
+    def product(mr, mi, box, value):
+        save(box, value)
+        out = []
+        for t in range(len(value) // 4):
+            y = [[None, None], [None, None]]
+            for l in range(NB):
+                lr = bcast(box[t, 0, l : l + 1, :])
+                li = bcast(box[t, 1, l : l + 1, :])
+                for kg in range(2):
+                    rows = slice(8 * kg, 8 * kg + 8)
+                    ar, ai = mr[t, l, rows, :], mi[t, l, rows, :]
+                    re = ar * lr - ai * li
+                    im = ar * li + ai * lr
+                    y[0][kg] = re if l == 0 else y[0][kg] + re
+                    y[1][kg] = im if l == 0 else y[1][kg] + im
+            out += [y[0][0], y[0][1], y[1][0], y[1][1]]
+        return out
+
+    def prepare(mr, mi, sr, si, cv, qv, box, count):
+        for t in range(count):
+
+            @pl.loop(0, NB)
+            def _(l):
+                for kg in range(2):
+                    rows = slice(8 * kg, 8 * kg + 8)
+                    re, im = 2.0 * mr[t, l, rows, :], 2.0 * mi[t, l, rows, :]
+                    for m in range(NB):
+                        lr = bcast(mr[t, l, m : m + 1, :])
+                        li = bcast(mi[t, l, m : m + 1, :])
+                        ar, ai = mr[t, m, rows, :], mi[t, m, rows, :]
+                        re = re + (ar * lr - ai * li)
+                        im = im + (ar * li + ai * lr)
+                    sr[t, l, rows, :] = re
+                    si[t, l, rows, :] = im
+
+        save(qv, product(mr, mi, box, load(cv, count)))
+
+    def joined(z, value):
+        out = []
+        for t in range(len(value) // 4):
+            zr, zi = z[4 * t : 4 * t + 2], z[4 * t + 2 : 4 * t + 4]
+            vr, vi = value[4 * t : 4 * t + 2], value[4 * t + 2 : 4 * t + 4]
+            ar = column_sum(zr[0] * vr[0] - zi[0] * vi[0] + (zr[1] * vr[1] - zi[1] * vi[1]))
+            ai = column_sum(zr[0] * vi[0] + zi[0] * vr[0] + (zr[1] * vi[1] + zi[1] * vr[1]))
+            out += [zr[i] * ar + zi[i] * ai for i in range(2)] + [zr[i] * ai - zi[i] * ar for i in range(2)]
+        return out
+
+    def conj(value):
+        return [part if (i // 2) % 2 == 0 else -part for i, part in enumerate(value)]
+
+    def norms_of(value, image, start):
+        out = []
+        for t in range(len(value) // 4):
+            total = None
+            for i in range(4 * t, 4 * t + 4):
+                term = value[i] * (image[i] + (2.0 * SCALE) * start[i])
+                total = term if total is None else total + term
+            out.append(lax.rsqrt(column_sum(total) + SCALE * SCALE))
+        return out
+
+    def solve(mr, mi, cv, box, count):
+        def turn(_, value):
+            return tuple(plus(value, product(mr, mi, box, value), load(cv, count)))
+
+        value = lax.fori_loop(0, ITERS - 1, turn, tuple(load(cv, count)))
+        value = times(SCALE, value)
+        return value, norms_of(value, product(mr, mi, box, value), load(cv, count))
+
+    def solve_joined(mr, mi, sr, si, cv, qv, zv, box, gbox, count):
+        z = load(zv, count)
+        r = conj(z)
+        kr = product(mr, mi, box, r)
+        c = plus(load(cv, count), times(START, r))
+        save(cv, c)
+        g = plus(r, kr)
+        for t in range(count):
+            squares = [z[4 * t + i] * z[4 * t + i] for i in range(4)]
+            half = 0.5 * column_sum(squares[0] + squares[1] + (squares[2] + squares[3]))
+            for i in range(4 * t, 4 * t + 4):
+                g[i] = g[i] + half * r[i]
+        save(gbox, g)
+        for t in range(count):
+            for l in range(NB):
+                zr, zi = bcast(zv[t, 0, l : l + 1, :]), bcast(zv[t, 1, l : l + 1, :])
+                gr, gi = bcast(gbox[t, 0, l : l + 1, :]), bcast(gbox[t, 1, l : l + 1, :])
+                for kg in range(2):
+                    rows = slice(8 * kg, 8 * kg + 8)
+                    hr, hi = g[4 * t + kg], g[4 * t + 2 + kg]
+                    xr, xi = z[4 * t + kg], z[4 * t + 2 + kg]
+                    sr[t, l, rows, :] = sr[t, l, rows, :] + (hr * zr - hi * zi + (xr * gr - xi * gi))
+                    si[t, l, rows, :] = si[t, l, rows, :] + (hr * zi + hi * zr - (xr * gi + xi * gr))
+
+        def square(value):
+            return plus(value, product(sr, si, box, value))
+
+        value = plus(c, c, load(qv, count), times(START, kr), joined(z, c))
+        value = plus(value, square(value))
+        value = plus(value, square(square(value)))
+
+        last = lax.fori_loop(0, 4, lambda _, v: tuple(square(v)), tuple(value))
+        value = times(SCALE, plus(value, last))
+        image = plus(product(mr, mi, box, value), joined(z, value))
+        return value, norms_of(value, image, c)
+
     @pl.when(sec >= 2)
     def _():
         hear(ready.at[2])
         tell(ready.at[3])
+
+    def prepare_own():
+        prepare(kre, kim, kre2, kim2, cvec, qvec, sbuf, TILES)
+
+    pl.when(jnp.logical_or(sec == 1, sec == 2))(prepare_own)
 
     @pl.when(sec == 2)
     def _():
@@ -346,6 +471,7 @@
             kimf[0, l] = jnp.broadcast_to(eall[0:16, 16 + l : 17 + l], (16, 128))
         for c in range(2):
             cref[0, c] = jnp.broadcast_to(eall[0:16, 32 + c : 33 + c], (16, 128))
+        prepare(kref, kimf, kref2, kimf2, cref, qref, sref, 1)
 
     @pl.when(sec == SECTIONS - 1)
     def _():
@@ -365,6 +491,7 @@
             emsg[pl.ds(16 + k, 1), :] = to_row(parts[0]) + to_row(parts[1], 64)
 
         start(*steps_e[0])
+        prepare_own()
         finish(*steps_e[0])
         emsg2[...] = sum_of(emsg, ebuf1)
         start(*steps_e[1])
@@ -381,15 +508,29 @@
         row = lax.broadcasted_iota(jnp.int32, (16, 128), 0)
         ncol[...] = jnp.where(row == NB, ref[0].astype(F32), column) - (pix * (TILES * 128)).astype(F32)
 
-    def add_date(kr, ki, zb, t, z0):
-        for l in range(NB):
-            lr = bcast(zb[t, 0, l : l + 1, :])
-            li = bcast(zb[t, 1, l : l + 1, :])
-            for kg in range(2):
-                rows = slice(8 * kg, 8 * kg + 8)
-                zr, zi = z0[kg]
-                kr[t, l, rows, :] = kr[t, l, rows, :] + (zr * lr + zi * li)
-                ki[t, l, rows, :] = ki[t, l, rows, :] + (zr * li - zi * lr)
+    def step_one():
+        @pl.when(sec == 2)
+        def _():
+            arrived(gbuf.at[1:8], g_recv)
+
+        @pl.when(sec != 2)
+        def _():
+            arrived(gbuf.at[0:8], g_recv)
+
+        total = gbuf[0]
+        for d in range(1, 8):
+            total = total + gbuf[d]
+        bmsg[2:4, :] = total
+        bmsg[0:2, :] = jnp.zeros((2, 128), F32)
+
+        @pl.when(sec < SECTIONS - 1)
+        def _():
+            finish(*steps_r)
+            bmsg[0:2, :] = sum_of(rmsg, rbuf1)
+
+        start(*steps_b)
+
+    pl.when(sec == SECTIONS - 1)(step_one)
 
     @pl.when(sec == 0)
     def _():
@@ -422,57 +563,22 @@
             for kg in range(2):
                 rows = slice(8 * kg, 8 * kg + 8)
                 zr, zi = z0[kg][0] * w, z0[kg][1] * w
-                z0[kg] = (zr, zi)
                 zbuf[t, 0, rows, :] = zr
                 zbuf[t, 1, rows, :] = zi
-                cvec[t, 0, rows, :] = cvec[t, 0, rows, :] + START * zr
-                cvec[t, 1, rows, :] = cvec[t, 1, rows, :] - START * zi
                 bvec[t, 0, rows, :] = bvec[t, 0, rows, :] + (zr * vr + zi * vi)
                 bvec[t, 1, rows, :] = bvec[t, 1, rows, :] + (zr * vi - zi * vr)
-            add_date(kre, kim, zbuf, t, z0)
-
-    def solve(kr, ki, cv, sb, count):
-        places = [(t, c, kg) for t in range(count) for c in range(2) for kg in range(2)]
-
-        def product(state):
-            for i, (t, c, kg) in enumerate(places):
-                sb[t, c, 8 * kg : 8 * kg + 8, :] = state[i]
-            out = []
-            for t in range(count):
-                y = [[None, None], [None, None]]
-                for l in range(NB):
-                    lr = bcast(sb[t, 0, l : l + 1, :])
-                    li = bcast(sb[t, 1, l : l + 1, :])
-                    for kg in range(2):
-                        rows = slice(8 * kg, 8 * kg + 8)
-                        ar, ai = kr[t, l, rows, :], ki[t, l, rows, :]
-                        re = ar * lr - ai * li
-                        im = ar * li + ai * lr
-                        y[0][kg] = re if l == 0 else y[0][kg] + re
-                        y[1][kg] = im if l == 0 else y[1][kg] + im
-                out += [y[0][0], y[0][1], y[1][0], y[1][1]]
-            return out
-
-        def c0(i):
-            t, c, kg = places[i]
-            return cv[t, c, 8 * kg : 8 * kg + 8, :]
-
-        def turn(_, state):
-            return tuple(a + y + c0(i) for i, (a, y) in enumerate(zip(state, product(state))))
-
-        state = lax.fori_loop(0, ITERS - 1, turn, tuple(c0(i) for i in range(len(places))))
-        state = [a * SCALE for a in state]
-        ks = product(state)
-        norms = []
-        for t in range(count):
-            total = None
-            for i in range(4 * t, 4 * t + 4):
-                term = state[i] * (ks[i] + (2.0 * SCALE) * c0(i))
-                total = term if total is None else total + term
-            norms.append(lax.rsqrt(column_sum(total) + SCALE * SCALE))
-        return state, norms
-
-    state, norms = solve(kre, kim, cvec, sbuf, TILES)
+
+    def keep(solved):
+        value, norms = solved
+        save(result, value)
+        for t, norm in enumerate(norms):
+            inverse[t] = norm
+
+    pl.when(sec == 0)(lambda: keep(solve(kre, kim, cvec, sbuf, TILES)))
+    pl.when(sec > 0)(lambda: keep(solve_joined(kre, kim, kre2, kim2, cvec, qvec, zbuf, sbuf, gvec, TILES)))
+
+    state = load(result, TILES)
+    norms = [inverse[t] for t in range(TILES)]
     for t in range(TILES):
         s = state[4 * t : 4 * t + 4]
         norm = norms[t]
@@ -546,7 +652,7 @@
 
     def vector():
         for i, (t, c, kg) in enumerate((t, c, kg) for t in range(TILES) for c in range(2) for kg in range(2)):
-            sbuf[t, c, 8 * kg : 8 * kg + 8, :] = state[i] * norms[t]
+            sbuf[t, c, 8 * kg : 8 * kg + 8, :] = result[t, c, 8 * kg : 8 * kg + 8, :] * inverse[t]
         for t in range(TILES):
 
             @pl.loop(0, GROUPS)
@@ -561,7 +667,7 @@
                     re = a if re is None else re + a
                     im = b if im is None else im + b
                 w = wbuf[t, rows, :]
-                series[t, 0, rows, :] = bcast((SCALE * START) * norms[t]) + w * re
+                series[t, 0, rows, :] = bcast((SCALE * START) * inverse[t]) + w * re
                 series[t, 1, rows, :] = w * im
 
     pl.when(sec < SECTIONS - 1)(vector)
@@ -584,33 +690,16 @@
         for c in range(2):
             rmsg[c : c + 1, :] = to_row(at_ref([series[t, c] for t in range(TILES)]))
         start(*steps_r)
+
+    pl.when(sec < SECTIONS - 1)(step_one)
+
+    pl.when(sec == SECTIONS - 1)(vector)
+
+    @pl.when(sec < SECTIONS - 1)
+    def _():
         remote(eall.at[pl.ds(0, 16)], eall.at[pl.ds(0, 16)], y_send, y_recv, (SECTIONS - 1, pix)).wait_recv()
         expand()
 
-    @pl.when(sec == 2)
-    def _():
-        arrived(gbuf.at[1:8], g_recv)
-
-    @pl.when(sec != 2)
-    def _():
-        arrived(gbuf.at[0:8], g_recv)
-
-    total = gbuf[0]
-    for d in range(1, 8):
-        total = total + gbuf[d]
-    bmsg[2:4, :] = total
-
-    @pl.when(sec < SECTIONS - 1)
-    def _():
-        finish(*steps_r)
-        bmsg[0:2, :] = sum_of(rmsg, rbuf1)
-
-    @pl.when(sec == SECTIONS - 1)
-    def _():
-        bmsg[0:2, :] = jnp.zeros((2, 128), F32)
-
-    start(*steps_b)
-    pl.when(sec == SECTIONS - 1)(vector)
     finish(*steps_b)
     total = sum_of(bmsg, bbuf)
 
@@ -622,10 +711,7 @@
     zr, zi = zr * w, zi * w
     zref[0, 0] = zr
     zref[0, 1] = zi
-    cref[0, 0] = cref[0, 0] + START * zr
-    cref[0, 1] = cref[0, 1] - START * zi
-    add_date(kref, kimf, zref, 0, [(zr[0:8], zi[0:8]), (zr[8:16], zi[8:16])])
-    state_ref, norm_ref = solve(kref, kimf, cref, sref, 1)
+    state_ref, norm_ref = solve_joined(kref, kimf, kref2, kimf2, cref, qref, zref, sref, gref, 1)
     sr = jnp.concatenate(state_ref[0:2], axis=0)
     si = jnp.concatenate(state_ref[2:4], axis=0)
     norm = norm_ref[0]
@@ -766,6 +852,16 @@
             pltpu.VMEM((1, 2, 16, 128), F32),
             pltpu.VMEM((1, 2, 16, 128), F32),
             pltpu.VMEM((1, 2, 16, 128), F32),
+            pltpu.VMEM((TILES, 16, 16, 128), F32),
+            pltpu.VMEM((TILES, 16, 16, 128), F32),
+            pltpu.VMEM((TILES, 2, 16, 128), F32),
+            pltpu.VMEM((TILES, 2, 16, 128), F32),
+            pltpu.VMEM((TILES, 2, 16, 128), F32),
+            pltpu.VMEM((TILES, 1, 128), F32),
+            pltpu.VMEM((1, 16, 16, 128), F32),
+            pltpu.VMEM((1, 16, 16, 128), F32),
+            pltpu.VMEM((1, 2, 16, 128), F32),
+            pltpu.VMEM((1, 2, 16, 128), F32),
             dma((3,)),
             dma((2,)),
             dma((2, 2)),

time: 38.7 us -> 37.5 us (0.969)
  Pallas kernels: 37.2 us -> 36.1 us
    pallas_call x1, Pallas kernels: 36.5 us -> 35.4 us  [on_device(): pl.pallas_call(kernel, out_shape=(jax.ShapeDtypeStruct((FLAT, 128), F32),...]
where the time goes in v8:
time: 37.5 us; the launch traced here: 37.4 us
  Pallas kernels  36.1 us (96%)
  between operations  1.28 us (3%)
    pallas_call x1, Pallas kernels, on_device(): pl.pallas_call(kernel, out_shape=(jax.ShapeDtypeStruct((FLAT, 128), F32),...  35.4 us

profile of v8, /device:TPU:1, one launch (start us, length us, event | category | flops | bytes accessed | tf_op | source)
XLA Modules:
  0.0 37.4 jit_solution(9865136750420568216)
XLA Ops:
  1.3 35.4 %shard_map.50 = (f32[200,128]{1,0:T(8,128)S(1)}, f32[2,1,256]{2,1,0:T(1,128)S(1)}) custom-call(f32[200,128]{1,0:T(8,128)} %bitcast.10, s32[15,256]{1,0:T(8,128)} %nbr_hbm.1, s32[1]{0:T(128)S(6)} %copy.7.ref), custom_call_target="tpu_custom_call" | custom-call | flops 100000000 | bytes 1000000 | tf_op jit(solution)/shard_map/pallas_call | solution.py:804
  36.7 0.7 %shard_map.51 = (f32[200,128]{1,0:T(8,128)}, f32[2,1,256]{2,1,0:T(1,128)}) custom-call(f32[200,128]{1,0:T(8,128)S(1)} %get-tuple-element.6.phases_in, f32[2,1,256]{2,1,0:T(1,128)S(1)} %get-tuple-element.7.comp_in), custom_call_target="tpu_custom_call" | custom-call | tf_op jit(solution)/shard_map/pallas_call | solution.py:886

commit v9 on v8

--- a/solution.py
+++ b/solution.py
@@ -76,6 +76,7 @@
     vbuf, msg, fmsg, fbuf, series, datum,
     nmsg, nbuf1, nmsg2, nbuf2, ncol, emsg, ebuf1, emsg2, ebuf2, eall, gmsg, gbuf, rmsg, rbuf1, bmsg, bbuf,
     kref, kimf, cref, zref, sref, kre2, kim2, qvec, gvec, result, inverse, kref2, kimf2, qref, gref,
+    ksum, ksum2, ksumf, ksumf2,
     load_sem, halo_send, halo_recv, v_send, v_recv, f_send, f_recv, early_sem,
     y_send, y_recv, g_send, g_recv, r_sem, b_sem, ready,
 ):
@@ -227,8 +228,6 @@
 
     for t in range(TILES):
         gather(t, (2 - t, 3 - t), True)
-    hear(ready.at[0])
-    tell(ready.at[1])
 
     def side(s, groups, halves=None):
         spread(2 * s, groups)
@@ -241,6 +240,8 @@
         for n in range(len(chunks)):
             arrived(blocks.at[2 * soon, spans[n]], halo_recv.at[1 - soon, n])
         side(soon, range(GROUPS))
+        hear(ready.at[0])
+        tell(ready.at[1])
         for n, (low, high) in enumerate(chunks):
             pl.when(inner)(lambda n=n: arrived(blocks.at[2 * late, spans[n]], halo_recv.at[1 - late, n]))
             side(late, range(low, high), range(2))
@@ -248,8 +249,10 @@
     pl.when(core == 0)(lambda: both(1))
     pl.when(core == 1)(lambda: both(0))
 
-    hear(ready.at[1])
-    tell(ready.at[2])
+    @pl.when(sec >= 2)
+    def _():
+        hear(ready.at[1])
+        tell(ready.at[2])
 
     @pl.when(sec == 2)
     def _():
@@ -328,6 +331,7 @@
                     cvec[t, 0, rows, :] = START * fold(4 * kg + slot, cr)
                     cvec[t, 1, rows, :] = -START * fold(4 * kg + slot + 1, ci)
                 slot = 2 - slot
+        ksum[t] = kre[t] + kim[t]
 
     def pieces(count):
         return [(t, c, kg) for t in range(count) for c in range(2) for kg in range(2)]
@@ -345,25 +349,28 @@
     def times(factor, value):
         return [factor * part for part in value]
 
-    def product(mr, mi, box, value):
-        save(box, value)
+    def product(m, box, value):
+        for t in range(len(value) // 4):
+            for kg in range(2):
+                re, im = value[4 * t + kg], value[4 * t + 2 + kg]
+                for c, part in enumerate((re, im, re + im)):
+                    box[t, c, 8 * kg : 8 * kg + 8, :] = part
         out = []
         for t in range(len(value) // 4):
-            y = [[None, None], [None, None]]
+            y = [[None, None] for _ in range(3)]
             for l in range(NB):
-                lr = bcast(box[t, 0, l : l + 1, :])
-                li = bcast(box[t, 1, l : l + 1, :])
-                for kg in range(2):
-                    rows = slice(8 * kg, 8 * kg + 8)
-                    ar, ai = mr[t, l, rows, :], mi[t, l, rows, :]
-                    re = ar * lr - ai * li
-                    im = ar * li + ai * lr
-                    y[0][kg] = re if l == 0 else y[0][kg] + re
-                    y[1][kg] = im if l == 0 else y[1][kg] + im
-            out += [y[0][0], y[0][1], y[1][0], y[1][1]]
+                for c in range(3):
+                    row = bcast(box[t, c, l : l + 1, :])
+                    for kg in range(2):
+                        part = m[c][t, l, 8 * kg : 8 * kg + 8, :] * row
+                        y[c][kg] = part if l == 0 else y[c][kg] + part
+            out += [y[0][kg] - y[1][kg] for kg in range(2)]
+            out += [y[2][kg] - (y[0][kg] + y[1][kg]) for kg in range(2)]
         return out
 
-    def prepare(mr, mi, sr, si, cv, qv, box, count):
+    def prepare(m3, s3, cv, qv, box, count):
+        mr, mi, _ = m3
+        sr, si, _ = s3
         for t in range(count):
 
             @pl.loop(0, NB)
@@ -380,7 +387,7 @@
                     sr[t, l, rows, :] = re
                     si[t, l, rows, :] = im
 
-        save(qv, product(mr, mi, box, load(cv, count)))
+        save(qv, product(m3, box, load(cv, count)))
 
     def joined(z, value):
         out = []
@@ -405,20 +412,19 @@
             out.append(lax.rsqrt(column_sum(total) + SCALE * SCALE))
         return out
 
-    def solve(mr, mi, cv, box, count):
+    def solve(m3, cv, box, count):
         def turn(_, value):
-            return tuple(plus(value, product(mr, mi, box, value), load(cv, count)))
+            return tuple(plus(value, product(m3, box, value), load(cv, count)))
 
         value = lax.fori_loop(0, ITERS - 1, turn, tuple(load(cv, count)))
         value = times(SCALE, value)
-        return value, norms_of(value, product(mr, mi, box, value), load(cv, count))
-
-    def solve_joined(mr, mi, sr, si, cv, qv, zv, box, gbox, count):
+        return value, norms_of(value, product(m3, box, value), load(cv, count))
+
+    def solve_joined(m3, s3, cv, qv, zv, box, gbox, count):
         z = load(zv, count)
         r = conj(z)
-        kr = product(mr, mi, box, r)
+        kr = product(m3, box, r)
         c = plus(load(cv, count), times(START, r))
-        save(cv, c)
         g = plus(r, kr)
         for t in range(count):
             squares = [z[4 * t + i] * z[4 * t + i] for i in range(4)]
@@ -426,6 +432,7 @@
             for i in range(4 * t, 4 * t + 4):
                 g[i] = g[i] + half * r[i]
         save(gbox, g)
+        sr, si, both = s3
         for t in range(count):
             for l in range(NB):
                 zr, zi = bcast(zv[t, 0, l : l + 1, :]), bcast(zv[t, 1, l : l + 1, :])
@@ -434,11 +441,14 @@
                     rows = slice(8 * kg, 8 * kg + 8)
                     hr, hi = g[4 * t + kg], g[4 * t + 2 + kg]
                     xr, xi = z[4 * t + kg], z[4 * t + 2 + kg]
-                    sr[t, l, rows, :] = sr[t, l, rows, :] + (hr * zr - hi * zi + (xr * gr - xi * gi))
-                    si[t, l, rows, :] = si[t, l, rows, :] + (hr * zi + hi * zr - (xr * gi + xi * gr))
+                    re = sr[t, l, rows, :] + (hr * zr - hi * zi + (xr * gr - xi * gi))
+                    im = si[t, l, rows, :] + (hr * zi + hi * zr - (xr * gi + xi * gr))
+                    sr[t, l, rows, :] = re
+                    si[t, l, rows, :] = im
+                    both[t, l, rows, :] = re + im
 
         def square(value):
-            return plus(value, product(sr, si, box, value))
+            return plus(value, product(s3, box, value))
 
         value = plus(c, c, load(qv, count), times(START, kr), joined(z, c))
         value = plus(value, square(value))
@@ -446,22 +456,24 @@
 
         last = lax.fori_loop(0, 4, lambda _, v: tuple(square(v)), tuple(value))
         value = times(SCALE, plus(value, last))
-        image = plus(product(mr, mi, box, value), joined(z, value))
+        image = plus(product(m3, box, value), joined(z, value))
         return value, norms_of(value, image, c)
 
-    @pl.when(sec >= 2)
-    def _():
+    @pl.when(sec == 1)
+    def _():
+        hear(ready.at[1])
+        tell(ready.at[2])
+
+    def prepare_own():
+        prepare((kre, kim, ksum), (kre2, kim2, ksum2), cvec, qvec, sbuf, TILES)
+
+    pl.when(jnp.logical_or(sec == 1, sec == 2))(prepare_own)
+
+    @pl.when(sec == 2)
+    def _():
+        finish(*steps_n[0])
         hear(ready.at[2])
         tell(ready.at[3])
-
-    def prepare_own():
-        prepare(kre, kim, kre2, kim2, cvec, qvec, sbuf, TILES)
-
-    pl.when(jnp.logical_or(sec == 1, sec == 2))(prepare_own)
-
-    @pl.when(sec == 2)
-    def _():
-        finish(*steps_n[0])
         nmsg2[...] = sum_of(nmsg, nbuf1)
         start(*steps_n[1])
 
@@ -471,7 +483,8 @@
             kimf[0, l] = jnp.broadcast_to(eall[0:16, 16 + l : 17 + l], (16, 128))
         for c in range(2):
             cref[0, c] = jnp.broadcast_to(eall[0:16, 32 + c : 33 + c], (16, 128))
-        prepare(kref, kimf, kref2, kimf2, cref, qref, sref, 1)
+        ksumf[...] = kref[...] + kimf[...]
+        prepare((kref, kimf, ksumf), (kref2, kimf2, ksumf2), cref, qref, sref, 1)
 
     @pl.when(sec == SECTIONS - 1)
     def _():
@@ -493,6 +506,8 @@
         start(*steps_e[0])
         prepare_own()
         finish(*steps_e[0])
+        hear(ready.at[2])
+        tell(ready.at[3])
         emsg2[...] = sum_of(emsg, ebuf1)
         start(*steps_e[1])
         finish(*steps_e[1])
@@ -532,9 +547,16 @@
 
     pl.when(sec == SECTIONS - 1)(step_one)
 
+    def keep(solved):
+        value, norms = solved
+        save(result, value)
+        for t, norm in enumerate(norms):
+            inverse[t] = norm
+
     @pl.when(sec == 0)
     def _():
         zbuf[...] = jnp.zeros_like(zbuf)
+        keep(solve((kre, kim, ksum), cvec, sbuf, TILES))
 
     @pl.when(sec > 0)
     def _():
@@ -567,15 +589,7 @@
                 zbuf[t, 1, rows, :] = zi
                 bvec[t, 0, rows, :] = bvec[t, 0, rows, :] + (zr * vr + zi * vi)
                 bvec[t, 1, rows, :] = bvec[t, 1, rows, :] + (zr * vi - zi * vr)
-
-    def keep(solved):
-        value, norms = solved
-        save(result, value)
-        for t, norm in enumerate(norms):
-            inverse[t] = norm
-
-    pl.when(sec == 0)(lambda: keep(solve(kre, kim, cvec, sbuf, TILES)))
-    pl.when(sec > 0)(lambda: keep(solve_joined(kre, kim, kre2, kim2, cvec, qvec, zbuf, sbuf, gvec, TILES)))
+        keep(solve_joined((kre, kim, ksum), (kre2, kim2, ksum2), cvec, qvec, zbuf, sbuf, gvec, TILES))
 
     state = load(result, TILES)
     norms = [inverse[t] for t in range(TILES)]
@@ -641,6 +655,11 @@
             for j in range(s):
                 remote(fmsg, fbuf.at[s - 1], f_send, f_recv.at[s - 1], (j, pix)).start()
 
+    @pl.when(sec == 0)
+    def _():
+        hear(ready.at[1])
+        tell(ready.at[2])
+
     @pl.when(sec < 2)
     def _():
         hear(ready.at[2])
@@ -711,7 +730,7 @@
     zr, zi = zr * w, zi * w
     zref[0, 0] = zr
     zref[0, 1] = zi
-    state_ref, norm_ref = solve_joined(kref, kimf, kref2, kimf2, cref, qref, zref, sref, gref, 1)
+    state_ref, norm_ref = solve_joined((kref, kimf, ksumf), (kref2, kimf2, ksumf2), cref, qref, zref, sref, gref, 1)
     sr = jnp.concatenate(state_ref[0:2], axis=0)
     si = jnp.concatenate(state_ref[2:4], axis=0)
     norm = norm_ref[0]
@@ -824,7 +843,7 @@
             pltpu.VMEM((TILES, 2, 16, 128), F32),
             pltpu.VMEM((TILES, 2, 128), F32),
             pltpu.VMEM((TILES, 2, 16, 128), F32),
-            pltpu.VMEM((TILES, 2, 16, 128), F32),
+            pltpu.VMEM((TILES, 3, 16, 128), F32),
             pltpu.VMEM((3, 2, pixels), F32),
             pltpu.VMEM((2, pixels), F32),
             pltpu.VMEM((2, pixels), F32),
@@ -851,7 +870,7 @@
             pltpu.VMEM((1, 16, 16, 128), F32),
             pltpu.VMEM((1, 2, 16, 128), F32),
             pltpu.VMEM((1, 2, 16, 128), F32),
-            pltpu.VMEM((1, 2, 16, 128), F32),
+            pltpu.VMEM((1, 3, 16, 128), F32),
             pltpu.VMEM((TILES, 16, 16, 128), F32),
             pltpu.VMEM((TILES, 16, 16, 128), F32),
             pltpu.VMEM((TILES, 2, 16, 128), F32),
@@ -862,6 +881,10 @@
             pltpu.VMEM((1, 16, 16, 128), F32),
             pltpu.VMEM((1, 2, 16, 128), F32),
             pltpu.VMEM((1, 2, 16, 128), F32),
+            pltpu.VMEM((TILES, 16, 16, 128), F32),
+            pltpu.VMEM((TILES, 16, 16, 128), F32),
+            pltpu.VMEM((1, 16, 16, 128), F32),
+            pltpu.VMEM((1, 16, 16, 128), F32),
             dma((3,)),
             dma((2,)),
             dma((2, 2)),

time: 37.5 us -> 37 us (0.987)
  Pallas kernels: 36.1 us -> 35.6 us
    pallas_call x1, Pallas kernels: 35.4 us -> 34.9 us  [on_device(): pl.pallas_call(kernel, out_shape=(jax.ShapeDtypeStruct((FLAT, 128), F32),...]
where the time goes in v9:
time: 37 us; the launch traced here: 36.9 us
  Pallas kernels  35.6 us (96%)
  between operations  1.28 us (3%)
    pallas_call x1, Pallas kernels, on_device(): pl.pallas_call(kernel, out_shape=(jax.ShapeDtypeStruct((FLAT, 128), F32),...  34.9 us

profile of v9, /device:TPU:1, one launch (start us, length us, event | category | flops | bytes accessed | tf_op | source)
XLA Modules:
  0.0 36.9 jit_solution(18319034263491801484)
XLA Ops:
  1.3 34.9 %shard_map.50 = (f32[200,128]{1,0:T(8,128)S(1)}, f32[2,1,256]{2,1,0:T(1,128)S(1)}) custom-call(f32[200,128]{1,0:T(8,128)} %bitcast.10, s32[15,256]{1,0:T(8,128)} %nbr_hbm.1, s32[1]{0:T(128)S(6)} %copy.7.ref), custom_call_target="tpu_custom_call" | custom-call | flops 100000000 | bytes 1000000 | tf_op jit(solution)/shard_map/pallas_call | solution.py:823
  36.2 0.7 %shard_map.51 = (f32[200,128]{1,0:T(8,128)}, f32[2,1,256]{2,1,0:T(1,128)}) custom-call(f32[200,128]{1,0:T(8,128)S(1)} %get-tuple-element.6.phases_in, f32[2,1,256]{2,1,0:T(1,128)S(1)} %get-tuple-element.7.comp_in), custom_call_target="tpu_custom_call" | custom-call | tf_op jit(solution)/shard_map/pallas_call | solution.py:909

commit v10 on v9

--- a/solution.py
+++ b/solution.py
@@ -141,20 +141,33 @@
     for load in loads:
         load.start()
     barrier = pltpu.get_barrier_semaphore()
-    peers = [(sec, before), (sec, after), (sec_up, pix), (sec_down, pix)]
-    peers += [(sec, x * 16 + lax.rem(z + d, 8) * 2 + core) for d in (1, 7)]
-    peers += [(sec, lax.rem(x + d, 4) * 16 + z * 2 + core) for d in (1, 3)]
+    line = [(sec, before), (sec, after)]
+    aside = [(sec_up, pix), (sec_down, pix)]
+    plane = [(sec, x * 16 + lax.rem(z + d, 8) * 2 + core) for d in (1, 7)]
+    plane += [(sec, lax.rem(x + d, 4) * 16 + z * 2 + core) for d in (1, 3)]
+    leads = sec == 0
+    follows = sec > 0
+
+    def signal(sem, devices):
+        for device in devices:
+            pl.semaphore_signal(sem, inc=1, device_id=device, device_id_type=MESH)
 
     def tell(sem):
-        for peer in peers:
-            pl.semaphore_signal(sem, inc=1, device_id=peer, device_id_type=MESH)
+        signal(sem, line + aside)
+        pl.when(follows)(lambda: signal(sem, plane))
 
     def hear(sem):
-        pl.semaphore_wait(sem, len(peers))
-
-    tell(barrier)
-    hear(barrier)
-    tell(ready.at[0])
+        pl.when(leads)(lambda: pl.semaphore_wait(sem, 4))
+        pl.when(follows)(lambda: pl.semaphore_wait(sem, 8))
+
+    signal(barrier, line)
+    pl.when(sec != SECTIONS - 1)(lambda: signal(barrier, aside[:1]))
+    pl.when(sec != 1)(lambda: signal(barrier, aside[1:]))
+    pl.when(follows)(lambda: signal(barrier, plane))
+    pl.when(leads)(lambda: pl.semaphore_wait(barrier, 2))
+    pl.when(follows)(lambda: pl.semaphore_wait(barrier, 8))
+    signal(ready.at[0], line)
+    pl.when(follows)(lambda: signal(ready.at[0], aside + plane))
 
     def halo(i, n):
         part = blocks.at[1, spans[n]]
@@ -162,8 +175,9 @@
 
     for n in range(len(chunks)):
         loads[n].wait()
-        for i in (0, 2):
-            pl.when(present[i])(halo(i, n).start)
+        pl.when(jnp.logical_and(present[0], core == 0))(halo(0, n).start)
+        pl.when(present[2])(halo(2, n).start)
+        pl.when(jnp.logical_and(present[0], core == 1))(halo(0, n).start)
 
     for i in range(3):
         blocks[i, FLAT:, :] = jnp.zeros((32 * GROUPS - FLAT, 128), F32)
@@ -241,6 +255,7 @@
             arrived(blocks.at[2 * soon, spans[n]], halo_recv.at[1 - soon, n])
         side(soon, range(GROUPS))
         hear(ready.at[0])
+        pl.when(leads)(lambda: signal(ready.at[0], aside))
         tell(ready.at[1])
         for n, (low, high) in enumerate(chunks):
             pl.when(inner)(lambda n=n: arrived(blocks.at[2 * late, spans[n]], halo_recv.at[1 - late, n]))
@@ -459,6 +474,29 @@
         image = plus(product(m3, box, value), joined(z, value))
         return value, norms_of(value, image, c)
 
+    def step_one():
+        @pl.when(sec == 2)
+        def _():
+            arrived(gbuf.at[1:8], g_recv)
+
+        @pl.when(sec != 2)
+        def _():
+            arrived(gbuf.at[0:8], g_recv)
+
+        total = gbuf[0]
+        for d in range(1, 8):
+            total = total + gbuf[d]
+        bmsg[2:4, :] = total
+        bmsg[0:2, :] = jnp.zeros((2, 128), F32)
+
+        @pl.when(sec < SECTIONS - 1)
+        def _():
+            finish(*steps_r)
+            bmsg[0:2, :] = sum_of(rmsg, rbuf1)
+
+        pl.when(leads)(lambda: pl.semaphore_wait(ready.at[4], 4))
+        start(*steps_b)
+
     @pl.when(sec == 1)
     def _():
         hear(ready.at[1])
@@ -510,6 +548,9 @@
         tell(ready.at[3])
         emsg2[...] = sum_of(emsg, ebuf1)
         start(*steps_e[1])
+        hear(ready.at[3])
+        tell(ready.at[4])
+        step_one()
         finish(*steps_e[1])
         eall[...] = sum_of(emsg2, ebuf2)
         for j in range(SECTIONS - 1):
@@ -522,30 +563,6 @@
         column = to_column(sum_of(nmsg2, nbuf2), 16)
         row = lax.broadcasted_iota(jnp.int32, (16, 128), 0)
         ncol[...] = jnp.where(row == NB, ref[0].astype(F32), column) - (pix * (TILES * 128)).astype(F32)
-
-    def step_one():
-        @pl.when(sec == 2)
-        def _():
-            arrived(gbuf.at[1:8], g_recv)
-
-        @pl.when(sec != 2)
-        def _():
-            arrived(gbuf.at[0:8], g_recv)
-
-        total = gbuf[0]
-        for d in range(1, 8):
-            total = total + gbuf[d]
-        bmsg[2:4, :] = total
-        bmsg[0:2, :] = jnp.zeros((2, 128), F32)
-
-        @pl.when(sec < SECTIONS - 1)
-        def _():
-            finish(*steps_r)
-            bmsg[0:2, :] = sum_of(rmsg, rbuf1)
-
-        start(*steps_b)
-
-    pl.when(sec == SECTIONS - 1)(step_one)
 
     def keep(solved):
         value, norms = solved
@@ -642,6 +659,7 @@
         for copy in steps_g:
             copy.start()
         gbuf[0] = gmsg[...]
+        tell(ready.at[4])
 
     @pl.when(sec < SECTIONS - 1)
     def _():
@@ -664,8 +682,9 @@
     def _():
         hear(ready.at[2])
         tell(ready.at[3])
-
-    pl.when(sec != 2)(lambda: hear(ready.at[3]))
+        hear(ready.at[3])
+        tell(ready.at[4])
+
     comp[0, 0:1, :] = msg[0:1, :]
     comp[1, 0:1, :] = msg[1:2, :]
 
@@ -781,6 +800,7 @@
                 count = min(8, ROWS - g * 8)
                 phases[pl.ds(g * 32 + t * 2 + c, count, stride=4), :] = part[g * 8 : g * 8 + count]
 
+    pl.when(follows)(lambda: pl.semaphore_wait(ready.at[4], 8))
     for i in (0, 2):
         pl.when(present[i])(lambda i=i: arrived(blocks.at[1, pl.ds(0, FLAT)], halo_send.at[i // 2]))
     @pl.when(sec == 2)
@@ -899,7 +919,7 @@
             dma(()),
             dma((2,)),
             dma((2,)),
-            pltpu.SemaphoreType.REGULAR((4,)),
+            pltpu.SemaphoreType.REGULAR((5,)),
         ],
         compiler_params=pltpu.CompilerParams(
             collective_id=0, has_side_effects=True, vmem_limit_bytes=16 * 2**20

time: 37 us -> 36.1 us (0.976)
  Pallas kernels: 35.6 us -> 34.6 us
    pallas_call x1, Pallas kernels: 34.9 us -> 34 us  [on_device(): pl.pallas_call(kernel, out_shape=(jax.ShapeDtypeStruct((FLAT, 128), F32),...]
where the time goes in v10:
time: 36.1 us; the launch traced here: 35.9 us
  Pallas kernels  34.6 us (96%)
  between operations  1.28 us (4%)
    pallas_call x1, Pallas kernels, on_device(): pl.pallas_call(kernel, out_shape=(jax.ShapeDtypeStruct((FLAT, 128), F32),...  34 us

profile of v10, /device:TPU:1, one launch (start us, length us, event | category | flops | bytes accessed | tf_op | source)
XLA Modules:
  0.0 35.9 jit_solution(17039250128610586866)
XLA Ops:
  1.3 34.0 %shard_map.50 = (f32[200,128]{1,0:T(8,128)S(1)}, f32[2,1,256]{2,1,0:T(1,128)S(1)}) custom-call(f32[200,128]{1,0:T(8,128)} %bitcast.10, s32[15,256]{1,0:T(8,128)} %nbr_hbm.1, s32[1]{0:T(128)S(6)} %copy.7.ref), custom_call_target="tpu_custom_call" | custom-call | flops 100000000 | bytes 1000000 | tf_op jit(solution)/shard_map/pallas_call | solution.py:843
  35.3 0.7 %shard_map.51 = (f32[200,128]{1,0:T(8,128)}, f32[2,1,256]{2,1,0:T(1,128)}) custom-call(f32[200,128]{1,0:T(8,128)S(1)} %get-tuple-element.6.phases_in, f32[2,1,256]{2,1,0:T(1,128)S(1)} %get-tuple-element.7.comp_in), custom_call_target="tpu_custom_call" | custom-call | tf_op jit(solution)/shard_map/pallas_call | solution.py:929

commit v11 on v10

--- a/solution.py
+++ b/solution.py
@@ -141,7 +141,6 @@
     for load in loads:
         load.start()
     barrier = pltpu.get_barrier_semaphore()
-    line = [(sec, before), (sec, after)]
     aside = [(sec_up, pix), (sec_down, pix)]
     plane = [(sec, x * 16 + lax.rem(z + d, 8) * 2 + core) for d in (1, 7)]
     plane += [(sec, lax.rem(x + d, 4) * 16 + z * 2 + core) for d in (1, 3)]
@@ -152,21 +151,31 @@
         for device in devices:
             pl.semaphore_signal(sem, inc=1, device_id=device, device_id_type=MESH)
 
+    def greet(sem):
+        for i in (0, 2):
+            pl.when(present[i])(lambda i=i: signal(sem, [(sec, near[i])]))
+
     def tell(sem):
-        signal(sem, line + aside)
+        greet(sem)
+        signal(sem, aside)
         pl.when(follows)(lambda: signal(sem, plane))
 
+    def receive(sem, lead, follow):
+        for first_one, wanted in ((leads, lead), (follows, follow)):
+            pl.when(jnp.logical_and(first_one, inner))(lambda wanted=wanted: pl.semaphore_wait(sem, wanted))
+            pl.when(jnp.logical_and(first_one, jnp.logical_not(inner)))(
+                lambda wanted=wanted: pl.semaphore_wait(sem, wanted - 1)
+            )
+
     def hear(sem):
-        pl.when(leads)(lambda: pl.semaphore_wait(sem, 4))
-        pl.when(follows)(lambda: pl.semaphore_wait(sem, 8))
-
-    signal(barrier, line)
+        receive(sem, 4, 8)
+
+    greet(barrier)
     pl.when(sec != SECTIONS - 1)(lambda: signal(barrier, aside[:1]))
     pl.when(sec != 1)(lambda: signal(barrier, aside[1:]))
     pl.when(follows)(lambda: signal(barrier, plane))
-    pl.when(leads)(lambda: pl.semaphore_wait(barrier, 2))
-    pl.when(follows)(lambda: pl.semaphore_wait(barrier, 8))
-    signal(ready.at[0], line)
+    receive(barrier, 2, 8)
+    greet(ready.at[0])
     pl.when(follows)(lambda: signal(ready.at[0], aside + plane))
 
     def halo(i, n):
@@ -494,7 +503,7 @@
             finish(*steps_r)
             bmsg[0:2, :] = sum_of(rmsg, rbuf1)
 
-        pl.when(leads)(lambda: pl.semaphore_wait(ready.at[4], 4))
+        pl.when(leads)(lambda: hear(ready.at[4]))
         start(*steps_b)
 
     @pl.when(sec == 1)
@@ -612,23 +621,35 @@
     norms = [inverse[t] for t in range(TILES)]
     for t in range(TILES):
         s = state[4 * t : 4 * t + 4]
-        norm = norms[t]
-        cr = ci = fr = fi = None
+        cr = ci = None
         for kg in range(2):
             rows = slice(8 * kg, 8 * kg + 8)
             sr, si = s[kg], s[2 + kg]
             br, bi = bvec[t, 0, rows, :], bvec[t, 1, rows, :]
-            zr, zi = zbuf[t, 0, rows, :], zbuf[t, 1, rows, :]
             a, b = sr * br + si * bi, sr * bi - si * br
-            e, f = zr * sr - zi * si, zr * si + zi * sr
             cr = a if kg == 0 else column_sum(cr + a)
             ci = b if kg == 0 else column_sum(ci + b)
+        cols = slice(t * 128, (t + 1) * 128)
+        msg[0:1, cols] = (cr + (SCALE * START) * xsum[t, 0:1, :]) * norms[t]
+        msg[1:2, cols] = (ci + (SCALE * START) * xsum[t, 1:2, :]) * norms[t]
+
+    def send_virtual():
+        for i in range(3):
+            pl.when(present[i])(remote(msg, vbuf.at[2 - i], v_send, v_recv, (sec_up, near[i])).start)
+
+    pl.when(sec < 2)(send_virtual)
+    for t in range(TILES):
+        s = state[4 * t : 4 * t + 4]
+        fr = fi = None
+        for kg in range(2):
+            rows = slice(8 * kg, 8 * kg + 8)
+            sr, si = s[kg], s[2 + kg]
+            zr, zi = zbuf[t, 0, rows, :], zbuf[t, 1, rows, :]
+            e, f = zr * sr - zi * si, zr * si + zi * sr
             fr = e if kg == 0 else column_sum(fr + e)
             fi = f if kg == 0 else column_sum(fi + f)
         cols = slice(t * 128, (t + 1) * 128)
-        msg[0:1, cols] = (cr + (SCALE * START) * xsum[t, 0:1, :]) * norm
-        msg[1:2, cols] = (ci + (SCALE * START) * xsum[t, 1:2, :]) * norm
-        fr, fi = unit((fr + SCALE * START) * norm, fi * norm)
+        fr, fi = unit((fr + SCALE * START) * norms[t], fi * norms[t])
         fmsg[0:1, cols] = fr
         fmsg[1:2, cols] = fi
 
@@ -661,10 +682,7 @@
         gbuf[0] = gmsg[...]
         tell(ready.at[4])
 
-    @pl.when(sec < SECTIONS - 1)
-    def _():
-        for i in range(3):
-            pl.when(present[i])(remote(msg, vbuf.at[2 - i], v_send, v_recv, (sec_up, near[i])).start)
+    pl.when(sec == 2)(send_virtual)
 
     for s in range(1, SECTIONS):
 
@@ -800,7 +818,7 @@
                 count = min(8, ROWS - g * 8)
                 phases[pl.ds(g * 32 + t * 2 + c, count, stride=4), :] = part[g * 8 : g * 8 + count]
 
-    pl.when(follows)(lambda: pl.semaphore_wait(ready.at[4], 8))
+    pl.when(follows)(lambda: hear(ready.at[4]))
     for i in (0, 2):
         pl.when(present[i])(lambda i=i: arrived(blocks.at[1, pl.ds(0, FLAT)], halo_send.at[i // 2]))
     @pl.when(sec == 2)

time: 36.1 us -> 36.1 us (level)
  no operation moved by 1% of the time
where the time goes in v11:
time: 36.1 us; the launch traced here: 35.9 us
  Pallas kernels  34.6 us (96%)
  between operations  1.28 us (4%)
    pallas_call x1, Pallas kernels, on_device(): pl.pallas_call(kernel, out_shape=(jax.ShapeDtypeStruct((FLAT, 128), F32),...  34 us

profile of v11, /device:TPU:1, one launch (start us, length us, event | category | flops | bytes accessed | tf_op | source)
XLA Modules:
  0.0 35.9 jit_solution(4130470530528484941)
XLA Ops:
  1.3 34.0 %shard_map.50 = (f32[200,128]{1,0:T(8,128)S(1)}, f32[2,1,256]{2,1,0:T(1,128)S(1)}) custom-call(f32[200,128]{1,0:T(8,128)} %bitcast.10, s32[15,256]{1,0:T(8,128)} %nbr_hbm.1, s32[1]{0:T(128)S(6)} %copy.7.ref), custom_call_target="tpu_custom_call" | custom-call | flops 100000000 | bytes 1000000 | tf_op jit(solution)/shard_map/pallas_call | solution.py:861
  35.3 0.7 %shard_map.51 = (f32[200,128]{1,0:T(8,128)}, f32[2,1,256]{2,1,0:T(1,128)}) custom-call(f32[200,128]{1,0:T(8,128)S(1)} %get-tuple-element.6.phases_in, f32[2,1,256]{2,1,0:T(1,128)S(1)} %get-tuple-element.7.comp_in), custom_call_target="tpu_custom_call" | custom-call | tf_op jit(solution)/shard_map/pallas_call | solution.py:947

commit v12 on v11

--- a/solution.py
+++ b/solution.py
@@ -506,7 +506,7 @@
         pl.when(leads)(lambda: hear(ready.at[4]))
         start(*steps_b)
 
-    @pl.when(sec == 1)
+    @pl.when(sec < 2)
     def _():
         hear(ready.at[1])
         tell(ready.at[2])
@@ -515,6 +515,11 @@
         prepare((kre, kim, ksum), (kre2, kim2, ksum2), cvec, qvec, sbuf, TILES)
 
     pl.when(jnp.logical_or(sec == 1, sec == 2))(prepare_own)
+
+    @pl.when(sec == 1)
+    def _():
+        hear(ready.at[2])
+        tell(ready.at[3])
 
     @pl.when(sec == 2)
     def _():
@@ -693,13 +698,11 @@
 
     @pl.when(sec == 0)
     def _():
-        hear(ready.at[1])
-        tell(ready.at[2])
-
-    @pl.when(sec < 2)
-    def _():
         hear(ready.at[2])
         tell(ready.at[3])
+
+    @pl.when(sec < 2)
+    def _():
         hear(ready.at[3])
         tell(ready.at[4])
 

time: 36.1 us -> 36.1 us (level)
  no operation moved by 1% of the time
where the time goes in v12:
time: 36.1 us; the launch traced here: 36 us
  Pallas kernels  34.7 us (96%)
  between operations  1.28 us (4%)
    pallas_call x1, Pallas kernels, on_device(): pl.pallas_call(kernel, out_shape=(jax.ShapeDtypeStruct((FLAT, 128), F32),...  34 us

profile of v12, /device:TPU:1, one launch (start us, length us, event | category | flops | bytes accessed | tf_op | source)
XLA Modules:
  0.0 36.0 jit_solution(17346929879581324667)
XLA Ops:
  1.3 34.0 %shard_map.50 = (f32[200,128]{1,0:T(8,128)S(1)}, f32[2,1,256]{2,1,0:T(1,128)S(1)}) custom-call(f32[200,128]{1,0:T(8,128)} %bitcast.10, s32[15,256]{1,0:T(8,128)} %nbr_hbm.1, s32[1]{0:T(128)S(6)} %copy.7.ref), custom_call_target="tpu_custom_call" | custom-call | flops 100000000 | bytes 1000000 | tf_op jit(solution)/shard_map/pallas_call | solution.py:864
  35.3 0.7 %shard_map.51 = (f32[200,128]{1,0:T(8,128)}, f32[2,1,256]{2,1,0:T(1,128)}) custom-call(f32[200,128]{1,0:T(8,128)S(1)} %get-tuple-element.6.phases_in, f32[2,1,256]{2,1,0:T(1,128)S(1)} %get-tuple-element.7.comp_in), custom_call_target="tpu_custom_call" | custom-call | tf_op jit(solution)/shard_map/pallas_call | solution.py:950

commit v13 on v12

--- a/solution.py
+++ b/solution.py
@@ -132,12 +132,12 @@
     steps_r = (rmsg, rbuf1, r_sem, first)
     steps_b = (bmsg, bbuf, b_sem, second)
 
-    chunks = [(0, 3), (3, GROUPS)]
+    chunks = [(0, 2), (2, 5), (5, GROUPS)]
     spans = [pl.ds(32 * low, min(32 * high, FLAT) - 32 * low) for low, high in chunks]
     loads = [
         pltpu.make_async_copy(slc_hbm.at[span], blocks.at[1, span], load_sem.at[i]) for i, span in enumerate(spans)
     ]
-    loads.append(pltpu.make_async_copy(nbr_hbm, nbr, load_sem.at[2]))
+    loads.append(pltpu.make_async_copy(nbr_hbm, nbr, load_sem.at[len(chunks)]))
     for load in loads:
         load.start()
     barrier = pltpu.get_barrier_semaphore()
@@ -202,7 +202,7 @@
             blocks[i] = jnp.zeros((32 * GROUPS, 128), F32)
             vbuf[i] = jnp.zeros_like(vbuf[i])
 
-    loads[2].wait()
+    loads[-1].wait()
 
     base = pix * (TILES * 128) - REACH
     for t in range(TILES):
@@ -926,9 +926,9 @@
             pltpu.VMEM((TILES, 16, 16, 128), F32),
             pltpu.VMEM((1, 16, 16, 128), F32),
             pltpu.VMEM((1, 16, 16, 128), F32),
-            dma((3,)),
+            dma((4,)),
             dma((2,)),
-            dma((2, 2)),
+            dma((2, 3)),
             dma(()),
             dma(()),
             dma(()),

time: 36.1 us -> 36.2 us (level)
  no operation moved by 1% of the time
where the time goes in v13:
time: 36.2 us; the launch traced here: 36.1 us
  Pallas kernels  34.8 us (96%)
  between operations  1.28 us (4%)
    pallas_call x1, Pallas kernels, on_device(): pl.pallas_call(kernel, out_shape=(jax.ShapeDtypeStruct((FLAT, 128), F32),...  34.2 us

profile of v13, /device:TPU:1, one launch (start us, length us, event | category | flops | bytes accessed | tf_op | source)
XLA Modules:
  0.0 36.1 jit_solution(9695993510054733713)
XLA Ops:
  1.3 34.2 %shard_map.50 = (f32[200,128]{1,0:T(8,128)S(1)}, f32[2,1,256]{2,1,0:T(1,128)S(1)}) custom-call(f32[200,128]{1,0:T(8,128)} %bitcast.10, s32[15,256]{1,0:T(8,128)} %nbr_hbm.1, s32[1]{0:T(128)S(6)} %copy.7.ref), custom_call_target="tpu_custom_call" | custom-call | flops 100000000 | bytes 1000000 | tf_op jit(solution)/shard_map/pallas_call | solution.py:864
  35.4 0.7 %shard_map.51 = (f32[200,128]{1,0:T(8,128)}, f32[2,1,256]{2,1,0:T(1,128)}) custom-call(f32[200,128]{1,0:T(8,128)S(1)} %get-tuple-element.6.phases_in, f32[2,1,256]{2,1,0:T(1,128)S(1)} %get-tuple-element.7.comp_in), custom_call_target="tpu_custom_call" | custom-call | tf_op jit(solution)/shard_map/pallas_call | solution.py:950
